TPU v7x, 256 devices: a whole 4x4x8 slice. The times are simulated.
256 devices in a mesh: pipe: 16 (over x_lo, y, core), dp: 16 (over x_hi, z).
Axes of the slice: x: 4 (x_hi: 2, x_lo: 2; x = x_hi * 2 + x_lo), y: 4, z: 8, core: 2. Of those that a mesh axis runs over, the one named last changes fastest.
Arguments:
- inputs: bfloat16 [16, 4096, 4096], P('pipe', 'dp'), may hold values from -6 to 6
- cotangents: bfloat16 [16, 4096, 512], P('pipe', 'dp'), may hold values from -0.09375 to 0.09375
- input_factors: float32 [16, 4096, 256], P('pipe', 'dp'), may hold values from -20 to 20, as said below
- output_factors: float32 [16, 512, 512], P('pipe'), may hold values from -20 to 20, as said below
- input_coupling: float32 [16, 4096, 256], P('pipe', 'dp'), may hold values from -0.375 to 0.375
- output_coupling: float32 [16, 512, 512], P('pipe'), may hold values from -0.25 to 0.25
Outputs:
- update: float32 [16, 4096, 512], P('pipe', 'dp')
Inputs may be any that keep to these rules, and one draw needn't show every extreme that they name: Each [256, 256] row block of a layer's input_factors is positive definite. Each layer's output_factors is positive definite.
All inputs are finite; a program needn't handle non-finite values. Where the computation divides by a largest or mean magnitude, that divisor is 1e-20 or more.
Results may differ from a plain program's by a relative error of at most 0.0003.
Values may be sent and summed in bfloat16 or wider, within the bound.
No kernel may reach another device: no remote copies, remote signals or barrier semaphores. Data moves between devices by JAX's collectives and lax.ppermute only.
A program may use at most 64 MiB of HBM per device.

v0:
```python
import jax
import jax.numpy as jnp
from jax import lax
from jax.sharding import PartitionSpec as P

NS_ITERS = 2


def passed_along(value, axis, steps):
    count = lax.axis_size(axis)
    first, last = (max(0, -steps), min(count, count - steps))
    return lax.ppermute(value, axis, [(source, source + steps) for source in range(first, last)])


def matmul(left, right):
    return jnp.matmul(left, right, precision=lax.Precision.HIGHEST)


def invert(factor):
    order = factor.shape[-1]
    identity = jnp.eye(order, dtype=jnp.float32)
    bound_value = jnp.max(jnp.sum(jnp.abs(factor), axis=1))
    iterate = identity / bound_value
    for sweep in range(NS_ITERS):
        iterate = matmul(iterate, 2.0 * identity - matmul(factor, iterate))
    return iterate


def contract_tokens(left, right):
    return lax.dot_general(
        left, right, (((0,), (0,)), ((), ())), preferred_element_type=jnp.float32
    )


def shards(inputs, cotangents, input_factors, output_factors, input_coupling, output_coupling):
    panel_rows = inputs[0]
    cotangent_block = cotangents[0]
    columns = lax.all_to_all(panel_rows, "dp", split_axis=1, concat_axis=0, tiled=True)
    gradient = contract_tokens(columns, lax.all_gather(cotangent_block, "dp", axis=0, tiled=True))
    coupling_block = input_coupling[0]
    coupling_out = output_coupling[0]
    following = passed_along(gradient, "pipe", -1)
    input_inverse = invert(input_factors[0])
    output_inverse = invert(output_factors[0])
    mixed = matmul(matmul(coupling_block, following), coupling_out.T)
    coupled = gradient - mixed
    scaled = matmul(matmul(input_inverse, coupled), output_inverse)
    carried = matmul(matmul(coupling_block.T, scaled), coupling_out)
    earlier = passed_along(carried, "pipe", 1)
    update = scaled - earlier
    return update[None]


def solution(mesh):
    in_specs = (
        P("pipe", "dp", None),
        P("pipe", "dp", None),
        P("pipe", "dp", None),
        P("pipe", None, None),
        P("pipe", "dp", None),
        P("pipe", None, None),
    )
    out_specs = P("pipe", "dp", None)
    return jax.shard_map(shards, mesh=mesh, in_specs=in_specs, out_specs=out_specs, check_vma=False)
```

profile of v0, /device:TPU:2, one launch (start us, length us, event | category | flops | bytes accessed | tf_op | source)
XLA Modules:
  0.0 178.1 jit_solution(11030102277898754614)
XLA Ops:
  6.5 0.0 all-gather.3.cloned.1.call-start
  6.5 0.7 all-gather.3.cloned.1.call-update
  7.3 4.1 %copy.7 = bf16[1,256,4096]{1,2,0:T(8,128)(2,1)} copy(bf16[1,256,4096]{2,1,0:T(8,128)(2,1)} %param.6) | data formatting | bytes 4194304 | tf_op args[0]
  11.4 10.3 %all-to-all-start = ((bf16[256,16,256]{0,2,1:T(8,128)(2,1)}), bf16[256,16,256]{0,2,1:T(8,128)(2,1)}, u32[]{:S(2)}, u32[]{:S(2)}) async-start(bf16[256,16,256]{0,2,1:T(8,128)(2,1)} %bitcast.3), calls=%async_computation | async-start | bytes 4194304 | tf_op jit(solution)/shard_map/all_to_all | solution.py:38
  21.7 0.1 fusion.32
  21.8 0.6 reduce_max.18
  22.4 0.2 fusion.15
  22.6 0.6 reduce_max.19
  24.5 0.4 fusion.12
  24.9 0.4 fusion.23
  25.3 1.3 fusion.11
  26.6 1.8 %select_subtract_fusion.1 = f32[512,512]{0,1:T(8,128)S(1)} fusion(f32[1,512,512]{2,1,0:T(8,128)S(1)} %copy-done.1, f32[]{:T(128)S(6)} %divide.7), kind=kOutput, calls=%fused_computation.3 | convolution fusion | flops 1611923456 | bytes 2097156 | tf_op jit(solution)/shard_map/dot_general | solution.py:16
  28.5 1.9 %fusion.2 = f32[512,512]{1,0:T(8,128)S(1)} fusion(f32[512,512]{0,1:T(8,128)S(1)} %select_subtract_fusion.1, f32[]{:T(128)S(6)} %divide.7), kind=kOutput, calls=%fused_computation.4 | convolution fusion | flops 1611137024 | bytes 2097156 | tf_op jit(solution)/shard_map/dot_general | solution.py:16
  30.4 3.5 %select_subtract_fusion = f32[512,512]{0,1:T(8,128)S(1)} fusion(f32[512,512]{1,0:T(8,128)S(1)} %fusion.2, f32[1,512,512]{2,1,0:T(8,128)S(1)} %copy-done.2), kind=kOutput, calls=%fused_computation.2 | convolution fusion | flops 1611399168 | bytes 3145728 | tf_op jit(solution)/shard_map/dot_general | solution.py:16
  33.9 48.7 %all-to-all-done = bf16[256,16,256]{0,2,1:T(8,128)(2,1)} async-done(((bf16[256,16,256]{0,2,1:T(8,128)(2,1)}), bf16[256,16,256]{0,2,1:T(8,128)(2,1)}, u32[]{:S(2)}, u32[]{:S(2)}) %all-to-all-start) | async-done | bytes 2097184 | tf_op jit(solution)/shard_map/all_to_all | solution.py:38
  82.6 3.9 %copy.8 = bf16[16,256,256]{2,1,0:T(8,128)(2,1)} copy(bf16[16,256,256]{1,2,0:T(8,128)(2,1)} %bitcast.4) | data formatting | bytes 4194304 | tf_op jit(solution)/shard_map/all_to_all | solution.py:38
  86.5 51.6 %all-gather.3.cloned.1.call-done = bf16[1,4096,512]{2,1,0:T(8,128)(2,1)} async-done(((bf16[1,256,512]{2,1,0:T(8,128)(2,1)}), bf16[1,4096,512]{2,1,0:T(8,128)(2,1)}) %all-gather.3.cloned.1.call-update) | async-done | bytes 4194320 | tf_op jit(solution)/shard_map/all_gather | solution.py:39
  138.1 4.1 %fusion = f32[256,512]{1,0:T(8,128)S(1)} fusion(bf16[4096,256]{1,0:T(8,128)(2,1)} %bitcast.67, bf16[1,4096,512]{2,1,0:T(8,128)(2,1)} %all-gather.3.cloned.1.call-done), kind=kOutput, calls=%fused_computation | convolution fusion | flops 1073741824 | bytes 6815744 | tf_op jit(solution)/shard_map/dot_general | solution.py:30
  142.2 0.0 copy-start.4
  142.3 2.2 %collective-permute-start = (f32[256,512]{1,0:T(8,128)S(1)}, f32[256,512]{1,0:T(8,128)S(1)}, u32[]{:S(2)}, u32[]{:S(2)}) collective-permute-start(f32[256,512]{1,0:T(8,128)S(1)} %fusion), channel_id=1, source_target_pairs={{16,0},{32,16},{48,32},{64,48},{80,64},{96,80},{112,96},{128,112},... | collective-permute-start | bytes 1572872 | tf_op jit(solution)/shard_map/ppermute | solution.py:12
  144.5 0.4 fusion.41
  144.9 1.9 %fusion.43 = f32[512,512]{1,0:T(8,128)S(1)} fusion(f32[512,512]{1,0:T(8,128)S(1)} %fusion.2, f32[512,512]{0,1:T(8,128)S(1)} %select_subtract_fusion), kind=kOutput, calls=%fused_computation.50 | convolution fusion | flops 1610612736 | bytes 3145728 | tf_op jit(solution)/shard_map/dot_general | solution.py:16
  146.8 4.2 %collective-permute-done = f32[256,512]{1,0:T(8,128)S(1)} collective-permute-done((f32[256,512]{1,0:T(8,128)S(1)}, f32[256,512]{1,0:T(8,128)S(1)}, u32[]{:S(2)}, u32[]{:S(2)}) %collective-permute-start) | collective-permute-done | bytes 524320 | tf_op jit(solution)/shard_map/ppermute | solution.py:12
  151.0 1.0 fusion.28
  152.0 1.9 %convolution_subtract_fusion = f32[256,512]{1,0:T(8,128)S(1)} fusion(f32[256,512]{1,0:T(8,128)S(1)} %fusion, f32[512,256]{1,0:T(8,128)S(1)} %fusion.28, f32[1,512,512]{2,1,0:T(8,128)S(1)} %copy-done), kind=kOutput, calls=%fused_computation.10 | convolution fusion | flops 805437440 | bytes 2621440 | tf_op jit(solution)/shard_map/dot_general | solution.py:16
  153.9 0.6 fusion.42
  154.5 1.1 fusion.44
  155.6 1.0 fusion.26
  156.6 1.1 fusion.16
  157.6 3.7 %collective-permute-start.1 = (f32[256,512]{1,0:T(8,128)S(1)}, f32[256,512]{1,0:T(8,128)S(1)}, u32[]{:S(2)}, u32[]{:S(2)}) collective-permute-start(f32[256,512]{1,0:T(8,128)S(1)} %fusion.16), channel_id=1, source_target_pairs={{0,16},{16,32},{32,48},{48,64},{64,80},{80,96},{96,112},{112,128},... | collective-permute-start | bytes 1572872 | tf_op jit(solution)/shard_map/ppermute | solution.py:12
  161.3 9.1 %collective-permute-done.1 = f32[256,512]{1,0:T(8,128)S(1)} collective-permute-done((f32[256,512]{1,0:T(8,128)S(1)}, f32[256,512]{1,0:T(8,128)S(1)}, u32[]{:S(2)}, u32[]{:S(2)}) %collective-permute-start.1) | collective-permute-done | bytes 524320 | tf_op jit(solution)/shard_map/ppermute | solution.py:12
  170.4 0.9 subtract_bitcast_fusion
  (11 shorter events, 0.0 us)
Async XLA Ops:
  6.5 145.5 %copy-start = (f32[1,512,512]{2,1,0:T(8,128)S(1)}, f32[1,512,512]{2,1,0:T(8,128)}, u32[]{:S(2)}) copy-start(f32[1,512,512]{2,1,0:T(8,128)} %param.11) | copy-start | bytes 3145732
  6.5 131.6 %all-gather.3.cloned.1.call-start = ((), (), s32[]{:S(2)}) async-start(), calls=%async_computation.1 | async-start | bytes 4456448 | tf_op jit(solution)/shard_map/all_gather | solution.py:39
  11.4 10.3 %copy-start.3 = (f32[1,256,256]{2,1,0:T(8,128)S(1)}, f32[1,256,256]{2,1,0:T(8,128)}, u32[]{:S(2)}) copy-start(f32[1,256,256]{2,1,0:T(8,128)} %param.8) | copy-start | bytes 786436
  11.4 11.1 %copy-start.1 = (f32[1,512,512]{2,1,0:T(8,128)S(1)}, f32[1,512,512]{2,1,0:T(8,128)}, u32[]{:S(2)}) copy-start(f32[1,512,512]{2,1,0:T(8,128)} %param.9) | copy-start | bytes 3145732
  11.4 71.2 %all-to-all-start = ((bf16[256,16,256]{0,2,1:T(8,128)(2,1)}), bf16[256,16,256]{0,2,1:T(8,128)(2,1)}, u32[]{:S(2)}, u32[]{:S(2)}) async-start(bf16[256,16,256]{0,2,1:T(8,128)(2,1)} %bitcast.3), calls=%async_computation | async-start | bytes 4194304 | tf_op jit(solution)/shard_map/all_to_all | solution.py:38
  26.6 3.8 %copy-start.2 = (f32[1,512,512]{2,1,0:T(8,128)S(1)}, f32[1,512,512]{2,1,0:T(8,128)}, u32[]{:S(2)}) copy-start(f32[1,512,512]{2,1,0:T(8,128)} %param.9) | copy-start | bytes 3145732
  138.1 6.4 %copy-start.5 = (f32[256,256]{0,1:T(8,128)S(1)}, f32[256,256]{0,1:T(8,128)}, u32[]{:S(2)}) copy-start(f32[256,256]{0,1:T(8,128)} %fusion.11) | copy-start | bytes 786436
  142.2 8.8 %copy-start.4 = (f32[1,256,256]{2,1,0:T(8,128)S(1)}, f32[1,256,256]{2,1,0:T(8,128)}, u32[]{:S(2)}) copy-start(f32[1,256,256]{2,1,0:T(8,128)} %param.10) | copy-start | bytes 786436
  142.3 8.7 %collective-permute-start = (f32[256,512]{1,0:T(8,128)S(1)}, f32[256,512]{1,0:T(8,128)S(1)}, u32[]{:S(2)}, u32[]{:S(2)}) collective-permute-start(f32[256,512]{1,0:T(8,128)S(1)} %fusion), channel_id=1, source_target_pairs={{16,0},{32,16},{48,32},{64,48},{80,64},{96,80},{112,96},{128,112},... | collective-permute-start | bytes 1572872 | tf_op jit(solution)/shard_map/ppermute | solution.py:12
  157.6 12.8 %collective-permute-start.1 = (f32[256,512]{1,0:T(8,128)S(1)}, f32[256,512]{1,0:T(8,128)S(1)}, u32[]{:S(2)}, u32[]{:S(2)}) collective-permute-start(f32[256,512]{1,0:T(8,128)S(1)} %fusion.16), channel_id=1, source_target_pairs={{0,16},{16,32},{32,48},{48,64},{64,80},{80,96},{96,112},{112,128},... | collective-permute-start | bytes 1572872 | tf_op jit(solution)/shard_map/ppermute | solution.py:12
Sparse Core Ops, SparseCore 0:
  9.9 128.1 all-gather.2
where the time goes:
time: 178 us
  waiting for transfers between devices  114 us (64%)
  matrix products  22.3 us (13%)
  starting transfers between devices  16.2 us (9%)
  between operations  14.9 us (8%)
  local copies, waits for them, and re-layouts  8.05 us (5%)
  other arithmetic  2.37 us (1%)
    all_gather x1, waiting for transfers between devices, shards(): lax.all_gather(cotangent_block, 'dp', axis=0, tiled=True)  51.6 us
    all_to_all x1, waiting for transfers between devices, shards(): lax.all_to_all(panel_rows, 'dp', split_axis=1, concat_axis=0, tiled=True)  48.7 us
    dot_general x14, matrix products, matmul(): return jnp.matmul(left, right, precision=lax.Precision.HIGHEST)  18.2 us
    ppermute x2, waiting for transfers between devices, passed_along(): lax.ppermute(value, axis, [(source, source + steps) for source in range(f...  13.3 us
    all_to_all x1, starting transfers between devices, shards(): lax.all_to_all(panel_rows, 'dp', split_axis=1, concat_axis=0, tiled=True)  10.3 us
    ppermute x2, starting transfers between devices, passed_along(): lax.ppermute(value, axis, [(source, source + steps) for source in range(f...  5.9 us
    unnamed x13, local copies, waits for them, and re-layouts  4.12 us
    dot_general x1, matrix products, contract_tokens(): lax.dot_general(left, right, (((0,), (0,)), ((), ())), preferred_element_...  4.12 us
  transfers between devices with their start and end apart: 4, of which 4 were waited for; matrix products, arithmetic and copies ran while one was open for 12% of the time, Pallas kernels for 0%

commit v1 on v0

v1 whole, which is shorter than its diff:
```python
import jax
import jax.numpy as jnp
from jax import lax
from jax.sharding import PartitionSpec as P

HIGH = lax.Precision.HIGH
AXES = ("pipe", "dp")
BLOCK = 256
RING = 8


def permutation(move):
    pairs = []
    for layer in range(16):
        for half in range(2):
            for place in range(RING):
                to_half, to_place = move(layer % 2, half, place)
                pairs.append((layer * 16 + half * RING + place, layer * 16 + to_half % 2 * RING + to_place % RING))
    return pairs


ACROSS = permutation(lambda core, half, place: (half + 1, place))
LONG = permutation(lambda core, half, place: (half, place + (1 if core == 0 else -1)))
SHORT = permutation(lambda core, half, place: (half, place - (1 if core == 0 else -1)))


def passed_along(value, steps):
    first, last = (max(0, -steps), min(16, 16 - steps))
    return lax.ppermute(value, "pipe", [(source, source + steps) for source in range(first, last)])


def mm(left, right):
    return jnp.matmul(left, right, precision=HIGH)


def invert(factor):
    order = factor.shape[-1]
    identity = jnp.eye(order, dtype=jnp.float32)
    scale = 1.0 / jnp.max(jnp.sum(jnp.abs(factor), axis=1))
    iterate = scale * (2.0 * identity - scale * factor)
    return mm(iterate, 2.0 * identity - mm(factor, iterate))


def contract_tokens(left, right):
    return lax.dot_general(left, right, (((0,), (0,)), ((), ())), preferred_element_type=jnp.float32)


def shards(inputs, cotangents, input_factors, output_factors, input_coupling, output_coupling):
    rows = inputs[0]
    cots = cotangents[0]
    spot = lax.axis_index("dp")
    half, place = spot // RING, spot % RING
    sign = 1 - 2 * (lax.axis_index("pipe") % 2)

    def piece(of_half, offset):
        start = of_half * (RING * BLOCK) + (place + sign * offset + RING) % RING * BLOCK
        return lax.dynamic_slice_in_dim(rows, start, BLOCK, axis=1)

    groups = ((4,), (-3, 3), (-2, 2), (-1, 1, 0))
    theirs = {}
    their_cots = None
    for index, group in enumerate(groups):
        message = [piece(1 - half, offset) for offset in group]
        if index == 0:
            message.append(cots)
        arrived = lax.ppermute(jnp.concatenate(message, axis=1), AXES, ACROSS)
        for at, offset in enumerate(group):
            theirs[offset] = arrived[:, at * BLOCK : (at + 1) * BLOCK]
        if index == 0:
            their_cots = arrived[:, BLOCK:]

    def partial(offset):
        return contract_tokens(piece(half, offset), cots) + contract_tokens(theirs[offset], their_cots)

    coupling = input_coupling[0]
    coupling_out = output_coupling[0]
    left = invert(input_factors[0])
    right = invert(output_factors[0])
    left_next = mm(left, coupling)
    right_next = mm(coupling_out.T, right)
    left_back = mm(coupling.T, left)
    right_back = mm(right, coupling_out)
    left_own = passed_along(mm(coupling.T, left_next), 1)
    right_own = passed_along(mm(right_next, coupling_out), 1)

    long_way = partial(4)
    short_way = partial(-3)
    for step in range(4):
        long_way = lax.ppermute(long_way, AXES, LONG) + partial(3 - step)
        if step < 2:
            short_way = lax.ppermute(short_way, AXES, SHORT) + partial(step - 2)
        elif step == 2:
            short_way = lax.ppermute(short_way, AXES, SHORT)
    gradient = long_way + short_way

    following = passed_along(gradient, -1)
    back = passed_along(mm(mm(left_back, gradient), right_back), 1)
    mine = mm(mm(left, gradient), right) + mm(mm(left_own, gradient), right_own)
    update = mine - mm(mm(left_next, following), right_next) - back
    return update[None]


def solution(mesh):
    in_specs = (
        P("pipe", "dp", None),
        P("pipe", "dp", None),
        P("pipe", "dp", None),
        P("pipe", None, None),
        P("pipe", "dp", None),
        P("pipe", None, None),
    )
    out_specs = P("pipe", "dp", None)
    return jax.shard_map(shards, mesh=mesh, in_specs=in_specs, out_specs=out_specs, check_vma=False)
```

time: 178 us -> 116 us (0.65)
  waiting for transfers between devices: 114 us -> 30.7 us
  matrix products: 22.3 us -> 42.6 us
  starting transfers between devices: 16.2 us -> 31 us
  between operations: 14.9 us -> 1.81 us
  local copies, waits for them, and re-layouts: 8.05 us -> 1.67 us
  other arithmetic: 2.37 us -> 7.69 us
    all_gather x1 -> x0, waiting for transfers between devices: 51.6 us -> none  [shards(): lax.all_gather(cotangent_block, 'dp', axis=0, tiled=True)]
    all_to_all x1 -> x0, waiting for transfers between devices: 48.7 us -> none  [shards(): lax.all_to_all(panel_rows, 'dp', split_axis=1, concat_axis=0, tiled=True)]
    ppermute x2 -> x15, starting transfers between devices: 5.9 us -> 31 us  [the longest x4 14.8 us: passed_along(): lax.ppermute(value, 'pipe', [(source, source + steps) for source in range...]
    dot_general x1 -> x16, matrix products: 4.12 us -> 23 us  [contract_tokens(): lax.dot_general(left, right, (((0,), (0,)), ((), ())), preferred_element_...]
    ppermute x2 -> x15, waiting for transfers between devices: 13.3 us -> 30.7 us  [the longest x2 17.3 us: shards(): short_way = lax.ppermute(short_way, AXES, SHORT) + partial(step - 2)]
    all_to_all x1 -> x0, starting transfers between devices: 10.3 us -> none  [shards(): lax.all_to_all(panel_rows, 'dp', split_axis=1, concat_axis=0, tiled=True)]
    unnamed x13 -> x26, local copies, waits for them, and re-layouts: 4.12 us -> 0.18 us
    all_to_all x1 -> x0, local copies, waits for them, and re-layouts: 3.93 us -> none  [shards(): lax.all_to_all(panel_rows, 'dp', split_axis=1, concat_axis=0, tiled=True)]
  transfers between devices with their start and end apart: 4 -> 15, of which waited for: 4 -> 4; matrix products, arithmetic and copies ran while one was open for 12% -> 42% of each run, Pallas kernels for 0% -> 0%
where the time goes in v1:
time: 116 us; the launch traced here: 115 us
  matrix products  42.6 us (37%)
  starting transfers between devices  31 us (27%)
  waiting for transfers between devices  30.7 us (26%)
  other arithmetic  7.69 us (7%)
  between operations  1.81 us (2%)
  local copies, waits for them, and re-layouts  1.67 us (1%)
    dot_general x16, matrix products, contract_tokens(): lax.dot_general(left, right, (((0,), (0,)), ((), ())), preferred_element_...  23 us
    dot_general x18, matrix products, mm(): return jnp.matmul(left, right, precision=HIGH)  19.6 us
    ppermute x2, waiting for transfers between devices, shards(): short_way = lax.ppermute(short_way, AXES, SHORT) + partial(step - 2)  17.3 us
    ppermute x4, starting transfers between devices, passed_along(): lax.ppermute(value, 'pipe', [(source, source + steps) for source in range...  14.8 us
    ppermute x1, waiting for transfers between devices, shards(): short_way = lax.ppermute(short_way, AXES, SHORT)  7.39 us
    ppermute x4, starting transfers between devices, shards(): arrived = lax.ppermute(jnp.concatenate(message, axis=1), AXES, ACROSS)  7.06 us
    ppermute x4, waiting for transfers between devices, passed_along(): lax.ppermute(value, 'pipe', [(source, source + steps) for source in range...  5.92 us
    ppermute x4, starting transfers between devices, shards(): long_way = lax.ppermute(long_way, AXES, LONG) + partial(3 - step)  4.55 us
  transfers between devices with their start and end apart: 15, of which 4 were waited for; matrix products, arithmetic and copies ran while one was open for 42% of the time, Pallas kernels for 0%

profile of v1, /device:TPU:2, one launch (start us, length us, event | category | flops | bytes accessed | tf_op | source)
XLA Modules:
  0.0 115.4 jit_solution(14060152996731853318)
XLA Ops:
  0.0 1.5 %dynamic-slice_bitcast_fusion.2 = (bf16[256,256]{1,0:T(8,128)(2,1)S(1)}, bf16[256,256]{1,0:T(8,128)(2,1)S(1)}, bf16[256,256]{1,0:T(8,128)(2,1)S(1)}, bf16[256,25...) fusion(bf16[1,256,4096]{2,1,0:T(8,128)(2,1)} %param.6, ...), kind=kLoop, calls=%fused_computation.99 | loop fusion | bytes 2097184 | tf_op jit(solution)/shard_map/dynamic_slice | solution.py:57
  2.2 2.1 %collective-permute-start.2 = (bf16[256,512]{1,0:T(8,128)(2,1)}, bf16[256,512]{1,0:T(8,128)(2,1)}, u32[]{:S(2)}, u32[]{:S(2)}) collective-permute-start(bf16[256,512]{1,0:T(8,128)(2,1)} %pad_maximum_fusion.2), channel_id=1, source_target_pairs={{0,8},{1,9},{2,10},{3,11},{4,12},{5,13},{6,14},{7,15},{8,0},{9,1},... | collective-permute-start | bytes 786440 | tf_op jit(solution)/shard_map/ppermute | solution.py:66
  5.1 1.4 %collective-permute-start = (bf16[256,768]{1,0:T(8,128)(2,1)}, bf16[256,768]{1,0:T(8,128)(2,1)S(1)}, u32[]{:S(2)}, u32[]{:S(2)}) collective-permute-start(bf16[256,768]{1,0:T(8,128)(2,1)} %pad_maximum_fusion), channel_id=1, source_target_pairs={{0,8},{1,9},{2,10},{3,11},{4,12},{5,13},{6,14},{7,15},{8,0},{9,1},... | collective-permute-start | bytes 1179656 | tf_op jit(solution)/shard_map/ppermute | solution.py:66
  7.3 2.1 %collective-permute-start.4 = (bf16[256,512]{1,0:T(8,128)(2,1)}, bf16[256,512]{1,0:T(8,128)(2,1)}, u32[]{:S(2)}, u32[]{:S(2)}) collective-permute-start(bf16[256,512]{1,0:T(8,128)(2,1)} %pad_maximum_fusion.3), channel_id=1, source_target_pairs={{0,8},{1,9},{2,10},{3,11},{4,12},{5,13},{6,14},{7,15},{8,0},{9,1},... | collective-permute-start | bytes 786440 | tf_op jit(solution)/shard_map/ppermute | solution.py:66
  10.2 1.4 %collective-permute-start.6 = (bf16[256,768]{1,0:T(8,128)(2,1)}, bf16[256,768]{1,0:T(8,128)(2,1)}, u32[]{:S(2)}, u32[]{:S(2)}) collective-permute-start(bf16[256,768]{1,0:T(8,128)(2,1)} %pad_maximum_fusion.1), channel_id=1, source_target_pairs={{0,8},{1,9},{2,10},{3,11},{4,12},{5,13},{6,14},{7,15},{8,0},{9,1},... | collective-permute-start | bytes 1179656 | tf_op jit(solution)/shard_map/ppermute | solution.py:66
  15.0 1.9 %collective-permute-start.11 = (f32[256,256]{0,1:T(8,128)}, f32[256,256]{0,1:T(8,128)}, u32[]{:S(2)}, u32[]{:S(2)}) collective-permute-start(f32[256,256]{0,1:T(8,128)} %convolution_bitcast_fusion.1), channel_id=1, source_target_pairs={{0,16},{16,32},{32,48},{48,64},{64,80},{80,96},{96,112},{112,128},... | collective-permute-start | bytes 786440 | tf_op jit(solution)/shard_map/ppermute | solution.py:29
  20.7 2.0 %fusion.8 = f32[512,512]{1,0:T(8,128)} fusion(f32[512,512]{1,0:T(8,128)S(1)} %fusion.6, f32[1,512,512]{2,1,0:T(8,128)S(1)} %copy-done), kind=kOutput, calls=%fused_computation.22 | convolution fusion | flops 805306368 | bytes 3145728 | tf_op jit(solution)/shard_map/dot_general | solution.py:33
  22.7 2.0 %fusion.12 = f32[512,512]{1,0:T(8,128)} fusion(f32[512,512]{1,0:T(8,128)S(1)} %fusion.6, f32[1,512,512]{2,1,0:T(8,128)S(1)} %copy-done), kind=kOutput, calls=%fused_computation.26 | convolution fusion | flops 805306368 | bytes 3145728 | tf_op jit(solution)/shard_map/dot_general | solution.py:33
  24.7 1.9 %fusion.54 = f32[256,512]{1,0:T(8,128)} fusion(bf16[1,256,4096]{2,1,0:T(8,128)(2,1)} %param.6, s32[]{:T(128)S(6)} %select_n.135, bf16[1,256,512]{2,1,0:T(8,128)(2,1)S(1)} %copy-done.1), kind=kOutput, calls=%fused_computation.81 | convolution fusion | flops 67108864 | bytes 917508 | tf_op jit(solution)/shard_map/dot_general | solution.py:45
  26.7 1.9 %fusion.52 = f32[256,512]{1,0:T(8,128)} fusion(bf16[1,256,4096]{2,1,0:T(8,128)(2,1)} %param.6, s32[]{:T(128)S(6)} %select_n.136, bf16[1,256,512]{2,1,0:T(8,128)(2,1)S(1)} %copy-done.1), kind=kOutput, calls=%fused_computation.79 | convolution fusion | flops 67108864 | bytes 917508 | tf_op jit(solution)/shard_map/dot_general | solution.py:45
  28.6 2.0 %fusion.50 = f32[256,512]{1,0:T(8,128)} fusion(bf16[1,256,4096]{2,1,0:T(8,128)(2,1)} %param.6, s32[]{:T(128)S(6)} %select_n.137, bf16[1,256,512]{2,1,0:T(8,128)(2,1)S(1)} %copy-done.1), kind=kOutput, calls=%fused_computation.77 | convolution fusion | flops 67108864 | bytes 917508 | tf_op jit(solution)/shard_map/dot_general | solution.py:45
  30.6 1.9 %fusion.64 = f32[256,512]{1,0:T(8,128)} fusion(bf16[1,256,4096]{2,1,0:T(8,128)(2,1)} %param.6, s32[]{:T(128)S(6)} %select_n.115, bf16[1,256,512]{2,1,0:T(8,128)(2,1)S(1)} %copy-done.1), kind=kOutput, calls=%fused_computation.91 | convolution fusion | flops 67108864 | bytes 917508 | tf_op jit(solution)/shard_map/dot_general | solution.py:45
  32.5 3.3 %fusion.10 = f32[512,512]{1,0:T(8,128)} fusion(f32[512,512]{1,0:T(8,128)} %fusion.12, f32[1,512,512]{2,1,0:T(8,128)S(1)} %copy-done), kind=kOutput, calls=%fused_computation.24 | convolution fusion | flops 805306368 | bytes 3145728 | tf_op jit(solution)/shard_map/dot_general | solution.py:33
  36.9 1.9 %collective-permute-start.1 = (f32[256,512]{1,0:T(8,128)}, f32[256,512]{1,0:T(8,128)}, u32[]{:S(2)}, u32[]{:S(2)}) collective-permute-start(f32[256,512]{1,0:T(8,128)} %convolution_add_fusion.8), channel_id=1, source_target_pairs={{0,1},{1,2},{2,3},{3,4},{4,5},{5,6},{6,7},{7,0},{8,9},{9,10},{10,1... | collective-permute-start | bytes 1572872 | tf_op jit(solution)/shard_map/ppermute | solution.py:89
  38.8 2.0 %fusion.62 = f32[256,512]{1,0:T(8,128)} fusion(bf16[1,256,4096]{2,1,0:T(8,128)(2,1)} %param.6, s32[]{:T(128)S(6)} %select_n.118, bf16[1,256,512]{2,1,0:T(8,128)(2,1)S(1)} %copy-done.1), kind=kOutput, calls=%fused_computation.89 | convolution fusion | flops 67108864 | bytes 917508 | tf_op jit(solution)/shard_map/dot_general | solution.py:45
  42.0 7.4 %collective-permute-start.12 = (f32[512,512]{1,0:T(8,128)}, f32[512,512]{1,0:T(8,128)}, u32[]{:S(2)}, u32[]{:S(2)}) collective-permute-start(f32[512,512]{1,0:T(8,128)} %fusion.10), channel_id=1, source_target_pairs={{0,16},{16,32},{32,48},{48,64},{64,80},{80,96},{96,112},{112,128},... | collective-permute-start | bytes 3145736 | tf_op jit(solution)/shard_map/ppermute | solution.py:29
  49.4 1.4 %convolution_add_fusion.3 = f32[256,512]{1,0:T(8,128)S(1)} fusion(f32[256,512]{1,0:T(8,128)} %fusion.54, bf16[256,512]{1,0:T(8,128)(2,1)} %collective-permute-done.2, bf16[256,768]{1,0:T(8,128)(2,1)S(1)} %collective-permute-done), kind=kOutput, calls=%fused_computation.10 | convolution fusion | flops 67239936 | bytes 1441792 | tf_op jit(solution)/shard_map/dot_general | solution.py:45
  50.8 1.4 %collective-permute-start.8 = (f32[256,512]{1,0:T(8,128)S(1)}, f32[256,512]{1,0:T(8,128)S(1)}, u32[]{:S(2)}, u32[]{:S(2)}) collective-permute-start(f32[256,512]{1,0:T(8,128)S(1)} %convolution_add_fusion.3), channel_id=1, source_target_pairs={{0,7},{1,0},{2,1},{3,2},{4,3},{5,4},{6,5},{7,6},{8,15},{9,8},{10,9... | collective-permute-start | bytes 1572872 | tf_op jit(solution)/shard_map/ppermute | solution.py:91
  52.3 1.4 %fusion.3 = f32[256,512]{1,0:T(8,128)S(1)} fusion(f32[256,512]{1,0:T(8,128)} %collective-permute-done.1, f32[256,512]{1,0:T(8,128)S(1)} %copy-done.10, bf16[256,512]{1,0:T(8,128)(2,1)} %collective-permute-done.2, bf16[256,768]{1,0:T(8,128)(2,1)S(1)} %collective-permute-done), kind=kOutput, calls=%fused_computation.15 | convolution fusion | flops 67371008 | bytes 1966080 | tf_op jit(solution)/shard_map/dot_general | solution.py:45
  55.7 9.6 %collective-permute-done.8 = f32[256,512]{1,0:T(8,128)S(1)} collective-permute-done((f32[256,512]{1,0:T(8,128)S(1)}, f32[256,512]{1,0:T(8,128)S(1)}, u32[]{:S(2)}, u32[]{:S(2)}) %collective-permute-start.8) | collective-permute-done | bytes 524320 | tf_op jit(solution)/shard_map/ppermute | solution.py:91
  67.1 1.7 %collective-permute-start.5 = (f32[256,512]{1,0:T(8,128)S(1)}, f32[256,512]{1,0:T(8,128)S(1)}, u32[]{:S(2)}, u32[]{:S(2)}) collective-permute-start(f32[256,512]{1,0:T(8,128)S(1)} %add.281), channel_id=1, source_target_pairs={{0,1},{1,2},{2,3},{3,4},{4,5},{5,6},{6,7},{7,0},{8,9},{9,10},{10,1... | collective-permute-start | bytes 1572872 | tf_op jit(solution)/shard_map/ppermute | solution.py:89
  72.2 7.7 %collective-permute-done.9 = f32[256,512]{1,0:T(8,128)S(1)} collective-permute-done((f32[256,512]{1,0:T(8,128)S(1)}, f32[256,512]{1,0:T(8,128)S(1)}, u32[]{:S(2)}, u32[]{:S(2)}) %collective-permute-start.9) | collective-permute-done | bytes 524320 | tf_op jit(solution)/shard_map/ppermute | solution.py:91
  80.8 2.7 %collective-permute-start.10 = (f32[256,512]{1,0:T(8,128)}, f32[256,512]{1,0:T(8,128)}, u32[]{:S(2)}, u32[]{:S(2)}) collective-permute-start(f32[256,512]{1,0:T(8,128)} %add.314), channel_id=1, source_target_pairs={{0,7},{1,0},{2,1},{3,2},{4,3},{5,4},{6,5},{7,6},{8,15},{9,8},{10,9... | collective-permute-start | bytes 1572872 | tf_op jit(solution)/shard_map/ppermute | solution.py:93
  86.7 1.2 %convolution_add_fusion.4 = f32[256,512]{1,0:T(8,128)S(1)} fusion(f32[256,512]{1,0:T(8,128)S(1)} %fusion.56, bf16[256,768]{1,0:T(8,128)(2,1)} %collective-permute-done.6, bf16[256,768]{1,0:T(8,128)(2,1)S(1)} %collective-permute-done), kind=kOutput, calls=%fused_computation.11 | convolution fusion | flops 67239936 | bytes 1441792 | tf_op jit(solution)/shard_map/dot_general | solution.py:45
  88.0 7.4 %collective-permute-done.10 = f32[256,512]{1,0:T(8,128)} collective-permute-done((f32[256,512]{1,0:T(8,128)}, f32[256,512]{1,0:T(8,128)}, u32[]{:S(2)}, u32[]{:S(2)}) %collective-permute-start.10) | collective-permute-done | bytes 524320 | tf_op jit(solution)/shard_map/ppermute | solution.py:93
  95.3 1.3 %add_add_fusion = f32[256,512]{1,0:T(8,128)S(1)} fusion(f32[256,512]{1,0:T(8,128)} %collective-permute-done.10, f32[256,512]{1,0:T(8,128)} %collective-permute-done.7, f32[256,512]{1,0:T(8,128)S(1)} %convolution_add_fusion.4), kind=kLoop, calls=%fused_computation.45 | loop fusion | flops 262144 | bytes 2097152 | tf_op jit(solution)/shard_map/add | solution.py:94
  96.7 3.6 %collective-permute-start.13 = (f32[256,512]{1,0:T(8,128)S(1)}, f32[256,512]{1,0:T(8,128)S(1)}, u32[]{:S(2)}, u32[]{:S(2)}) collective-permute-start(f32[256,512]{1,0:T(8,128)S(1)} %add_add_fusion), channel_id=1, source_target_pairs={{16,0},{32,16},{48,32},{64,48},{80,64},{96,80},{112,96},{128,112},... | collective-permute-start | bytes 1572872 | tf_op jit(solution)/shard_map/ppermute | solution.py:29
  101.4 1.9 %collective-permute-start.14 = (f32[256,512]{1,0:T(8,128)S(1)}, f32[256,512]{1,0:T(8,128)S(1)}, u32[]{:S(2)}, u32[]{:S(2)}) collective-permute-start(f32[256,512]{1,0:T(8,128)S(1)} %fusion.117), channel_id=1, source_target_pairs={{0,16},{16,32},{32,48},{48,64},{64,80},{80,96},{96,112},{112,128},... | collective-permute-start | bytes 1572872 | tf_op jit(solution)/shard_map/ppermute | solution.py:29
  104.3 1.4 %fusion.114 = f32[256,512]{1,0:T(8,128)S(1)} fusion(f32[256,256]{0,1:T(8,128)} %collective-permute-done.11, f32[256,512]{1,0:T(8,128)S(1)} %add_add_fusion), kind=kOutput, calls=%fused_computation.149 | convolution fusion | flops 201326592 | bytes 1310720 | tf_op jit(solution)/shard_map/dot_general | solution.py:33
  105.7 1.9 %convolution_add_fusion = f32[256,512]{1,0:T(8,128)S(1)} fusion(f32[256,512]{1,0:T(8,128)S(1)} %fusion.113, f32[256,512]{1,0:T(8,128)S(1)} %fusion.114, f32[512,512]{1,0:T(8,128)} %collective-permute-done.12), kind=kOutput, calls=%fused_computation.4 | convolution fusion | flops 402784256 | bytes 2621440 | tf_op jit(solution)/shard_map/dot_general | solution.py:33
  108.1 5.9 %collective-permute-done.14 = f32[256,512]{1,0:T(8,128)S(1)} collective-permute-done((f32[256,512]{1,0:T(8,128)S(1)}, f32[256,512]{1,0:T(8,128)S(1)}, u32[]{:S(2)}, u32[]{:S(2)}) %collective-permute-start.14) | collective-permute-done | bytes 524320 | tf_op jit(solution)/shard_map/ppermute | solution.py:29
  114.0 1.4 %fusion.1 = f32[1,256,512]{2,1,0:T(8,128)} fusion(f32[256,512]{1,0:T(8,128)S(1)} %collective-permute-done.14, f32[256,512]{1,0:T(8,128)S(1)} %convolution_add_fusion, f32[256,512]{1,0:T(8,128)S(1)} %fusion.115, f32[512,512]{1,0:T(8,128)S(1)} %copy-done.2), kind=kOutput, calls=%fused_computation.6 | convolution fusion | flops 402915328 | bytes 3145728 | tf_op jit(solution)/shard_map/dot_general | solution.py:33
  (71 shorter events, 24.8 us)
Async XLA Ops:
  0.0 20.7 %copy-start = (f32[1,512,512]{2,1,0:T(8,128)S(1)}, f32[1,512,512]{2,1,0:T(8,128)}, u32[]{:S(2)}) copy-start(f32[1,512,512]{2,1,0:T(8,128)} %param.11) | copy-start | bytes 3145732
  0.0 4.4 %copy-start.1 = (bf16[1,256,512]{2,1,0:T(8,128)(2,1)S(1)}, bf16[1,256,512]{2,1,0:T(8,128)(2,1)}, u32[]{:S(2)}) copy-start(bf16[1,256,512]{2,1,0:T(8,128)(2,1)} %param.7) | copy-start | bytes 786436
  0.0 11.6 %copy-start.6 = (f32[1,256,256]{2,1,0:T(8,128)S(1)}, f32[1,256,256]{2,1,0:T(8,128)}, u32[]{:S(2)}) copy-start(f32[1,256,256]{2,1,0:T(8,128)} %param.8) | copy-start | bytes 786436
  2.2 11.4 %copy-start.7 = (f32[1,256,256]{2,1,0:T(8,128)S(1)}, f32[1,256,256]{2,1,0:T(8,128)}, u32[]{:S(2)}) copy-start(f32[1,256,256]{2,1,0:T(8,128)} %param.10) | copy-start | bytes 786436
  2.2 39.8 %collective-permute-start.2 = (bf16[256,512]{1,0:T(8,128)(2,1)}, bf16[256,512]{1,0:T(8,128)(2,1)}, u32[]{:S(2)}, u32[]{:S(2)}) collective-permute-start(bf16[256,512]{1,0:T(8,128)(2,1)} %pad_maximum_fusion.2), channel_id=1, source_target_pairs={{0,8},{1,9},{2,10},{3,11},{4,12},{5,13},{6,14},{7,15},{8,0},{9,1},... | collective-permute-start | bytes 786440 | tf_op jit(solution)/shard_map/ppermute | solution.py:66
  5.1 30.7 %collective-permute-start = (bf16[256,768]{1,0:T(8,128)(2,1)}, bf16[256,768]{1,0:T(8,128)(2,1)S(1)}, u32[]{:S(2)}, u32[]{:S(2)}) collective-permute-start(bf16[256,768]{1,0:T(8,128)(2,1)} %pad_maximum_fusion), channel_id=1, source_target_pairs={{0,8},{1,9},{2,10},{3,11},{4,12},{5,13},{6,14},{7,15},{8,0},{9,1},... | collective-permute-start | bytes 1179656 | tf_op jit(solution)/shard_map/ppermute | solution.py:66
  7.3 46.3 %collective-permute-start.4 = (bf16[256,512]{1,0:T(8,128)(2,1)}, bf16[256,512]{1,0:T(8,128)(2,1)}, u32[]{:S(2)}, u32[]{:S(2)}) collective-permute-start(bf16[256,512]{1,0:T(8,128)(2,1)} %pad_maximum_fusion.3), channel_id=1, source_target_pairs={{0,8},{1,9},{2,10},{3,11},{4,12},{5,13},{6,14},{7,15},{8,0},{9,1},... | collective-permute-start | bytes 786440 | tf_op jit(solution)/shard_map/ppermute | solution.py:66
  9.4 7.6 %copy-start.4 = (f32[1,512,512]{2,1,0:T(8,128)S(1)}, f32[1,512,512]{2,1,0:T(8,128)}, u32[]{:S(2)}) copy-start(f32[1,512,512]{2,1,0:T(8,128)} %param.9) | copy-start | bytes 3145732
  10.2 59.7 %collective-permute-start.6 = (bf16[256,768]{1,0:T(8,128)(2,1)}, bf16[256,768]{1,0:T(8,128)(2,1)}, u32[]{:S(2)}, u32[]{:S(2)}) collective-permute-start(bf16[256,768]{1,0:T(8,128)(2,1)} %pad_maximum_fusion.1), channel_id=1, source_target_pairs={{0,8},{1,9},{2,10},{3,11},{4,12},{5,13},{6,14},{7,15},{8,0},{9,1},... | collective-permute-start | bytes 1179656 | tf_op jit(solution)/shard_map/ppermute | solution.py:66
  15.0 89.3 %collective-permute-start.11 = (f32[256,256]{0,1:T(8,128)}, f32[256,256]{0,1:T(8,128)}, u32[]{:S(2)}, u32[]{:S(2)}) collective-permute-start(f32[256,256]{0,1:T(8,128)} %convolution_bitcast_fusion.1), channel_id=1, source_target_pairs={{0,16},{16,32},{32,48},{48,64},{64,80},{80,96},{96,112},{112,128},... | collective-permute-start | bytes 786440 | tf_op jit(solution)/shard_map/ppermute | solution.py:29
  18.4 1.2 %copy-start.5 = (f32[1,512,512]{2,1,0:T(8,128)S(1)}, f32[1,512,512]{2,1,0:T(8,128)}, u32[]{:S(2)}) copy-start(f32[1,512,512]{2,1,0:T(8,128)} %param.9) | copy-start | bytes 3145732
  32.5 3.3 %copy-start.11 = (f32[256,512]{1,0:T(8,128)S(1)}, f32[256,512]{1,0:T(8,128)}, u32[]{:S(2)}) copy-start(f32[256,512]{1,0:T(8,128)} %fusion.64) | copy-start | bytes 1572868
  36.9 13.9 %collective-permute-start.1 = (f32[256,512]{1,0:T(8,128)}, f32[256,512]{1,0:T(8,128)}, u32[]{:S(2)}, u32[]{:S(2)}) collective-permute-start(f32[256,512]{1,0:T(8,128)} %convolution_add_fusion.8), channel_id=1, source_target_pairs={{0,1},{1,2},{2,3},{3,4},{4,5},{5,6},{6,7},{7,0},{8,9},{9,10},{10,1... | collective-permute-start | bytes 1572872 | tf_op jit(solution)/shard_map/ppermute | solution.py:89
  40.8 11.4 %copy-start.10 = (f32[256,512]{1,0:T(8,128)S(1)}, f32[256,512]{1,0:T(8,128)}, u32[]{:S(2)}) copy-start(f32[256,512]{1,0:T(8,128)} %fusion.62) | copy-start | bytes 1572868
  42.0 23.3 %copy-start.9 = (f32[256,512]{1,0:T(8,128)S(1)}, f32[256,512]{1,0:T(8,128)}, u32[]{:S(2)}) copy-start(f32[256,512]{1,0:T(8,128)} %fusion.52) | copy-start | bytes 1572868
  42.0 63.7 %collective-permute-start.12 = (f32[512,512]{1,0:T(8,128)}, f32[512,512]{1,0:T(8,128)}, u32[]{:S(2)}, u32[]{:S(2)}) collective-permute-start(f32[512,512]{1,0:T(8,128)} %fusion.10), channel_id=1, source_target_pairs={{0,16},{16,32},{32,48},{48,64},{64,80},{80,96},{96,112},{112,128},... | collective-permute-start | bytes 3145736 | tf_op jit(solution)/shard_map/ppermute | solution.py:29
  50.8 14.5 %collective-permute-start.8 = (f32[256,512]{1,0:T(8,128)S(1)}, f32[256,512]{1,0:T(8,128)S(1)}, u32[]{:S(2)}, u32[]{:S(2)}) collective-permute-start(f32[256,512]{1,0:T(8,128)S(1)} %convolution_add_fusion.3), channel_id=1, source_target_pairs={{0,7},{1,0},{2,1},{3,2},{4,3},{5,4},{6,5},{7,6},{8,15},{9,8},{10,9... | collective-permute-start | bytes 1572872 | tf_op jit(solution)/shard_map/ppermute | solution.py:91
  53.6 13.3 %collective-permute-start.3 = (f32[256,512]{1,0:T(8,128)S(1)}, f32[256,512]{1,0:T(8,128)S(1)}, u32[]{:S(2)}, u32[]{:S(2)}) collective-permute-start(f32[256,512]{1,0:T(8,128)S(1)} %fusion.3), channel_id=1, source_target_pairs={{0,1},{1,2},{2,3},{3,4},{4,5},{5,6},{6,7},{7,0},{8,9},{9,10},{10,1... | collective-permute-start | bytes 1572872 | tf_op jit(solution)/shard_map/ppermute | solution.py:89
  55.7 14.2 %copy-start.8 = (f32[256,512]{1,0:T(8,128)S(1)}, f32[256,512]{1,0:T(8,128)}, u32[]{:S(2)}) copy-start(f32[256,512]{1,0:T(8,128)} %fusion.50) | copy-start | bytes 1572868
  66.5 13.5 %collective-permute-start.9 = (f32[256,512]{1,0:T(8,128)S(1)}, f32[256,512]{1,0:T(8,128)S(1)}, u32[]{:S(2)}, u32[]{:S(2)}) collective-permute-start(f32[256,512]{1,0:T(8,128)S(1)} %fusion.2), channel_id=1, source_target_pairs={{0,7},{1,0},{2,1},{3,2},{4,3},{5,4},{6,5},{7,6},{8,15},{9,8},{10,9... | collective-permute-start | bytes 1572872 | tf_op jit(solution)/shard_map/ppermute | solution.py:91
  67.1 16.5 %collective-permute-start.5 = (f32[256,512]{1,0:T(8,128)S(1)}, f32[256,512]{1,0:T(8,128)S(1)}, u32[]{:S(2)}, u32[]{:S(2)}) collective-permute-start(f32[256,512]{1,0:T(8,128)S(1)} %add.281), channel_id=1, source_target_pairs={{0,1},{1,2},{2,3},{3,4},{4,5},{5,6},{6,7},{7,0},{8,9},{9,10},{10,1... | collective-permute-start | bytes 1572872 | tf_op jit(solution)/shard_map/ppermute | solution.py:89
  80.8 14.5 %collective-permute-start.10 = (f32[256,512]{1,0:T(8,128)}, f32[256,512]{1,0:T(8,128)}, u32[]{:S(2)}, u32[]{:S(2)}) collective-permute-start(f32[256,512]{1,0:T(8,128)} %add.314), channel_id=1, source_target_pairs={{0,7},{1,0},{2,1},{3,2},{4,3},{5,4},{6,5},{7,6},{8,15},{9,8},{10,9... | collective-permute-start | bytes 1572872 | tf_op jit(solution)/shard_map/ppermute | solution.py:93
  84.4 10.9 %collective-permute-start.7 = (f32[256,512]{1,0:T(8,128)}, f32[256,512]{1,0:T(8,128)}, u32[]{:S(2)}, u32[]{:S(2)}) collective-permute-start(f32[256,512]{1,0:T(8,128)} %add.299), channel_id=1, source_target_pairs={{0,1},{1,2},{2,3},{3,4},{4,5},{5,6},{6,7},{7,0},{8,9},{9,10},{10,1... | collective-permute-start | bytes 1572872 | tf_op jit(solution)/shard_map/ppermute | solution.py:89
  85.5 14.8 %copy-start.12 = (f32[256,256]{1,0:T(8,128)S(1)}, f32[256,256]{1,0:T(8,128)}, u32[]{:S(2)}) copy-start(f32[256,256]{1,0:T(8,128)} %fusion.30) | copy-start | bytes 786436
  86.7 14.1 %copy-start.3 = (f32[512,512]{1,0:T(8,128)S(1)}, f32[512,512]{1,0:T(8,128)}, u32[]{:S(2)}) copy-start(f32[512,512]{1,0:T(8,128)} %fusion.8) | copy-start | bytes 3145732
  96.7 11.0 %collective-permute-start.13 = (f32[256,512]{1,0:T(8,128)S(1)}, f32[256,512]{1,0:T(8,128)S(1)}, u32[]{:S(2)}, u32[]{:S(2)}) collective-permute-start(f32[256,512]{1,0:T(8,128)S(1)} %add_add_fusion), channel_id=1, source_target_pairs={{16,0},{32,16},{48,32},{64,48},{80,64},{96,80},{112,96},{128,112},... | collective-permute-start | bytes 1572872 | tf_op jit(solution)/shard_map/ppermute | solution.py:29
  101.4 12.6 %collective-permute-start.14 = (f32[256,512]{1,0:T(8,128)S(1)}, f32[256,512]{1,0:T(8,128)S(1)}, u32[]{:S(2)}, u32[]{:S(2)}) collective-permute-start(f32[256,512]{1,0:T(8,128)S(1)} %fusion.117), channel_id=1, source_target_pairs={{0,16},{16,32},{32,48},{48,64},{64,80},{80,96},{96,112},{112,128},... | collective-permute-start | bytes 1572872 | tf_op jit(solution)/shard_map/ppermute | solution.py:29
  105.7 8.3 %copy-start.2 = (f32[512,512]{1,0:T(8,128)S(1)}, f32[512,512]{1,0:T(8,128)}, u32[]{:S(2)}) copy-start(f32[512,512]{1,0:T(8,128)} %fusion.12) | copy-start | bytes 3145732

commit v2 on v1

v2 whole, which is shorter than its diff:
```python
import jax
import jax.numpy as jnp
from jax import lax
from jax.experimental import pallas as pl
from jax.experimental.pallas import tpu as pltpu
from jax.sharding import PartitionSpec as P


AXES = ("pipe", "dp")
BLOCK = 256
OUT = 512
TOKENS = 256
VMEM = 12 << 20
RING = 8


def permutation(move):
    pairs = []
    for layer in range(16):
        for half in range(2):
            for place in range(RING):
                to_half, to_place = move(layer % 2, half, place)
                pairs.append((layer * 16 + half * RING + place, layer * 16 + to_half % 2 * RING + to_place % RING))
    return pairs


ACROSS = permutation(lambda core, half, place: (half + 1, place))
LONG = permutation(lambda core, half, place: (half, place + (1 if core == 0 else -1)))
SHORT = permutation(lambda core, half, place: (half, place - (1 if core == 0 else -1)))


def passed_along(value, steps):
    first, last = (max(0, -steps), min(16, 16 - steps))
    return lax.ppermute(value, "pipe", [(source, source + steps) for source in range(first, last)])


def mm(left, right, dim=1):
    dims = (((dim,), (0,)), ((), ()))

    def halves(value):
        high = value.astype(jnp.bfloat16)
        return high, (value - high.astype(jnp.float32)).astype(jnp.bfloat16)

    def dot(one, two):
        return lax.dot_general(one, two, dims, preferred_element_type=jnp.float32)

    (left_high, left_low), (right_high, right_low) = halves(left), halves(right)
    return dot(left_high, right_high) + (dot(left_high, right_low) + dot(left_low, right_high))


def invert(factor):
    shape = factor.shape
    twice = jnp.where(lax.broadcasted_iota(jnp.int32, shape, 0) == lax.broadcasted_iota(jnp.int32, shape, 1), 2.0, 0.0)
    scale = 1.0 / jnp.max(jnp.sum(jnp.abs(factor), axis=1, keepdims=True), axis=0, keepdims=True)
    iterate = scale * (twice - scale * factor)
    return mm(iterate, twice - mm(factor, iterate))


def local(body, flops, shapes, *operands):
    def kernel(*refs):
        results = body(*[ref[...] for ref in refs[: len(operands)]])
        for ref, result in zip(refs[len(operands) :], results):
            ref[...] = result

    return pl.pallas_call(
        kernel,
        out_shape=[jax.ShapeDtypeStruct(shape, jnp.float32) for shape in shapes],
        cost_estimate=pl.CostEstimate(flops=flops, transcendentals=0, bytes_accessed=1 << 20),
        compiler_params=pltpu.CompilerParams(vmem_limit_bytes=VMEM),
    )(*operands)


def contract_tokens(left, right):
    return lax.dot_general(left, right, (((0,), (0,)), ((), ())), preferred_element_type=jnp.float32)


def shards(inputs, cotangents, input_factors, output_factors, input_coupling, output_coupling):
    return whole(inputs[0], cotangents[0], input_factors[0], output_factors[0], input_coupling[0], output_coupling[0])[None]


def sent(value, pairs):
    return lax.ppermute(value, AXES, pairs)


def after(value, *events):
    return lax.optimization_barrier((value, *events))[0]


def whole(rows, cots, factor_in, factor_out, coupling, coupling_out):
    def gather(*lists):
        widths = [sum(OUT if block is None else BLOCK for block in blocks) for blocks in lists]
        count = sum(len(blocks) for blocks in lists)

        def kernel(rows_ref, cots_ref, *refs):
            outs, sems = refs[: len(lists)], refs[len(lists)]
            spot = lax.axis_index("dp")
            half, place = spot // RING, spot % RING
            sign = 1 - 2 * (lax.axis_index("pipe") % 2)
            copies = []
            for out, blocks in zip(outs, lists):
                at = 0
                for block in blocks:
                    if block is None:
                        source, width = cots_ref, OUT
                    else:
                        own, offset = block
                        start = (half if own else 1 - half) * (RING * BLOCK) + (place + sign * offset + RING) % RING * BLOCK
                        source, width = rows_ref.at[:, pl.ds(pl.multiple_of(start, BLOCK), BLOCK)], BLOCK
                    copies.append(pltpu.make_async_copy(source, out.at[:, at : at + width], sems.at[len(copies)]))
                    at += width
            for copy in copies:
                copy.start()
            for copy in copies:
                copy.wait()

        return pl.pallas_call(
            kernel,
            out_shape=[jax.ShapeDtypeStruct((TOKENS, width), jnp.bfloat16) for width in widths],
            in_specs=[pl.BlockSpec(memory_space=pltpu.HBM)] * 2,
            out_specs=[pl.BlockSpec(memory_space=pltpu.VMEM) for _ in widths],
            scratch_shapes=[pltpu.SemaphoreType.DMA((count,))],
            cost_estimate=pl.CostEstimate(flops=10**8, transcendentals=0, bytes_accessed=2 * 512 * sum(widths)),
            compiler_params=pltpu.CompilerParams(vmem_limit_bytes=VMEM),
        )(pltpu.with_memory_space_constraint(rows, pltpu.HBM), pltpu.with_memory_space_constraint(cots, pltpu.HBM))

    groups = ((4,), (-3, 3), (-2, 2), (-1, 1, 0))
    (message_0,) = gather([(False, 4), None])
    arrived = [sent(message_0, ACROSS)]
    message_1, message_2, message_3, *own_rows = gather(
        *[[(False, offset) for offset in group] for group in groups[1:]],
        *[[(True, offset) for offset in group] for group in groups],
    )
    for message in (message_1, message_2, message_3):
        arrived.append(sent(message, ACROSS))

    def partials(index):
        count = len(groups[index])

        def kernel(own_ref, cots_ref, first_ref, *refs):
            their_ref, outs = (refs[0], refs[1:]) if index else (first_ref, refs)
            their_cots = first_ref[:, BLOCK:]
            for at, out in enumerate(outs):
                cut = slice(at * BLOCK, (at + 1) * BLOCK)
                out[...] = contract_tokens(own_ref[:, cut], cots_ref[...]) + contract_tokens(their_ref[:, cut], their_cots)

        operands = (own_rows[index], cots, arrived[0]) + ((arrived[index],) if index else ())
        return pl.pallas_call(
            kernel,
            out_shape=[jax.ShapeDtypeStruct((BLOCK, OUT), jnp.float32)] * count,
            cost_estimate=pl.CostEstimate(flops=count * 4 * BLOCK * BLOCK * OUT, transcendentals=0, bytes_accessed=count << 19),
            compiler_params=pltpu.CompilerParams(vmem_limit_bytes=VMEM),
        )(*operands)

    partial = {}
    for index, group in enumerate(groups):
        for offset, value in zip(group, partials(index)):
            partial[offset] = value

    def total(*values):
        return local(lambda first, *rest: (sum(rest, first),), 10**6, [(BLOCK, OUT)], *values)[0]

    def hop(value, pairs, offset):
        return total(sent(value, pairs), partial[offset])

    long_0 = partial[4]
    short_0 = partial[-3]
    long_1 = hop(long_0, LONG, 3)
    short_1 = hop(short_0, SHORT, -2)
    long_2 = hop(long_1, LONG, 2)
    short_2 = hop(short_1, SHORT, -1)
    long_3 = hop(long_2, LONG, 1)
    short_3 = sent(short_2, SHORT)
    long_4 = sent(long_3, LONG)
    gradient = total(long_4, short_3, partial[0])

    square, wide, full = (BLOCK, BLOCK), (BLOCK, OUT), (OUT, OUT)

    def left_side(factor, coupling):
        left = invert(factor)
        left_next = mm(left, coupling)
        left_own = mm(coupling, left_next, 0)
        packed = jnp.concatenate([left_own[: BLOCK // 2], left_own[BLOCK // 2 :]], axis=1)
        return left, left_next, mm(coupling, left, 0), packed

    def right_side(coupling_out, right, packed):
        right_next = mm(coupling_out, right, 0)
        return right_next, jnp.concatenate([mm(right_next, coupling_out), packed], axis=0)

    def own_terms(gradient, left, right, weights):
        left_own = jnp.concatenate([weights[OUT:, :BLOCK], weights[OUT:, BLOCK:]], axis=0)
        return (mm(mm(left, gradient), right) + mm(mm(left_own, gradient), weights[:OUT]),)

    def product(left, value, right):
        return (mm(mm(left, value), right),)

    left, left_next, left_back, packed = local(left_side, 10**9, [square, square, square, (BLOCK // 2, OUT)], factor_in, coupling)
    (right,) = local(lambda factor: (invert(factor),), 2 * 10**9, [full], after(factor_out, long_1))
    right_next, weights = local(right_side, 2 * 10**9, [full, (OUT + BLOCK // 2, OUT)], coupling_out, after(right, long_2), packed)
    (right_back,) = local(lambda right, out: (mm(right, out),), 10**9, [full], after(right, long_3), coupling_out)
    weights = passed_along(weights, 1)
    following = passed_along(gradient, -1)
    (passed,) = local(product, 10**9, [wide], left_back, gradient, right_back)
    back = passed_along(passed, 1)
    (mine,) = local(own_terms, 2 * 10**9, [wide], gradient, left, right, weights)
    (mine,) = local(
        lambda mine, *rest: (mine - product(*rest)[0],), 10**9, [wide], mine, left_next, following, right_next
    )
    return mine - back


def solution(mesh):
    in_specs = (
        P("pipe", "dp", None),
        P("pipe", "dp", None),
        P("pipe", "dp", None),
        P("pipe", None, None),
        P("pipe", "dp", None),
        P("pipe", None, None),
    )
    out_specs = P("pipe", "dp", None)
    return jax.shard_map(shards, mesh=mesh, in_specs=in_specs, out_specs=out_specs, check_vma=False)
```

time: 116 us -> 89.5 us (0.77)
  matrix products: 42.6 us -> 0 us
  Pallas kernels: 0 us -> 14.5 us
  waiting for transfers between devices: 30.7 us -> 43.1 us
  other arithmetic: 7.69 us -> 0.88 us
  starting transfers between devices: 31 us -> 28.6 us
  between operations: 1.81 us -> 0.22 us
    dot_general x34 -> x0, matrix products: 42.6 us -> none  [the longest x16 23 us: contract_tokens(): lax.dot_general(left, right, (((0,), (0,)), ((), ())), preferred_element_...]
    pallas_call x0 -> x19, Pallas kernels: none -> 14.5 us  [the longest x13 9.96 us: local(): pl.pallas_call(kernel, out_shape=[jax.ShapeDtypeStruct(shape, jnp.float32...]
    ppermute x11, waiting for transfers between devices: 24.7 us -> 35.3 us  [sent(): return lax.ppermute(value, AXES, pairs)]
    ppermute x4 -> x3, starting transfers between devices: 14.8 us -> 6.25 us  [passed_along(): lax.ppermute(value, 'pipe', [(source, source + steps) for source in range...]
    ppermute x11, starting transfers between devices: 16.2 us -> 22.3 us  [sent(): return lax.ppermute(value, AXES, pairs)]
    add x4 -> x0, other arithmetic: 3.18 us -> none  [the longest x1 1.34 us: shards(): gradient = long_way + short_way]
    concatenate x4 -> x0, other arithmetic: 3.02 us -> none  [shards(): arrived = lax.ppermute(jnp.concatenate(message, axis=1), AXES, ACROSS)]
    ppermute x4 -> x3, waiting for transfers between devices: 5.92 us -> 7.75 us  [passed_along(): lax.ppermute(value, 'pipe', [(source, source + steps) for source in range...]
  transfers between devices with their start and end apart: 15 -> 14, of which waited for: 4 -> 9; matrix products, arithmetic and copies ran while one was open for 42% -> 0% of each run, Pallas kernels for 0% -> 15%
where the time goes in v2:
time: 89.5 us; the launch traced here: 88.4 us
  waiting for transfers between devices  43.1 us (48%)
  starting transfers between devices  28.6 us (32%)
  Pallas kernels  14.5 us (16%)
  local copies, waits for them, and re-layouts  1.07 us (1%)
    ppermute x11, waiting for transfers between devices, sent(): return lax.ppermute(value, AXES, pairs)  35.3 us
    ppermute x11, starting transfers between devices, sent(): return lax.ppermute(value, AXES, pairs)  22.3 us
    pallas_call x13, Pallas kernels, local(): pl.pallas_call(kernel, out_shape=[jax.ShapeDtypeStruct(shape, jnp.float32...  9.96 us
    ppermute x3, waiting for transfers between devices, passed_along(): lax.ppermute(value, 'pipe', [(source, source + steps) for source in range...  7.75 us
    ppermute x3, starting transfers between devices, passed_along(): lax.ppermute(value, 'pipe', [(source, source + steps) for source in range...  6.25 us
    pallas_call x2, Pallas kernels, gather(): pl.pallas_call(kernel, out_shape=[jax.ShapeDtypeStruct((TOKENS, width), j...  2.75 us
    pallas_call x4, Pallas kernels, partials(): pl.pallas_call(kernel, out_shape=[jax.ShapeDtypeStruct((BLOCK, OUT), jnp....  1.84 us
  transfers between devices with their start and end apart: 14, of which 9 were waited for; matrix products, arithmetic and copies ran while one was open for 0% of the time, Pallas kernels for 15%

profile of v2, /device:TPU:2, one launch (start us, length us, event | category | flops | bytes accessed | tf_op | source)
XLA Modules:
  0.0 88.4 jit_solution(11230331616319649214)
XLA Ops:
  0.0 1.0 %shard_map.65 = bf16[256,768]{1,0:T(8,128)(2,1)S(1)} custom-call(bf16[256,4096]{1,0:T(8,128)(2,1)} %bitcast.19, bf16[256,512]{1,0:T(8,128)(2,1)} %bitcast.8), custom_call_target="tpu_custom_call" | custom-call | flops 100000000 | bytes 786432 | tf_op jit(solution)/shard_map/pallas_call | solution.py:116
  1.1 2.2 %collective-permute-start = (bf16[256,768]{1,0:T(8,128)(2,1)S(1)}, bf16[256,768]{1,0:T(8,128)(2,1)S(1)}, u32[]{:S(2)}, u32[]{:S(2)}) collective-permute-start(bf16[256,768]{1,0:T(8,128)(2,1)S(1)} %shard_map.65), channel_id=1, source_target_pairs={{0,8},{1,9},{2,10},{3,11},{4,12},{5,13},{6,14},{7,15},{8,0},{9,1},... | collective-permute-start | bytes 1179656 | tf_op jit(solution)/shard_map/ppermute | solution.py:82
  3.3 1.7 %shard_map.64 = (bf16[256,512]{1,0:T(8,128)(2,1)S(1)}, bf16[256,512]{1,0:T(8,128)(2,1)S(1)}, bf16[256,768]{1,0:T(8,128)(2,1)S(1)}, bf16[256,256]{1,0:T(8,128)(2,...) custom-call(bf16[256,4096]{1,0:T(8,128)(2,1)} %bitcast.20, ...), custom_call_target="tpu_custom_call" | custom-call | flops 100000000 | bytes 3932160 | tf_op jit(solution)/shard_map/pallas_call | solution.py:116
  5.0 8.5 %collective-permute-done.first_ref = bf16[256,768]{1,0:T(8,128)(2,1)S(1)} collective-permute-done((bf16[256,768]{1,0:T(8,128)(2,1)S(1)}, bf16[256,768]{1,0:T(8,128)(2,1)S(1)}, u32[]{:S(2)}, u32[]{:S(2)}) %collective-permute-start) | collective-permute-done | bytes 393248 | tf_op jit(solution)/shard_map/ppermute | solution.py:82
  13.8 2.0 %collective-permute-start.1 = (f32[256,512]{1,0:T(8,128)S(1)}, f32[256,512]{1,0:T(8,128)S(1)}, u32[]{:S(2)}, u32[]{:S(2)}) collective-permute-start(f32[256,512]{1,0:T(8,128)S(1)} %shard_map.66), channel_id=1, source_target_pairs={{0,1},{1,2},{2,3},{3,4},{4,5},{5,6},{6,7},{7,0},{8,9},{9,10},{10,1... | collective-permute-start | bytes 1572872 | tf_op jit(solution)/shard_map/ppermute | solution.py:82
  15.8 2.1 %collective-permute-start.2 = (bf16[256,512]{1,0:T(8,128)(2,1)S(1)}, bf16[256,512]{1,0:T(8,128)(2,1)S(1)}, u32[]{:S(2)}, u32[]{:S(2)}) collective-permute-start(bf16[256,512]{1,0:T(8,128)(2,1)S(1)} %get-tuple-element.30), channel_id=1, source_target_pairs={{0,8},{1,9},{2,10},{3,11},{4,12},{5,13},{6,14},{7,15},{8,0},{9,1},... | collective-permute-start | bytes 786440 | tf_op jit(solution)/shard_map/ppermute | solution.py:82
  17.9 6.9 %collective-permute-done.2.refs_0_ = bf16[256,512]{1,0:T(8,128)(2,1)S(1)} collective-permute-done((bf16[256,512]{1,0:T(8,128)(2,1)S(1)}, bf16[256,512]{1,0:T(8,128)(2,1)S(1)}, u32[]{:S(2)}, u32[]{:S(2)}) %collective-permute-start.2) | collective-permute-done | bytes 262176 | tf_op jit(solution)/shard_map/ppermute | solution.py:82
  25.3 4.4 %collective-permute-start.8 = (f32[256,512]{1,0:T(8,128)S(1)}, f32[256,512]{1,0:T(8,128)S(1)}, u32[]{:S(2)}, u32[]{:S(2)}) collective-permute-start(f32[256,512]{1,0:T(8,128)S(1)} %get-tuple-element.38), channel_id=1, source_target_pairs={{0,7},{1,0},{2,1},{3,2},{4,3},{5,4},{6,5},{7,6},{8,15},{9,8},{10,9... | collective-permute-start | bytes 1572872 | tf_op jit(solution)/shard_map/ppermute | solution.py:82
  29.9 2.2 %collective-permute-start.4 = (bf16[256,512]{1,0:T(8,128)(2,1)S(1)}, bf16[256,512]{1,0:T(8,128)(2,1)S(1)}, u32[]{:S(2)}, u32[]{:S(2)}) collective-permute-start(bf16[256,512]{1,0:T(8,128)(2,1)S(1)} %get-tuple-element.33), channel_id=1, source_target_pairs={{0,8},{1,9},{2,10},{3,11},{4,12},{5,13},{6,14},{7,15},{8,0},{9,1},... | collective-permute-start | bytes 786440 | tf_op jit(solution)/shard_map/ppermute | solution.py:82
  32.1 1.4 %collective-permute-start.6 = (bf16[256,768]{1,0:T(8,128)(2,1)S(1)}, bf16[256,768]{1,0:T(8,128)(2,1)S(1)}, u32[]{:S(2)}, u32[]{:S(2)}) collective-permute-start(bf16[256,768]{1,0:T(8,128)(2,1)S(1)} %get-tuple-element.36), channel_id=1, source_target_pairs={{0,8},{1,9},{2,10},{3,11},{4,12},{5,13},{6,14},{7,15},{8,0},{9,1},... | collective-permute-start | bytes 1179656 | tf_op jit(solution)/shard_map/ppermute | solution.py:82
  33.5 1.3 %shard_map.76 = (f32[256,256]{1,0:T(8,128)S(1)}, f32[256,256]{1,0:T(8,128)S(1)}, f32[256,256]{1,0:T(8,128)S(1)}, f32[128,512]{1,0:T(8,128)S(1)}) custom-call(f32[256,256]{1,0:T(8,128)S(1)} %bitcast.17, f32[256,256]{1,0:T(8,128)S(1)} %bitcast.18), custom_call_target="tpu_custom_call" | custom-call | flops 1000000000 | bytes 1048576 | tf_op jit(solution)/shard_map/pallas_call | solution.py:65
  34.8 5.8 %collective-permute-done.4.refs_0_ = bf16[256,512]{1,0:T(8,128)(2,1)S(1)} collective-permute-done((bf16[256,512]{1,0:T(8,128)(2,1)S(1)}, bf16[256,512]{1,0:T(8,128)(2,1)S(1)}, u32[]{:S(2)}, u32[]{:S(2)}) %collective-permute-start.4) | collective-permute-done | bytes 262176 | tf_op jit(solution)/shard_map/ppermute | solution.py:82
  41.1 0.5 collective-permute-done.8.refs_0_
  41.7 3.8 %collective-permute-start.9 = (f32[256,512]{1,0:T(8,128)S(1)}, f32[256,512]{1,0:T(8,128)S(1)}, u32[]{:S(2)}, u32[]{:S(2)}) collective-permute-start(f32[256,512]{1,0:T(8,128)S(1)} %shard_map.73), channel_id=1, source_target_pairs={{0,7},{1,0},{2,1},{3,2},{4,3},{5,4},{6,5},{7,6},{8,15},{9,8},{10,9... | collective-permute-start | bytes 1572872 | tf_op jit(solution)/shard_map/ppermute | solution.py:82
  45.4 2.2 %shard_map.77.refs_1_.refs_2_.refs_0_ = f32[512,512]{1,0:T(8,128)S(1)} custom-call(f32[512,512]{1,0:T(8,128)S(1)} %bitcast.14), custom_call_target="tpu_custom_call" | custom-call | flops 2000000000 | bytes 1048576 | tf_op jit(solution)/shard_map/pallas_call | solution.py:65
  47.8 1.0 %copy-done.2 = f32[1,512,512]{2,1,0:T(8,128)S(1)} copy-done((f32[1,512,512]{2,1,0:T(8,128)S(1)}, f32[1,512,512]{2,1,0:T(8,128)}, u32[]{:S(2)}) %copy-start.2) | copy-done | bytes 1048600
  48.9 1.8 %shard_map.78 = (f32[512,512]{1,0:T(8,128)S(1)}, f32[640,512]{1,0:T(8,128)S(1)}) custom-call(f32[512,512]{1,0:T(8,128)S(1)} %bitcast.15, f32[512,512]{1,0:T(8,128)S(1)} %shard_map.77.refs_1_.refs_2_.refs_0_, f32[128,512]{1,0:T(8,128)S(1)} %get-tuple-element.45.refs_2_), custom_call_target="tpu_custom_call" | custom-call | flops 2000000000 | bytes 1048576 | tf_op jit(solution)/shard_map/pallas_call | solution.py:65
  50.7 1.9 %collective-permute-start.11 = (f32[640,512]{1,0:T(8,128)S(1)}, f32[640,512]{1,0:T(8,128)S(1)}, u32[]{:S(2)}, u32[]{:S(2)}) collective-permute-start(f32[640,512]{1,0:T(8,128)S(1)} %get-tuple-element.46), channel_id=1, source_target_pairs={{0,16},{16,32},{32,48},{48,64},{64,80},{80,96},{96,112},{112,128},... | collective-permute-start | bytes 3932168 | tf_op jit(solution)/shard_map/ppermute | solution.py:34
  52.6 0.6 shard_map.71
  53.2 3.2 %collective-permute-done.9.refs_0_ = f32[256,512]{1,0:T(8,128)S(1)} collective-permute-done((f32[256,512]{1,0:T(8,128)S(1)}, f32[256,512]{1,0:T(8,128)S(1)}, u32[]{:S(2)}, u32[]{:S(2)}) %collective-permute-start.9) | collective-permute-done | bytes 524320 | tf_op jit(solution)/shard_map/ppermute | solution.py:82
  56.5 3.9 %collective-permute-start.10 = (f32[256,512]{1,0:T(8,128)S(1)}, f32[256,512]{1,0:T(8,128)S(1)}, u32[]{:S(2)}, u32[]{:S(2)}) collective-permute-start(f32[256,512]{1,0:T(8,128)S(1)} %shard_map.74), channel_id=1, source_target_pairs={{0,7},{1,0},{2,1},{3,2},{4,3},{5,4},{6,5},{7,6},{8,15},{9,8},{10,9... | collective-permute-start | bytes 1572872 | tf_op jit(solution)/shard_map/ppermute | solution.py:82
  60.6 9.8 %collective-permute-done.10.refs_1_ = f32[256,512]{1,0:T(8,128)S(1)} collective-permute-done((f32[256,512]{1,0:T(8,128)S(1)}, f32[256,512]{1,0:T(8,128)S(1)}, u32[]{:S(2)}, u32[]{:S(2)}) %collective-permute-start.10) | collective-permute-done | bytes 524320 | tf_op jit(solution)/shard_map/ppermute | solution.py:82
  70.5 0.5 collective-permute-done.7.refs_0_
  71.1 1.9 %collective-permute-start.12 = (f32[256,512]{1,0:T(8,128)S(1)}, f32[256,512]{1,0:T(8,128)S(1)}, u32[]{:S(2)}, u32[]{:S(2)}) collective-permute-start(f32[256,512]{1,0:T(8,128)S(1)} %shard_map.75.refs_0_.refs_1_), channel_id=1, source_target_pairs={{16,0},{32,16},{48,32},{64,48},{80,64},{96,80},{112,96},{128,112},... | collective-permute-start | bytes 1572872 | tf_op jit(solution)/shard_map/ppermute | solution.py:34
  73.0 1.0 %shard_map.81.refs_2_ = f32[512,512]{1,0:T(8,128)S(1)} custom-call(f32[512,512]{1,0:T(8,128)S(1)} %shard_map.77.refs_1_.refs_2_.refs_0_, f32[512,512]{1,0:T(8,128)S(1)} %bitcast.16), custom_call_target="tpu_custom_call" | custom-call | flops 1000000000 | bytes 1048576 | tf_op jit(solution)/shard_map/pallas_call | solution.py:65
  74.0 0.9 shard_map.82
  74.9 2.4 %collective-permute-start.13 = (f32[256,512]{1,0:T(8,128)S(1)}, f32[256,512]{1,0:T(8,128)S(1)}, u32[]{:S(2)}, u32[]{:S(2)}) collective-permute-start(f32[256,512]{1,0:T(8,128)S(1)} %shard_map.82), channel_id=1, source_target_pairs={{0,16},{16,32},{32,48},{48,64},{64,80},{80,96},{96,112},{112,128},... | collective-permute-start | bytes 1572872 | tf_op jit(solution)/shard_map/ppermute | solution.py:34
  77.3 1.6 %shard_map.79.refs_0_ = f32[256,512]{1,0:T(8,128)S(1)} custom-call(f32[256,512]{1,0:T(8,128)S(1)} %shard_map.75.refs_0_.refs_1_, f32[256,256]{1,0:T(8,128)S(1)} %get-tuple-element.42.refs_1_, f32[512,512]{1,0:T(8,128)S(1)} %shard_map.77.refs_1_.refs_2_.refs_0_, f32[640,512]{1,0:T(8,128)S(1)} %collective-permute-done.11.refs_3_), custom_call_target="tpu_custom_call" | custom-call | flops 2000000000 | bytes 1048576 | tf_op jit(solution)/shard_map/pallas_call | solution.py:65
  78.9 0.8 collective-permute-done.12.refs_2_
  79.7 0.9 shard_map.80
  80.6 6.9 %collective-permute-done.13 = f32[256,512]{1,0:T(8,128)S(1)} collective-permute-done((f32[256,512]{1,0:T(8,128)S(1)}, f32[256,512]{1,0:T(8,128)S(1)}, u32[]{:S(2)}, u32[]{:S(2)}) %collective-permute-start.13) | collective-permute-done | bytes 524320 | tf_op jit(solution)/shard_map/ppermute | solution.py:34
  87.5 0.9 subtract_bitcast_fusion
  (26 shorter events, 1.9 us)
Async XLA Ops:
  1.0 12.5 %copy-start = (bf16[1,256,512]{2,1,0:T(8,128)(2,1)S(1)}, bf16[1,256,512]{2,1,0:T(8,128)(2,1)}, u32[]{:S(2)}) copy-start(bf16[1,256,512]{2,1,0:T(8,128)(2,1)} %param.7) | copy-start | bytes 786436
  1.1 12.4 %collective-permute-start = (bf16[256,768]{1,0:T(8,128)(2,1)S(1)}, bf16[256,768]{1,0:T(8,128)(2,1)S(1)}, u32[]{:S(2)}, u32[]{:S(2)}) collective-permute-start(bf16[256,768]{1,0:T(8,128)(2,1)S(1)} %shard_map.65), channel_id=1, source_target_pairs={{0,8},{1,9},{2,10},{3,11},{4,12},{5,13},{6,14},{7,15},{8,0},{9,1},... | collective-permute-start | bytes 1179656 | tf_op jit(solution)/shard_map/ppermute | solution.py:82
  13.8 15.9 %collective-permute-start.1 = (f32[256,512]{1,0:T(8,128)S(1)}, f32[256,512]{1,0:T(8,128)S(1)}, u32[]{:S(2)}, u32[]{:S(2)}) collective-permute-start(f32[256,512]{1,0:T(8,128)S(1)} %shard_map.66), channel_id=1, source_target_pairs={{0,1},{1,2},{2,3},{3,4},{4,5},{5,6},{6,7},{7,0},{8,9},{9,10},{10,1... | collective-permute-start | bytes 1572872 | tf_op jit(solution)/shard_map/ppermute | solution.py:82
  15.8 9.0 %collective-permute-start.2 = (bf16[256,512]{1,0:T(8,128)(2,1)S(1)}, bf16[256,512]{1,0:T(8,128)(2,1)S(1)}, u32[]{:S(2)}, u32[]{:S(2)}) collective-permute-start(bf16[256,512]{1,0:T(8,128)(2,1)S(1)} %get-tuple-element.30), channel_id=1, source_target_pairs={{0,8},{1,9},{2,10},{3,11},{4,12},{5,13},{6,14},{7,15},{8,0},{9,1},... | collective-permute-start | bytes 786440 | tf_op jit(solution)/shard_map/ppermute | solution.py:82
  24.8 8.7 %copy-start.3 = (f32[1,256,256]{2,1,0:T(8,128)S(1)}, f32[1,256,256]{2,1,0:T(8,128)}, u32[]{:S(2)}) copy-start(f32[1,256,256]{2,1,0:T(8,128)} %param.8) | copy-start | bytes 786436
  24.8 8.7 %copy-start.4 = (f32[1,256,256]{2,1,0:T(8,128)S(1)}, f32[1,256,256]{2,1,0:T(8,128)}, u32[]{:S(2)}) copy-start(f32[1,256,256]{2,1,0:T(8,128)} %param.10) | copy-start | bytes 786436
  25.3 16.3 %collective-permute-start.8 = (f32[256,512]{1,0:T(8,128)S(1)}, f32[256,512]{1,0:T(8,128)S(1)}, u32[]{:S(2)}, u32[]{:S(2)}) collective-permute-start(f32[256,512]{1,0:T(8,128)S(1)} %get-tuple-element.38), channel_id=1, source_target_pairs={{0,7},{1,0},{2,1},{3,2},{4,3},{5,4},{6,5},{7,6},{8,15},{9,8},{10,9... | collective-permute-start | bytes 1572872 | tf_op jit(solution)/shard_map/ppermute | solution.py:82
  29.8 17.8 %collective-permute-start.3 = (f32[256,512]{1,0:T(8,128)S(1)}, f32[256,512]{1,0:T(8,128)S(1)}, u32[]{:S(2)}, u32[]{:S(2)}) collective-permute-start(f32[256,512]{1,0:T(8,128)S(1)} %shard_map.68), channel_id=1, source_target_pairs={{0,1},{1,2},{2,3},{3,4},{4,5},{5,6},{6,7},{7,0},{8,9},{9,10},{10,1... | collective-permute-start | bytes 1572872 | tf_op jit(solution)/shard_map/ppermute | solution.py:82
  29.9 10.8 %collective-permute-start.4 = (bf16[256,512]{1,0:T(8,128)(2,1)S(1)}, bf16[256,512]{1,0:T(8,128)(2,1)S(1)}, u32[]{:S(2)}, u32[]{:S(2)}) collective-permute-start(bf16[256,512]{1,0:T(8,128)(2,1)S(1)} %get-tuple-element.33), channel_id=1, source_target_pairs={{0,8},{1,9},{2,10},{3,11},{4,12},{5,13},{6,14},{7,15},{8,0},{9,1},... | collective-permute-start | bytes 786440 | tf_op jit(solution)/shard_map/ppermute | solution.py:82
  32.1 20.5 %collective-permute-start.6 = (bf16[256,768]{1,0:T(8,128)(2,1)S(1)}, bf16[256,768]{1,0:T(8,128)(2,1)S(1)}, u32[]{:S(2)}, u32[]{:S(2)}) collective-permute-start(bf16[256,768]{1,0:T(8,128)(2,1)S(1)} %get-tuple-element.36), channel_id=1, source_target_pairs={{0,8},{1,9},{2,10},{3,11},{4,12},{5,13},{6,14},{7,15},{8,0},{9,1},... | collective-permute-start | bytes 1179656 | tf_op jit(solution)/shard_map/ppermute | solution.py:82
  40.7 4.8 %copy-start.1 = (f32[1,512,512]{2,1,0:T(8,128)S(1)}, f32[1,512,512]{2,1,0:T(8,128)}, u32[]{:S(2)}) copy-start(f32[1,512,512]{2,1,0:T(8,128)} %param.9) | copy-start | bytes 3145732
  41.7 14.8 %collective-permute-start.9 = (f32[256,512]{1,0:T(8,128)S(1)}, f32[256,512]{1,0:T(8,128)S(1)}, u32[]{:S(2)}, u32[]{:S(2)}) collective-permute-start(f32[256,512]{1,0:T(8,128)S(1)} %shard_map.73), channel_id=1, source_target_pairs={{0,7},{1,0},{2,1},{3,2},{4,3},{5,4},{6,5},{7,6},{8,15},{9,8},{10,9... | collective-permute-start | bytes 1572872 | tf_op jit(solution)/shard_map/ppermute | solution.py:82
  47.6 1.2 %copy-start.2 = (f32[1,512,512]{2,1,0:T(8,128)S(1)}, f32[1,512,512]{2,1,0:T(8,128)}, u32[]{:S(2)}) copy-start(f32[1,512,512]{2,1,0:T(8,128)} %param.11) | copy-start | bytes 3145732
  47.7 12.8 %collective-permute-start.5 = (f32[256,512]{1,0:T(8,128)S(1)}, f32[256,512]{1,0:T(8,128)S(1)}, u32[]{:S(2)}, u32[]{:S(2)}) collective-permute-start(f32[256,512]{1,0:T(8,128)S(1)} %shard_map.70), channel_id=1, source_target_pairs={{0,1},{1,2},{2,3},{3,4},{4,5},{5,6},{6,7},{7,0},{8,9},{9,10},{10,1... | collective-permute-start | bytes 1572872 | tf_op jit(solution)/shard_map/ppermute | solution.py:82
  50.7 26.6 %collective-permute-start.11 = (f32[640,512]{1,0:T(8,128)S(1)}, f32[640,512]{1,0:T(8,128)S(1)}, u32[]{:S(2)}, u32[]{:S(2)}) collective-permute-start(f32[640,512]{1,0:T(8,128)S(1)} %get-tuple-element.46), channel_id=1, source_target_pairs={{0,16},{16,32},{32,48},{48,64},{64,80},{80,96},{96,112},{112,128},... | collective-permute-start | bytes 3932168 | tf_op jit(solution)/shard_map/ppermute | solution.py:34
  56.5 13.9 %collective-permute-start.10 = (f32[256,512]{1,0:T(8,128)S(1)}, f32[256,512]{1,0:T(8,128)S(1)}, u32[]{:S(2)}, u32[]{:S(2)}) collective-permute-start(f32[256,512]{1,0:T(8,128)S(1)} %shard_map.74), channel_id=1, source_target_pairs={{0,7},{1,0},{2,1},{3,2},{4,3},{5,4},{6,5},{7,6},{8,15},{9,8},{10,9... | collective-permute-start | bytes 1572872 | tf_op jit(solution)/shard_map/ppermute | solution.py:82
  60.5 10.5 %collective-permute-start.7 = (f32[256,512]{1,0:T(8,128)S(1)}, f32[256,512]{1,0:T(8,128)S(1)}, u32[]{:S(2)}, u32[]{:S(2)}) collective-permute-start(f32[256,512]{1,0:T(8,128)S(1)} %shard_map.72), channel_id=1, source_target_pairs={{0,1},{1,2},{2,3},{3,4},{4,5},{5,6},{6,7},{7,0},{8,9},{9,10},{10,1... | collective-permute-start | bytes 1572872 | tf_op jit(solution)/shard_map/ppermute | solution.py:82
  71.1 8.6 %collective-permute-start.12 = (f32[256,512]{1,0:T(8,128)S(1)}, f32[256,512]{1,0:T(8,128)S(1)}, u32[]{:S(2)}, u32[]{:S(2)}) collective-permute-start(f32[256,512]{1,0:T(8,128)S(1)} %shard_map.75.refs_0_.refs_1_), channel_id=1, source_target_pairs={{16,0},{32,16},{48,32},{64,48},{80,64},{96,80},{112,96},{128,112},... | collective-permute-start | bytes 1572872 | tf_op jit(solution)/shard_map/ppermute | solution.py:34
  74.9 12.6 %collective-permute-start.13 = (f32[256,512]{1,0:T(8,128)S(1)}, f32[256,512]{1,0:T(8,128)S(1)}, u32[]{:S(2)}, u32[]{:S(2)}) collective-permute-start(f32[256,512]{1,0:T(8,128)S(1)} %shard_map.82), channel_id=1, source_target_pairs={{0,16},{16,32},{32,48},{48,64},{64,80},{80,96},{96,112},{112,128},... | collective-permute-start | bytes 1572872 | tf_op jit(solution)/shard_map/ppermute | solution.py:34

commit v3 on v2

--- a/solution.py
+++ b/solution.py
@@ -88,7 +88,7 @@
 
 def whole(rows, cots, factor_in, factor_out, coupling, coupling_out):
     def gather(*lists):
-        widths = [sum(OUT if block is None else BLOCK for block in blocks) for blocks in lists]
+        widths = [BLOCK * len(blocks) for blocks in lists]
         count = sum(len(blocks) for blocks in lists)
 
         def kernel(rows_ref, cots_ref, *refs):
@@ -100,8 +100,8 @@
             for out, blocks in zip(outs, lists):
                 at = 0
                 for block in blocks:
-                    if block is None:
-                        source, width = cots_ref, OUT
+                    if isinstance(block, int):
+                        source, width = cots_ref.at[:, block * BLOCK : (block + 1) * BLOCK], BLOCK
                     else:
                         own, offset = block
                         start = (half if own else 1 - half) * (RING * BLOCK) + (place + sign * offset + RING) % RING * BLOCK
@@ -123,55 +123,72 @@
             compiler_params=pltpu.CompilerParams(vmem_limit_bytes=VMEM),
         )(pltpu.with_memory_space_constraint(rows, pltpu.HBM), pltpu.with_memory_space_constraint(cots, pltpu.HBM))
 
-    groups = ((4,), (-3, 3), (-2, 2), (-1, 1, 0))
-    (message_0,) = gather([(False, 4), None])
-    arrived = [sent(message_0, ACROSS)]
-    message_1, message_2, message_3, *own_rows = gather(
-        *[[(False, offset) for offset in group] for group in groups[1:]],
+    groups = ((4,), (-3,), (3, -2), (2, -1), (1, 0))
+    (message,) = gather([(False, 4), 0])
+    arrived = [sent(message, ACROSS)]
+    *messages, own_0, own_1, own_2, own_3, own_4 = gather(
+        [1, (False, -3)],
+        *[[(False, offset) for offset in group] for group in groups[2:]],
         *[[(True, offset) for offset in group] for group in groups],
     )
-    for message in (message_1, message_2, message_3):
+    for index, message in enumerate(messages, 1):
         arrived.append(sent(message, ACROSS))
 
-    def partials(index):
-        count = len(groups[index])
-
-        def kernel(own_ref, cots_ref, first_ref, *refs):
-            their_ref, outs = (refs[0], refs[1:]) if index else (first_ref, refs)
-            their_cots = first_ref[:, BLOCK:]
-            for at, out in enumerate(outs):
-                cut = slice(at * BLOCK, (at + 1) * BLOCK)
-                out[...] = contract_tokens(own_ref[:, cut], cots_ref[...]) + contract_tokens(their_ref[:, cut], their_cots)
-
-        operands = (own_rows[index], cots, arrived[0]) + ((arrived[index],) if index else ())
-        return pl.pallas_call(
-            kernel,
-            out_shape=[jax.ShapeDtypeStruct((BLOCK, OUT), jnp.float32)] * count,
-            cost_estimate=pl.CostEstimate(flops=count * 4 * BLOCK * BLOCK * OUT, transcendentals=0, bytes_accessed=count << 19),
-            compiler_params=pltpu.CompilerParams(vmem_limit_bytes=VMEM),
-        )(*operands)
+    def sums(mine, cots, theirs, their_cots):
+        return contract_tokens(mine, cots) + contract_tokens(theirs, their_cots)
+
+    def first(mine, cots, zero):
+        return (sums(mine, cots[:, :BLOCK], zero[:, :BLOCK], zero[:, BLOCK:]),)
+
+    def second(mine_0, mine_1, cots, zero, one):
+        near, far = zero[:, BLOCK:], one[:, :BLOCK]
+        return (
+            sums(mine_0, cots[:, BLOCK:], zero[:, :BLOCK], far),
+            sums(mine_1, cots[:, :BLOCK], one[:, BLOCK:], near),
+            sums(mine_1, cots[:, BLOCK:], one[:, BLOCK:], far),
+        )
+
+    def later(mine, cots, zero, one, theirs):
+        return tuple(
+            sums(mine[:, at : at + BLOCK], cots[:, part * BLOCK : (part + 1) * BLOCK], theirs[:, at : at + BLOCK], their_cots)
+            for at in (0, BLOCK)
+            for part, their_cots in enumerate((zero[:, BLOCK:], one[:, :BLOCK]))
+        )
 
     partial = {}
-    for index, group in enumerate(groups):
-        for offset, value in zip(group, partials(index)):
-            partial[offset] = value
-
-    def total(*values):
-        return local(lambda first, *rest: (sum(rest, first),), 10**6, [(BLOCK, OUT)], *values)[0]
-
-    def hop(value, pairs, offset):
-        return total(sent(value, pairs), partial[offset])
-
-    long_0 = partial[4]
-    short_0 = partial[-3]
-    long_1 = hop(long_0, LONG, 3)
-    short_1 = hop(short_0, SHORT, -2)
-    long_2 = hop(long_1, LONG, 2)
-    short_2 = hop(short_1, SHORT, -1)
-    long_3 = hop(long_2, LONG, 1)
-    short_3 = sent(short_2, SHORT)
-    long_4 = sent(long_3, LONG)
-    gradient = total(long_4, short_3, partial[0])
+    tile, work = (BLOCK, BLOCK), 4 * BLOCK**3
+    partial[4, 0] = local(first, work, [tile], own_0, cots, arrived[0])[0]
+    partial[4, 1], partial[-3, 0], partial[-3, 1] = local(
+        second, 3 * work, [tile] * 3, own_0, own_1, cots, arrived[0], arrived[1]
+    )
+    for index, mine in ((2, own_2), (3, own_3), (4, own_4)):
+        values = local(later, 4 * work, [tile] * 4, mine, cots, arrived[0], arrived[1], arrived[index])
+        for at, offset in enumerate(groups[index]):
+            partial[offset, 0], partial[offset, 1] = values[2 * at : 2 * at + 2]
+
+    def hop(value, pairs, offset, part):
+        value = sent(value, pairs)
+        return local(lambda one, two: (one + two,), 10**6, [tile], value, partial[offset, part])[0]
+
+    long_way = [partial[4, 0], partial[4, 1]]
+    short_way = [partial[-3, 0], partial[-3, 1]]
+    marks = []
+    for long_next, short_next in ((3, -2), (2, -1), (1, None)):
+        for part in range(2):
+            long_way[part] = hop(long_way[part], LONG, long_next, part)
+        for part in range(2):
+            if short_next is None:
+                short_way[part] = sent(short_way[part], SHORT)
+            else:
+                short_way[part] = hop(short_way[part], SHORT, short_next, part)
+        marks.append(long_way[1])
+    long_1, long_2, long_3 = marks
+    long_way = [sent(long_way[part], LONG) for part in range(2)]
+
+    def whole_gradient(*values):
+        return (jnp.concatenate([values[part] + values[2 + part] + values[4 + part] for part in range(2)], axis=1),)
+
+    (gradient,) = local(whole_gradient, 10**6, [(BLOCK, OUT)], *long_way, *short_way, partial[0, 0], partial[0, 1])
 
     square, wide, full = (BLOCK, BLOCK), (BLOCK, OUT), (OUT, OUT)
 

time: 89.5 us -> 99.7 us (1.11)
  starting transfers between devices: 28.6 us -> 36.2 us
  waiting for transfers between devices: 43.1 us -> 46.9 us
    ppermute x11 -> x19, starting transfers between devices: 22.3 us -> 26.4 us  [sent(): return lax.ppermute(value, AXES, pairs)]
    ppermute x3, starting transfers between devices: 6.25 us -> 9.82 us  [passed_along(): lax.ppermute(value, 'pipe', [(source, source + steps) for source in range...]
    ppermute x11 -> x19, waiting for transfers between devices: 35.3 us -> 38.7 us  [sent(): return lax.ppermute(value, AXES, pairs)]
    pallas_call x13 -> x23, Pallas kernels: 9.96 us -> 12 us  [local(): pl.pallas_call(kernel, out_shape=[jax.ShapeDtypeStruct(shape, jnp.float32...]
    pallas_call x4 -> x0, Pallas kernels: 1.84 us -> none  [partials(): pl.pallas_call(kernel, out_shape=[jax.ShapeDtypeStruct((BLOCK, OUT), jnp....]
  transfers between devices with their start and end apart: 14 -> 22, of which waited for: 9 -> 14; matrix products, arithmetic and copies ran while one was open for 0% -> 0% of each run, Pallas kernels for 15% -> 13%
where the time goes in v3:
time: 99.7 us; the launch traced here: 99.5 us
  waiting for transfers between devices  46.9 us (47%)
  starting transfers between devices  36.2 us (36%)
  Pallas kernels  14.8 us (15%)
    ppermute x19, waiting for transfers between devices, sent(): return lax.ppermute(value, AXES, pairs)  38.7 us
    ppermute x19, starting transfers between devices, sent(): return lax.ppermute(value, AXES, pairs)  26.4 us
    pallas_call x23, Pallas kernels, local(): pl.pallas_call(kernel, out_shape=[jax.ShapeDtypeStruct(shape, jnp.float32...  12 us
    ppermute x3, starting transfers between devices, passed_along(): lax.ppermute(value, 'pipe', [(source, source + steps) for source in range...  9.82 us
    ppermute x3, waiting for transfers between devices, passed_along(): lax.ppermute(value, 'pipe', [(source, source + steps) for source in range...  8.24 us
    pallas_call x2, Pallas kernels, gather(): pl.pallas_call(kernel, out_shape=[jax.ShapeDtypeStruct((TOKENS, width), j...  2.75 us
  transfers between devices with their start and end apart: 22, of which 14 were waited for; matrix products, arithmetic and copies ran while one was open for 0% of the time, Pallas kernels for 13%

profile of v3, /device:TPU:2, one launch (start us, length us, event | category | flops | bytes accessed | tf_op | source)
XLA Modules:
  0.0 99.5 jit_solution(5302056197849906104)
XLA Ops:
  0.0 1.8 %shard_map.64 = (bf16[256,512]{1,0:T(8,128)(2,1)S(1)}, bf16[256,512]{1,0:T(8,128)(2,1)S(1)}, bf16[256,512]{1,0:T(8,128)(2,1)S(1)}, bf16[256,512]{1,0:T(8,128)(2,...) custom-call(bf16[256,4096]{1,0:T(8,128)(2,1)} %bitcast.20, ...), custom_call_target="tpu_custom_call" | custom-call | flops 100000000 | bytes 4194304 | tf_op jit(solution)/shard_map/pallas_call | solution.py:116
  1.8 2.2 %collective-permute-start.2 = (bf16[256,512]{1,0:T(8,128)(2,1)S(1)}, bf16[256,512]{1,0:T(8,128)(2,1)S(1)}, u32[]{:S(2)}, u32[]{:S(2)}) collective-permute-start(bf16[256,512]{1,0:T(8,128)(2,1)S(1)} %get-tuple-element.40), channel_id=1, source_target_pairs={{0,8},{1,9},{2,10},{3,11},{4,12},{5,13},{6,14},{7,15},{8,0},{9,1},... | collective-permute-start | bytes 786440 | tf_op jit(solution)/shard_map/ppermute | solution.py:82
  5.0 1.5 %collective-permute-start = (bf16[256,512]{1,0:T(8,128)(2,1)S(1)}, bf16[256,512]{1,0:T(8,128)(2,1)S(1)}, u32[]{:S(2)}, u32[]{:S(2)}) collective-permute-start(bf16[256,512]{1,0:T(8,128)(2,1)S(1)} %shard_map.65), channel_id=1, source_target_pairs={{0,8},{1,9},{2,10},{3,11},{4,12},{5,13},{6,14},{7,15},{8,0},{9,1},... | collective-permute-start | bytes 786440 | tf_op jit(solution)/shard_map/ppermute | solution.py:82
  6.5 2.1 %collective-permute-start.3 = (bf16[256,512]{1,0:T(8,128)(2,1)S(1)}, bf16[256,512]{1,0:T(8,128)(2,1)S(1)}, u32[]{:S(2)}, u32[]{:S(2)}) collective-permute-start(bf16[256,512]{1,0:T(8,128)(2,1)S(1)} %get-tuple-element.41), channel_id=1, source_target_pairs={{0,8},{1,9},{2,10},{3,11},{4,12},{5,13},{6,14},{7,15},{8,0},{9,1},... | collective-permute-start | bytes 786440 | tf_op jit(solution)/shard_map/ppermute | solution.py:82
  8.6 3.9 %collective-permute-done.2.refs_3_.refs_4_ = bf16[256,512]{1,0:T(8,128)(2,1)S(1)} collective-permute-done((bf16[256,512]{1,0:T(8,128)(2,1)S(1)}, bf16[256,512]{1,0:T(8,128)(2,1)S(1)}, u32[]{:S(2)}, u32[]{:S(2)}) %collective-permute-start.2) | collective-permute-done | bytes 262176 | tf_op jit(solution)/shard_map/ppermute | solution.py:82
  12.6 5.6 %collective-permute-done.refs_2_.refs_3_ = bf16[256,512]{1,0:T(8,128)(2,1)S(1)} collective-permute-done((bf16[256,512]{1,0:T(8,128)(2,1)S(1)}, bf16[256,512]{1,0:T(8,128)(2,1)S(1)}, u32[]{:S(2)}, u32[]{:S(2)}) %collective-permute-start) | collective-permute-done | bytes 262176 | tf_op jit(solution)/shard_map/ppermute | solution.py:82
  18.6 2.0 %collective-permute-start.9 = (f32[256,256]{1,0:T(8,128)S(1)}, f32[256,256]{1,0:T(8,128)S(1)}, u32[]{:S(2)}, u32[]{:S(2)}) collective-permute-start(f32[256,256]{1,0:T(8,128)S(1)} %get-tuple-element.50), channel_id=1, source_target_pairs={{0,1},{1,2},{2,3},{3,4},{4,5},{5,6},{6,7},{7,0},{8,9},{9,10},{10,1... | collective-permute-start | bytes 786440 | tf_op jit(solution)/shard_map/ppermute | solution.py:82
  20.6 2.1 %collective-permute-start.5 = (bf16[256,512]{1,0:T(8,128)(2,1)S(1)}, bf16[256,512]{1,0:T(8,128)(2,1)S(1)}, u32[]{:S(2)}, u32[]{:S(2)}) collective-permute-start(bf16[256,512]{1,0:T(8,128)(2,1)S(1)} %get-tuple-element.44), channel_id=1, source_target_pairs={{0,8},{1,9},{2,10},{3,11},{4,12},{5,13},{6,14},{7,15},{8,0},{9,1},... | collective-permute-start | bytes 786440 | tf_op jit(solution)/shard_map/ppermute | solution.py:82
  23.2 5.7 %collective-permute-done.9.refs_0_ = f32[256,256]{1,0:T(8,128)S(1)} collective-permute-done((f32[256,256]{1,0:T(8,128)S(1)}, f32[256,256]{1,0:T(8,128)S(1)}, u32[]{:S(2)}, u32[]{:S(2)}) %collective-permute-start.9) | collective-permute-done | bytes 262176 | tf_op jit(solution)/shard_map/ppermute | solution.py:82
  29.0 1.3 %shard_map.82 = (f32[256,256]{1,0:T(8,128)S(1)}, f32[256,256]{1,0:T(8,128)S(1)}, f32[256,256]{1,0:T(8,128)S(1)}, f32[128,512]{1,0:T(8,128)S(1)}) custom-call(f32[256,256]{1,0:T(8,128)S(1)} %bitcast.18, f32[256,256]{1,0:T(8,128)S(1)} %bitcast.19), custom_call_target="tpu_custom_call" | custom-call | flops 1000000000 | bytes 1048576 | tf_op jit(solution)/shard_map/pallas_call | solution.py:65
  31.6 2.2 %shard_map.83.refs_1_.refs_2_.refs_0_ = f32[512,512]{1,0:T(8,128)S(1)} custom-call(f32[512,512]{1,0:T(8,128)S(1)} %bitcast.15), custom_call_target="tpu_custom_call" | custom-call | flops 2000000000 | bytes 1048576 | tf_op jit(solution)/shard_map/pallas_call | solution.py:65
  33.8 2.8 %collective-permute-done.10.refs_0_ = f32[256,256]{1,0:T(8,128)S(1)} collective-permute-done((f32[256,256]{1,0:T(8,128)S(1)}, f32[256,256]{1,0:T(8,128)S(1)}, u32[]{:S(2)}, u32[]{:S(2)}) %collective-permute-start.10) | collective-permute-done | bytes 262176 | tf_op jit(solution)/shard_map/ppermute | solution.py:82
  36.6 1.8 %shard_map.84 = (f32[512,512]{1,0:T(8,128)S(1)}, f32[640,512]{1,0:T(8,128)S(1)}) custom-call(f32[512,512]{1,0:T(8,128)S(1)} %bitcast.16, f32[512,512]{1,0:T(8,128)S(1)} %shard_map.83.refs_1_.refs_2_.refs_0_, f32[128,512]{1,0:T(8,128)S(1)} %get-tuple-element.65.refs_2_), custom_call_target="tpu_custom_call" | custom-call | flops 2000000000 | bytes 1048576 | tf_op jit(solution)/shard_map/pallas_call | solution.py:65
  38.5 1.9 %collective-permute-start.19 = (f32[640,512]{1,0:T(8,128)S(1)}, f32[640,512]{1,0:T(8,128)S(1)}, u32[]{:S(2)}, u32[]{:S(2)}) collective-permute-start(f32[640,512]{1,0:T(8,128)S(1)} %get-tuple-element.66), channel_id=1, source_target_pairs={{0,16},{16,32},{32,48},{48,64},{64,80},{80,96},{96,112},{112,128},... | collective-permute-start | bytes 3932168 | tf_op jit(solution)/shard_map/ppermute | solution.py:34
  41.3 1.3 %collective-permute-start.13 = (f32[256,256]{1,0:T(8,128)S(1)}, f32[256,256]{1,0:T(8,128)S(1)}, u32[]{:S(2)}, u32[]{:S(2)}) collective-permute-start(f32[256,256]{1,0:T(8,128)S(1)} %get-tuple-element.54), channel_id=1, source_target_pairs={{0,7},{1,0},{2,1},{3,2},{4,3},{5,4},{6,5},{7,6},{8,15},{9,8},{10,9... | collective-permute-start | bytes 786440 | tf_op jit(solution)/shard_map/ppermute | solution.py:82
  43.6 2.1 %collective-permute-start.7 = (bf16[256,512]{1,0:T(8,128)(2,1)S(1)}, bf16[256,512]{1,0:T(8,128)(2,1)S(1)}, u32[]{:S(2)}, u32[]{:S(2)}) collective-permute-start(bf16[256,512]{1,0:T(8,128)(2,1)S(1)} %get-tuple-element.47), channel_id=1, source_target_pairs={{0,8},{1,9},{2,10},{3,11},{4,12},{5,13},{6,14},{7,15},{8,0},{9,1},... | collective-permute-start | bytes 786440 | tf_op jit(solution)/shard_map/ppermute | solution.py:82
  45.7 1.1 %collective-permute-done.16.refs_0_ = f32[256,256]{1,0:T(8,128)S(1)} collective-permute-done((f32[256,256]{1,0:T(8,128)S(1)}, f32[256,256]{1,0:T(8,128)S(1)}, u32[]{:S(2)}, u32[]{:S(2)}) %collective-permute-start.16) | collective-permute-done | bytes 262176 | tf_op jit(solution)/shard_map/ppermute | solution.py:82
  46.9 2.1 %collective-permute-start.17 = (f32[256,256]{1,0:T(8,128)S(1)}, f32[256,256]{1,0:T(8,128)S(1)}, u32[]{:S(2)}, u32[]{:S(2)}) collective-permute-start(f32[256,256]{1,0:T(8,128)S(1)} %shard_map.79), channel_id=1, source_target_pairs={{0,7},{1,0},{2,1},{3,2},{4,3},{5,4},{6,5},{7,6},{8,15},{9,8},{10,9... | collective-permute-start | bytes 786440 | tf_op jit(solution)/shard_map/ppermute | solution.py:82
  49.0 2.8 %collective-permute-done.13.refs_0_ = f32[256,256]{1,0:T(8,128)S(1)} collective-permute-done((f32[256,256]{1,0:T(8,128)S(1)}, f32[256,256]{1,0:T(8,128)S(1)}, u32[]{:S(2)}, u32[]{:S(2)}) %collective-permute-start.13) | collective-permute-done | bytes 262176 | tf_op jit(solution)/shard_map/ppermute | solution.py:82
  51.8 2.4 %collective-permute-start.14 = (f32[256,256]{1,0:T(8,128)S(1)}, f32[256,256]{1,0:T(8,128)S(1)}, u32[]{:S(2)}, u32[]{:S(2)}) collective-permute-start(f32[256,256]{1,0:T(8,128)S(1)} %shard_map.77), channel_id=1, source_target_pairs={{0,7},{1,0},{2,1},{3,2},{4,3},{5,4},{6,5},{7,6},{8,15},{9,8},{10,9... | collective-permute-start | bytes 786440 | tf_op jit(solution)/shard_map/ppermute | solution.py:82
  55.5 2.6 %collective-permute-start.18 = (f32[256,256]{1,0:T(8,128)S(1)}, f32[256,256]{1,0:T(8,128)S(1)}, u32[]{:S(2)}, u32[]{:S(2)}) collective-permute-start(f32[256,256]{1,0:T(8,128)S(1)} %shard_map.80), channel_id=1, source_target_pairs={{0,7},{1,0},{2,1},{3,2},{4,3},{5,4},{6,5},{7,6},{8,15},{9,8},{10,9... | collective-permute-start | bytes 786440 | tf_op jit(solution)/shard_map/ppermute | solution.py:82
  58.1 1.1 %collective-permute-done.14.refs_0_ = f32[256,256]{1,0:T(8,128)S(1)} collective-permute-done((f32[256,256]{1,0:T(8,128)S(1)}, f32[256,256]{1,0:T(8,128)S(1)}, u32[]{:S(2)}, u32[]{:S(2)}) %collective-permute-start.14) | collective-permute-done | bytes 262176 | tf_op jit(solution)/shard_map/ppermute | solution.py:82
  59.2 3.0 %collective-permute-start.15 = (f32[256,256]{1,0:T(8,128)S(1)}, f32[256,256]{1,0:T(8,128)S(1)}, u32[]{:S(2)}, u32[]{:S(2)}) collective-permute-start(f32[256,256]{1,0:T(8,128)S(1)} %shard_map.78), channel_id=1, source_target_pairs={{0,7},{1,0},{2,1},{3,2},{4,3},{5,4},{6,5},{7,6},{8,15},{9,8},{10,9... | collective-permute-start | bytes 786440 | tf_op jit(solution)/shard_map/ppermute | solution.py:82
  62.2 2.3 %collective-permute-done.11.refs_0_ = f32[256,256]{1,0:T(8,128)S(1)} collective-permute-done((f32[256,256]{1,0:T(8,128)S(1)}, f32[256,256]{1,0:T(8,128)S(1)}, u32[]{:S(2)}, u32[]{:S(2)}) %collective-permute-start.11) | collective-permute-done | bytes 262176 | tf_op jit(solution)/shard_map/ppermute | solution.py:82
  64.7 5.5 %collective-permute-done.6.refs_0_ = f32[256,256]{1,0:T(8,128)S(1)} collective-permute-done((f32[256,256]{1,0:T(8,128)S(1)}, f32[256,256]{1,0:T(8,128)S(1)}, u32[]{:S(2)}, u32[]{:S(2)}) %collective-permute-start.6) | collective-permute-done | bytes 262176 | tf_op jit(solution)/shard_map/ppermute | solution.py:82
  70.4 4.8 %collective-permute-done.12.refs_1_ = f32[256,256]{1,0:T(8,128)S(1)} collective-permute-done((f32[256,256]{1,0:T(8,128)S(1)}, f32[256,256]{1,0:T(8,128)S(1)}, u32[]{:S(2)}, u32[]{:S(2)}) %collective-permute-start.12) | collective-permute-done | bytes 262176 | tf_op jit(solution)/shard_map/ppermute | solution.py:82
  75.3 2.8 %collective-permute-done.8.refs_0_ = f32[256,256]{1,0:T(8,128)S(1)} collective-permute-done((f32[256,256]{1,0:T(8,128)S(1)}, f32[256,256]{1,0:T(8,128)S(1)}, u32[]{:S(2)}, u32[]{:S(2)}) %collective-permute-start.8) | collective-permute-done | bytes 262176 | tf_op jit(solution)/shard_map/ppermute | solution.py:82
  78.2 6.0 %collective-permute-start.20 = (f32[256,512]{1,0:T(8,128)S(1)}, f32[256,512]{1,0:T(8,128)S(1)}, u32[]{:S(2)}, u32[]{:S(2)}) collective-permute-start(f32[256,512]{1,0:T(8,128)S(1)} %shard_map.81.refs_0_.refs_1_), channel_id=1, source_target_pairs={{16,0},{32,16},{48,32},{64,48},{80,64},{96,80},{112,96},{128,112},... | collective-permute-start | bytes 1572872 | tf_op jit(solution)/shard_map/ppermute | solution.py:34
  86.0 1.9 %collective-permute-start.21 = (f32[256,512]{1,0:T(8,128)S(1)}, f32[256,512]{1,0:T(8,128)S(1)}, u32[]{:S(2)}, u32[]{:S(2)}) collective-permute-start(f32[256,512]{1,0:T(8,128)S(1)} %shard_map.88), channel_id=1, source_target_pairs={{0,16},{16,32},{32,48},{48,64},{64,80},{80,96},{96,112},{112,128},... | collective-permute-start | bytes 1572872 | tf_op jit(solution)/shard_map/ppermute | solution.py:34
  87.9 1.6 %shard_map.85.refs_0_ = f32[256,512]{1,0:T(8,128)S(1)} custom-call(f32[256,512]{1,0:T(8,128)S(1)} %shard_map.81.refs_0_.refs_1_, f32[256,256]{1,0:T(8,128)S(1)} %get-tuple-element.62.refs_1_, f32[512,512]{1,0:T(8,128)S(1)} %shard_map.83.refs_1_.refs_2_.refs_0_, f32[640,512]{1,0:T(8,128)S(1)} %collective-permute-done.19.refs_3_), custom_call_target="tpu_custom_call" | custom-call | flops 2000000000 | bytes 1048576 | tf_op jit(solution)/shard_map/pallas_call | solution.py:65
  89.5 1.3 %collective-permute-done.20.refs_2_ = f32[256,512]{1,0:T(8,128)S(1)} collective-permute-done((f32[256,512]{1,0:T(8,128)S(1)}, f32[256,512]{1,0:T(8,128)S(1)}, u32[]{:S(2)}, u32[]{:S(2)}) %collective-permute-start.20) | collective-permute-done | bytes 524320 | tf_op jit(solution)/shard_map/ppermute | solution.py:34
  91.7 6.9 %collective-permute-done.21 = f32[256,512]{1,0:T(8,128)S(1)} collective-permute-done((f32[256,512]{1,0:T(8,128)S(1)}, f32[256,512]{1,0:T(8,128)S(1)}, u32[]{:S(2)}, u32[]{:S(2)}) %collective-permute-start.21) | collective-permute-done | bytes 524320 | tf_op jit(solution)/shard_map/ppermute | solution.py:34
  (48 shorter events, 10.6 us)
Async XLA Ops:
  1.8 16.4 %copy-start = (bf16[1,256,512]{2,1,0:T(8,128)(2,1)S(1)}, bf16[1,256,512]{2,1,0:T(8,128)(2,1)}, u32[]{:S(2)}) copy-start(bf16[1,256,512]{2,1,0:T(8,128)(2,1)} %param.7) | copy-start | bytes 786436
  1.8 10.8 %collective-permute-start.2 = (bf16[256,512]{1,0:T(8,128)(2,1)S(1)}, bf16[256,512]{1,0:T(8,128)(2,1)S(1)}, u32[]{:S(2)}, u32[]{:S(2)}) collective-permute-start(bf16[256,512]{1,0:T(8,128)(2,1)S(1)} %get-tuple-element.40), channel_id=1, source_target_pairs={{0,8},{1,9},{2,10},{3,11},{4,12},{5,13},{6,14},{7,15},{8,0},{9,1},... | collective-permute-start | bytes 786440 | tf_op jit(solution)/shard_map/ppermute | solution.py:82
  5.0 13.2 %collective-permute-start = (bf16[256,512]{1,0:T(8,128)(2,1)S(1)}, bf16[256,512]{1,0:T(8,128)(2,1)S(1)}, u32[]{:S(2)}, u32[]{:S(2)}) collective-permute-start(bf16[256,512]{1,0:T(8,128)(2,1)S(1)} %shard_map.65), channel_id=1, source_target_pairs={{0,8},{1,9},{2,10},{3,11},{4,12},{5,13},{6,14},{7,15},{8,0},{9,1},... | collective-permute-start | bytes 786440 | tf_op jit(solution)/shard_map/ppermute | solution.py:82
  6.5 16.2 %collective-permute-start.3 = (bf16[256,512]{1,0:T(8,128)(2,1)S(1)}, bf16[256,512]{1,0:T(8,128)(2,1)S(1)}, u32[]{:S(2)}, u32[]{:S(2)}) collective-permute-start(bf16[256,512]{1,0:T(8,128)(2,1)S(1)} %get-tuple-element.41), channel_id=1, source_target_pairs={{0,8},{1,9},{2,10},{3,11},{4,12},{5,13},{6,14},{7,15},{8,0},{9,1},... | collective-permute-start | bytes 786440 | tf_op jit(solution)/shard_map/ppermute | solution.py:82
  18.6 10.4 %copy-start.3 = (f32[1,256,256]{2,1,0:T(8,128)S(1)}, f32[1,256,256]{2,1,0:T(8,128)}, u32[]{:S(2)}) copy-start(f32[1,256,256]{2,1,0:T(8,128)} %param.8) | copy-start | bytes 786436
  18.6 10.4 %copy-start.4 = (f32[1,256,256]{2,1,0:T(8,128)S(1)}, f32[1,256,256]{2,1,0:T(8,128)}, u32[]{:S(2)}) copy-start(f32[1,256,256]{2,1,0:T(8,128)} %param.10) | copy-start | bytes 786436
  18.6 10.3 %collective-permute-start.9 = (f32[256,256]{1,0:T(8,128)S(1)}, f32[256,256]{1,0:T(8,128)S(1)}, u32[]{:S(2)}, u32[]{:S(2)}) collective-permute-start(f32[256,256]{1,0:T(8,128)S(1)} %get-tuple-element.50), channel_id=1, source_target_pairs={{0,1},{1,2},{2,3},{3,4},{4,5},{5,6},{6,7},{7,0},{8,9},{9,10},{10,1... | collective-permute-start | bytes 786440 | tf_op jit(solution)/shard_map/ppermute | solution.py:82
  20.6 10.2 %collective-permute-start.5 = (bf16[256,512]{1,0:T(8,128)(2,1)S(1)}, bf16[256,512]{1,0:T(8,128)(2,1)S(1)}, u32[]{:S(2)}, u32[]{:S(2)}) collective-permute-start(bf16[256,512]{1,0:T(8,128)(2,1)S(1)} %get-tuple-element.44), channel_id=1, source_target_pairs={{0,8},{1,9},{2,10},{3,11},{4,12},{5,13},{6,14},{7,15},{8,0},{9,1},... | collective-permute-start | bytes 786440 | tf_op jit(solution)/shard_map/ppermute | solution.py:82
  28.9 7.7 %collective-permute-start.10 = (f32[256,256]{1,0:T(8,128)S(1)}, f32[256,256]{1,0:T(8,128)S(1)}, u32[]{:S(2)}, u32[]{:S(2)}) collective-permute-start(f32[256,256]{1,0:T(8,128)S(1)} %shard_map.74), channel_id=1, source_target_pairs={{0,1},{1,2},{2,3},{3,4},{4,5},{5,6},{6,7},{7,0},{8,9},{9,10},{10,1... | collective-permute-start | bytes 786440 | tf_op jit(solution)/shard_map/ppermute | solution.py:82
  30.4 1.2 %copy-start.1 = (f32[1,512,512]{2,1,0:T(8,128)S(1)}, f32[1,512,512]{2,1,0:T(8,128)}, u32[]{:S(2)}) copy-start(f32[1,512,512]{2,1,0:T(8,128)} %param.9) | copy-start | bytes 3145732
  30.7 11.9 %collective-permute-start.1 = (f32[256,256]{1,0:T(8,128)S(1)}, f32[256,256]{1,0:T(8,128)S(1)}, u32[]{:S(2)}, u32[]{:S(2)}) collective-permute-start(f32[256,256]{1,0:T(8,128)S(1)} %shard_map.66), channel_id=1, source_target_pairs={{0,1},{1,2},{2,3},{3,4},{4,5},{5,6},{6,7},{7,0},{8,9},{9,10},{10,1... | collective-permute-start | bytes 786440 | tf_op jit(solution)/shard_map/ppermute | solution.py:82
  31.6 5.0 %copy-start.2 = (f32[1,512,512]{2,1,0:T(8,128)S(1)}, f32[1,512,512]{2,1,0:T(8,128)}, u32[]{:S(2)}) copy-start(f32[1,512,512]{2,1,0:T(8,128)} %param.11) | copy-start | bytes 3145732
  38.5 49.5 %collective-permute-start.19 = (f32[640,512]{1,0:T(8,128)S(1)}, f32[640,512]{1,0:T(8,128)S(1)}, u32[]{:S(2)}, u32[]{:S(2)}) collective-permute-start(f32[640,512]{1,0:T(8,128)S(1)} %get-tuple-element.66), channel_id=1, source_target_pairs={{0,16},{16,32},{32,48},{48,64},{64,80},{80,96},{96,112},{112,128},... | collective-permute-start | bytes 3932168 | tf_op jit(solution)/shard_map/ppermute | solution.py:34
  40.4 6.5 %collective-permute-start.16 = (f32[256,256]{1,0:T(8,128)S(1)}, f32[256,256]{1,0:T(8,128)S(1)}, u32[]{:S(2)}, u32[]{:S(2)}) collective-permute-start(f32[256,256]{1,0:T(8,128)S(1)} %get-tuple-element.57), channel_id=1, source_target_pairs={{0,7},{1,0},{2,1},{3,2},{4,3},{5,4},{6,5},{7,6},{8,15},{9,8},{10,9... | collective-permute-start | bytes 786440 | tf_op jit(solution)/shard_map/ppermute | solution.py:82
  41.3 10.5 %collective-permute-start.13 = (f32[256,256]{1,0:T(8,128)S(1)}, f32[256,256]{1,0:T(8,128)S(1)}, u32[]{:S(2)}, u32[]{:S(2)}) collective-permute-start(f32[256,256]{1,0:T(8,128)S(1)} %get-tuple-element.54), channel_id=1, source_target_pairs={{0,7},{1,0},{2,1},{3,2},{4,3},{5,4},{6,5},{7,6},{8,15},{9,8},{10,9... | collective-permute-start | bytes 786440 | tf_op jit(solution)/shard_map/ppermute | solution.py:82
  42.6 11.6 %collective-permute-start.4 = (f32[256,256]{1,0:T(8,128)S(1)}, f32[256,256]{1,0:T(8,128)S(1)}, u32[]{:S(2)}, u32[]{:S(2)}) collective-permute-start(f32[256,256]{1,0:T(8,128)S(1)} %shard_map.68), channel_id=1, source_target_pairs={{0,1},{1,2},{2,3},{3,4},{4,5},{5,6},{6,7},{7,0},{8,9},{9,10},{10,1... | collective-permute-start | bytes 786440 | tf_op jit(solution)/shard_map/ppermute | solution.py:82
  43.6 10.6 %collective-permute-start.7 = (bf16[256,512]{1,0:T(8,128)(2,1)S(1)}, bf16[256,512]{1,0:T(8,128)(2,1)S(1)}, u32[]{:S(2)}, u32[]{:S(2)}) collective-permute-start(bf16[256,512]{1,0:T(8,128)(2,1)S(1)} %get-tuple-element.47), channel_id=1, source_target_pairs={{0,8},{1,9},{2,10},{3,11},{4,12},{5,13},{6,14},{7,15},{8,0},{9,1},... | collective-permute-start | bytes 786440 | tf_op jit(solution)/shard_map/ppermute | solution.py:82
  46.9 8.6 %collective-permute-start.17 = (f32[256,256]{1,0:T(8,128)S(1)}, f32[256,256]{1,0:T(8,128)S(1)}, u32[]{:S(2)}, u32[]{:S(2)}) collective-permute-start(f32[256,256]{1,0:T(8,128)S(1)} %shard_map.79), channel_id=1, source_target_pairs={{0,7},{1,0},{2,1},{3,2},{4,3},{5,4},{6,5},{7,6},{8,15},{9,8},{10,9... | collective-permute-start | bytes 786440 | tf_op jit(solution)/shard_map/ppermute | solution.py:82
  51.8 7.4 %collective-permute-start.14 = (f32[256,256]{1,0:T(8,128)S(1)}, f32[256,256]{1,0:T(8,128)S(1)}, u32[]{:S(2)}, u32[]{:S(2)}) collective-permute-start(f32[256,256]{1,0:T(8,128)S(1)} %shard_map.77), channel_id=1, source_target_pairs={{0,7},{1,0},{2,1},{3,2},{4,3},{5,4},{6,5},{7,6},{8,15},{9,8},{10,9... | collective-permute-start | bytes 786440 | tf_op jit(solution)/shard_map/ppermute | solution.py:82
  54.2 10.4 %collective-permute-start.11 = (f32[256,256]{1,0:T(8,128)S(1)}, f32[256,256]{1,0:T(8,128)S(1)}, u32[]{:S(2)}, u32[]{:S(2)}) collective-permute-start(f32[256,256]{1,0:T(8,128)S(1)} %shard_map.75), channel_id=1, source_target_pairs={{0,1},{1,2},{2,3},{3,4},{4,5},{5,6},{6,7},{7,0},{8,9},{9,10},{10,1... | collective-permute-start | bytes 786440 | tf_op jit(solution)/shard_map/ppermute | solution.py:82
  54.2 16.0 %collective-permute-start.6 = (f32[256,256]{1,0:T(8,128)S(1)}, f32[256,256]{1,0:T(8,128)S(1)}, u32[]{:S(2)}, u32[]{:S(2)}) collective-permute-start(f32[256,256]{1,0:T(8,128)S(1)} %shard_map.70), channel_id=1, source_target_pairs={{0,1},{1,2},{2,3},{3,4},{4,5},{5,6},{6,7},{7,0},{8,9},{9,10},{10,1... | collective-permute-start | bytes 786440 | tf_op jit(solution)/shard_map/ppermute | solution.py:82
  55.5 14.8 %collective-permute-start.18 = (f32[256,256]{1,0:T(8,128)S(1)}, f32[256,256]{1,0:T(8,128)S(1)}, u32[]{:S(2)}, u32[]{:S(2)}) collective-permute-start(f32[256,256]{1,0:T(8,128)S(1)} %shard_map.80), channel_id=1, source_target_pairs={{0,7},{1,0},{2,1},{3,2},{4,3},{5,4},{6,5},{7,6},{8,15},{9,8},{10,9... | collective-permute-start | bytes 786440 | tf_op jit(solution)/shard_map/ppermute | solution.py:82
  59.2 11.2 %collective-permute-start.15 = (f32[256,256]{1,0:T(8,128)S(1)}, f32[256,256]{1,0:T(8,128)S(1)}, u32[]{:S(2)}, u32[]{:S(2)}) collective-permute-start(f32[256,256]{1,0:T(8,128)S(1)} %shard_map.78), channel_id=1, source_target_pairs={{0,7},{1,0},{2,1},{3,2},{4,3},{5,4},{6,5},{7,6},{8,15},{9,8},{10,9... | collective-permute-start | bytes 786440 | tf_op jit(solution)/shard_map/ppermute | solution.py:82
  64.6 10.7 %collective-permute-start.12 = (f32[256,256]{1,0:T(8,128)S(1)}, f32[256,256]{1,0:T(8,128)S(1)}, u32[]{:S(2)}, u32[]{:S(2)}) collective-permute-start(f32[256,256]{1,0:T(8,128)S(1)} %shard_map.76), channel_id=1, source_target_pairs={{0,1},{1,2},{2,3},{3,4},{4,5},{5,6},{6,7},{7,0},{8,9},{9,10},{10,1... | collective-permute-start | bytes 786440 | tf_op jit(solution)/shard_map/ppermute | solution.py:82
  70.2 7.9 %collective-permute-start.8 = (f32[256,256]{1,0:T(8,128)S(1)}, f32[256,256]{1,0:T(8,128)S(1)}, u32[]{:S(2)}, u32[]{:S(2)}) collective-permute-start(f32[256,256]{1,0:T(8,128)S(1)} %shard_map.72), channel_id=1, source_target_pairs={{0,1},{1,2},{2,3},{3,4},{4,5},{5,6},{6,7},{7,0},{8,9},{9,10},{10,1... | collective-permute-start | bytes 786440 | tf_op jit(solution)/shard_map/ppermute | solution.py:82
  78.2 12.7 %collective-permute-start.20 = (f32[256,512]{1,0:T(8,128)S(1)}, f32[256,512]{1,0:T(8,128)S(1)}, u32[]{:S(2)}, u32[]{:S(2)}) collective-permute-start(f32[256,512]{1,0:T(8,128)S(1)} %shard_map.81.refs_0_.refs_1_), channel_id=1, source_target_pairs={{16,0},{32,16},{48,32},{64,48},{80,64},{96,80},{112,96},{128,112},... | collective-permute-start | bytes 1572872 | tf_op jit(solution)/shard_map/ppermute | solution.py:34
  86.0 12.6 %collective-permute-start.21 = (f32[256,512]{1,0:T(8,128)S(1)}, f32[256,512]{1,0:T(8,128)S(1)}, u32[]{:S(2)}, u32[]{:S(2)}) collective-permute-start(f32[256,512]{1,0:T(8,128)S(1)} %shard_map.88), channel_id=1, source_target_pairs={{0,16},{16,32},{32,48},{48,64},{64,80},{80,96},{96,112},{112,128},... | collective-permute-start | bytes 1572872 | tf_op jit(solution)/shard_map/ppermute | solution.py:34

commit v4 on v3

--- a/solution.py
+++ b/solution.py
@@ -123,16 +123,17 @@
             compiler_params=pltpu.CompilerParams(vmem_limit_bytes=VMEM),
         )(pltpu.with_memory_space_constraint(rows, pltpu.HBM), pltpu.with_memory_space_constraint(cots, pltpu.HBM))
 
-    groups = ((4,), (-3,), (3, -2), (2, -1), (1, 0))
+    groups = ((4,), (-3,), (3,), (-2,), (2, -1), (1, 0))
     (message,) = gather([(False, 4), 0])
-    arrived = [sent(message, ACROSS)]
-    *messages, own_0, own_1, own_2, own_3, own_4 = gather(
-        [1, (False, -3)],
+    arrived = {0: sent(message, ACROSS)}
+    *messages, own_4, own_m3, own_3, own_m2, own_5, own_6 = gather(
+        [(False, -3)],
+        [1],
         *[[(False, offset) for offset in group] for group in groups[2:]],
         *[[(True, offset) for offset in group] for group in groups],
     )
     for index, message in enumerate(messages, 1):
-        arrived.append(sent(message, ACROSS))
+        arrived[index] = sent(message, ACROSS)
 
     def sums(mine, cots, theirs, their_cots):
         return contract_tokens(mine, cots) + contract_tokens(theirs, their_cots)
@@ -140,30 +141,32 @@
     def first(mine, cots, zero):
         return (sums(mine, cots[:, :BLOCK], zero[:, :BLOCK], zero[:, BLOCK:]),)
 
-    def second(mine_0, mine_1, cots, zero, one):
-        near, far = zero[:, BLOCK:], one[:, :BLOCK]
-        return (
-            sums(mine_0, cots[:, BLOCK:], zero[:, :BLOCK], far),
-            sums(mine_1, cots[:, :BLOCK], one[:, BLOCK:], near),
-            sums(mine_1, cots[:, BLOCK:], one[:, BLOCK:], far),
-        )
-
-    def later(mine, cots, zero, one, theirs):
+    def other(mine, cots, zero, theirs):
+        return (sums(mine, cots[:, :BLOCK], theirs, zero[:, BLOCK:]),)
+
+    def second(mine_0, mine_1, cots, zero, one, far):
+        far_cots = cots[:, BLOCK:]
+        return sums(mine_0, far_cots, zero[:, :BLOCK], far), sums(mine_1, far_cots, one, far)
+
+    def later(mine, cots, zero, far, theirs):
         return tuple(
             sums(mine[:, at : at + BLOCK], cots[:, part * BLOCK : (part + 1) * BLOCK], theirs[:, at : at + BLOCK], their_cots)
-            for at in (0, BLOCK)
-            for part, their_cots in enumerate((zero[:, BLOCK:], one[:, :BLOCK]))
+            for at in range(0, mine.shape[1], BLOCK)
+            for part, their_cots in enumerate((zero[:, BLOCK:], far))
         )
 
     partial = {}
     tile, work = (BLOCK, BLOCK), 4 * BLOCK**3
-    partial[4, 0] = local(first, work, [tile], own_0, cots, arrived[0])[0]
-    partial[4, 1], partial[-3, 0], partial[-3, 1] = local(
-        second, 3 * work, [tile] * 3, own_0, own_1, cots, arrived[0], arrived[1]
-    )
-    for index, mine in ((2, own_2), (3, own_3), (4, own_4)):
-        values = local(later, 4 * work, [tile] * 4, mine, cots, arrived[0], arrived[1], arrived[index])
-        for at, offset in enumerate(groups[index]):
+    partial[4, 0] = local(first, work, [tile], own_4, cots, arrived[0])[0]
+    partial[-3, 0] = local(other, work, [tile], own_m3, cots, arrived[0], arrived[1])[0]
+    partial[4, 1], partial[-3, 1] = local(
+        second, 2 * work, [tile] * 2, own_4, own_m3, cots, arrived[0], arrived[1], arrived[2]
+    )
+    for index, mine in ((3, own_3), (4, own_m2), (5, own_5), (6, own_6)):
+        group = groups[index - 1]
+        count = 2 * len(group)
+        values = local(later, count * work, [tile] * count, mine, cots, arrived[0], arrived[2], arrived[index])
+        for at, offset in enumerate(group):
             partial[offset, 0], partial[offset, 1] = values[2 * at : 2 * at + 2]
 
     def hop(value, pairs, offset, part):

time: 99.7 us -> 107 us (1.073)
  starting transfers between devices: 36.2 us -> 48.5 us
  waiting for transfers between devices: 46.9 us -> 41.5 us
    ppermute x19 -> x21, starting transfers between devices: 26.4 us -> 37.4 us  [sent(): return lax.ppermute(value, AXES, pairs)]
    ppermute x19 -> x21, waiting for transfers between devices: 38.7 us -> 33.3 us  [sent(): return lax.ppermute(value, AXES, pairs)]
    ppermute x3, starting transfers between devices: 9.82 us -> 11.1 us  [passed_along(): lax.ppermute(value, 'pipe', [(source, source + steps) for source in range...]
    pallas_call x23 -> x25, Pallas kernels: 12 us -> 12.4 us  [local(): pl.pallas_call(kernel, out_shape=[jax.ShapeDtypeStruct(shape, jnp.float32...]
  transfers between devices with their start and end apart: 22 -> 24, of which waited for: 14 -> 13; matrix products, arithmetic and copies ran while one was open for 0% -> 0% of each run, Pallas kernels for 13% -> 13%
where the time goes in v4:
time: 107 us; the launch traced here: 106 us
  starting transfers between devices  48.5 us (45%)
  waiting for transfers between devices  41.5 us (39%)
  Pallas kernels  15.1 us (14%)
    ppermute x21, starting transfers between devices, sent(): return lax.ppermute(value, AXES, pairs)  37.4 us
    ppermute x21, waiting for transfers between devices, sent(): return lax.ppermute(value, AXES, pairs)  33.3 us
    pallas_call x25, Pallas kernels, local(): pl.pallas_call(kernel, out_shape=[jax.ShapeDtypeStruct(shape, jnp.float32...  12.4 us
    ppermute x3, starting transfers between devices, passed_along(): lax.ppermute(value, 'pipe', [(source, source + steps) for source in range...  11.1 us
    ppermute x3, waiting for transfers between devices, passed_along(): lax.ppermute(value, 'pipe', [(source, source + steps) for source in range...  8.24 us
    pallas_call x2, Pallas kernels, gather(): pl.pallas_call(kernel, out_shape=[jax.ShapeDtypeStruct((TOKENS, width), j...  2.75 us
  transfers between devices with their start and end apart: 24, of which 13 were waited for; matrix products, arithmetic and copies ran while one was open for 0% of the time, Pallas kernels for 13%

profile of v4, /device:TPU:2, one launch (start us, length us, event | category | flops | bytes accessed | tf_op | source)
XLA Modules:
  0.0 106.5 jit_solution(5084429665115416547)
XLA Ops:
  1.0 2.2 %collective-permute-start = (bf16[256,512]{1,0:T(8,128)(2,1)S(1)}, bf16[256,512]{1,0:T(8,128)(2,1)S(1)}, u32[]{:S(2)}, u32[]{:S(2)}) collective-permute-start(bf16[256,512]{1,0:T(8,128)(2,1)S(1)} %shard_map.65), channel_id=1, source_target_pairs={{0,8},{1,9},{2,10},{3,11},{4,12},{5,13},{6,14},{7,15},{8,0},{9,1},... | collective-permute-start | bytes 786440 | tf_op jit(solution)/shard_map/ppermute | solution.py:82
  3.2 1.8 %shard_map.64 = (bf16[256,256]{1,0:T(8,128)(2,1)S(1)}, bf16[256,256]{1,0:T(8,128)(2,1)S(1)}, bf16[256,256]{1,0:T(8,128)(2,1)S(1)}, bf16[256,256]{1,0:T(8,128)(2,...) custom-call(bf16[256,4096]{1,0:T(8,128)(2,1)} %bitcast.23, ...), custom_call_target="tpu_custom_call" | custom-call | flops 100000000 | bytes 4194304 | tf_op jit(solution)/shard_map/pallas_call | solution.py:116
  5.0 1.5 %collective-permute-start.2 = (bf16[256,256]{1,0:T(8,128)(2,1)S(1)}, bf16[256,256]{1,0:T(8,128)(2,1)S(1)}, u32[]{:S(2)}, u32[]{:S(2)}) collective-permute-start(bf16[256,256]{1,0:T(8,128)(2,1)S(1)} %get-tuple-element.42), channel_id=1, source_target_pairs={{0,8},{1,9},{2,10},{3,11},{4,12},{5,13},{6,14},{7,15},{8,0},{9,1},... | collective-permute-start | bytes 393224 | tf_op jit(solution)/shard_map/ppermute | solution.py:82
  6.5 2.1 %collective-permute-start.9 = (bf16[256,256]{1,0:T(8,128)(2,1)S(1)}, bf16[256,256]{1,0:T(8,128)(2,1)S(1)}, u32[]{:S(2)}, u32[]{:S(2)}) collective-permute-start(bf16[256,256]{1,0:T(8,128)(2,1)S(1)} %get-tuple-element.52), channel_id=1, source_target_pairs={{0,8},{1,9},{2,10},{3,11},{4,12},{5,13},{6,14},{7,15},{8,0},{9,1},... | collective-permute-start | bytes 393224 | tf_op jit(solution)/shard_map/ppermute | solution.py:82
  8.6 6.0 %collective-permute-done.2.refs_3_.refs_5_ = bf16[256,256]{1,0:T(8,128)(2,1)S(1)} collective-permute-done((bf16[256,256]{1,0:T(8,128)(2,1)S(1)}, bf16[256,256]{1,0:T(8,128)(2,1)S(1)}, u32[]{:S(2)}, u32[]{:S(2)}) %collective-permute-start.2) | collective-permute-done | bytes 131104 | tf_op jit(solution)/shard_map/ppermute | solution.py:82
  14.6 1.7 %collective-permute-done.9.refs_4_.refs_3_ = bf16[256,256]{1,0:T(8,128)(2,1)S(1)} collective-permute-done((bf16[256,256]{1,0:T(8,128)(2,1)S(1)}, bf16[256,256]{1,0:T(8,128)(2,1)S(1)}, u32[]{:S(2)}, u32[]{:S(2)}) %collective-permute-start.9) | collective-permute-done | bytes 131104 | tf_op jit(solution)/shard_map/ppermute | solution.py:82
  16.6 2.0 %collective-permute-start.10 = (f32[256,256]{1,0:T(8,128)S(1)}, f32[256,256]{1,0:T(8,128)S(1)}, u32[]{:S(2)}, u32[]{:S(2)}) collective-permute-start(f32[256,256]{1,0:T(8,128)S(1)} %get-tuple-element.53), channel_id=1, source_target_pairs={{0,1},{1,2},{2,3},{3,4},{4,5},{5,6},{6,7},{7,0},{8,9},{9,10},{10,1... | collective-permute-start | bytes 786440 | tf_op jit(solution)/shard_map/ppermute | solution.py:82
  18.6 2.1 %collective-permute-start.5 = (bf16[256,512]{1,0:T(8,128)(2,1)S(1)}, bf16[256,512]{1,0:T(8,128)(2,1)S(1)}, u32[]{:S(2)}, u32[]{:S(2)}) collective-permute-start(bf16[256,512]{1,0:T(8,128)(2,1)S(1)} %get-tuple-element.46), channel_id=1, source_target_pairs={{0,8},{1,9},{2,10},{3,11},{4,12},{5,13},{6,14},{7,15},{8,0},{9,1},... | collective-permute-start | bytes 786440 | tf_op jit(solution)/shard_map/ppermute | solution.py:82
  20.8 1.4 %collective-permute-start.3 = (bf16[256,256]{1,0:T(8,128)(2,1)S(1)}, bf16[256,256]{1,0:T(8,128)(2,1)S(1)}, u32[]{:S(2)}, u32[]{:S(2)}) collective-permute-start(bf16[256,256]{1,0:T(8,128)(2,1)S(1)} %get-tuple-element.43), channel_id=1, source_target_pairs={{0,8},{1,9},{2,10},{3,11},{4,12},{5,13},{6,14},{7,15},{8,0},{9,1},... | collective-permute-start | bytes 393224 | tf_op jit(solution)/shard_map/ppermute | solution.py:82
  22.2 2.1 %collective-permute-start.15 = (bf16[256,256]{1,0:T(8,128)(2,1)S(1)}, bf16[256,256]{1,0:T(8,128)(2,1)S(1)}, u32[]{:S(2)}, u32[]{:S(2)}) collective-permute-start(bf16[256,256]{1,0:T(8,128)(2,1)S(1)} %get-tuple-element.58), channel_id=1, source_target_pairs={{0,8},{1,9},{2,10},{3,11},{4,12},{5,13},{6,14},{7,15},{8,0},{9,1},... | collective-permute-start | bytes 393224 | tf_op jit(solution)/shard_map/ppermute | solution.py:82
  24.3 6.2 %collective-permute-done.3.refs_4_ = bf16[256,256]{1,0:T(8,128)(2,1)S(1)} collective-permute-done((bf16[256,256]{1,0:T(8,128)(2,1)S(1)}, bf16[256,256]{1,0:T(8,128)(2,1)S(1)}, u32[]{:S(2)}, u32[]{:S(2)}) %collective-permute-start.3) | collective-permute-done | bytes 131104 | tf_op jit(solution)/shard_map/ppermute | solution.py:82
  33.7 2.0 %collective-permute-start.1 = (f32[256,256]{1,0:T(8,128)S(1)}, f32[256,256]{1,0:T(8,128)S(1)}, u32[]{:S(2)}, u32[]{:S(2)}) collective-permute-start(f32[256,256]{1,0:T(8,128)S(1)} %shard_map.66), channel_id=1, source_target_pairs={{0,1},{1,2},{2,3},{3,4},{4,5},{5,6},{6,7},{7,0},{8,9},{9,10},{10,1... | collective-permute-start | bytes 786440 | tf_op jit(solution)/shard_map/ppermute | solution.py:82
  36.2 2.2 %shard_map.85.refs_1_.refs_2_.refs_0_ = f32[512,512]{1,0:T(8,128)S(1)} custom-call(f32[512,512]{1,0:T(8,128)S(1)} %bitcast.17), custom_call_target="tpu_custom_call" | custom-call | flops 2000000000 | bytes 1048576 | tf_op jit(solution)/shard_map/pallas_call | solution.py:65
  38.4 2.6 %collective-permute-done.11.refs_0_ = f32[256,256]{1,0:T(8,128)S(1)} collective-permute-done((f32[256,256]{1,0:T(8,128)S(1)}, f32[256,256]{1,0:T(8,128)S(1)}, u32[]{:S(2)}, u32[]{:S(2)}) %collective-permute-start.11) | collective-permute-done | bytes 262176 | tf_op jit(solution)/shard_map/ppermute | solution.py:82
  41.0 1.8 %shard_map.86 = (f32[512,512]{1,0:T(8,128)S(1)}, f32[640,512]{1,0:T(8,128)S(1)}) custom-call(f32[512,512]{1,0:T(8,128)S(1)} %bitcast.18, f32[512,512]{1,0:T(8,128)S(1)} %shard_map.85.refs_1_.refs_2_.refs_0_, f32[128,512]{1,0:T(8,128)S(1)} %get-tuple-element.69.refs_2_), custom_call_target="tpu_custom_call" | custom-call | flops 2000000000 | bytes 1048576 | tf_op jit(solution)/shard_map/pallas_call | solution.py:65
  42.8 1.9 %collective-permute-start.21 = (f32[640,512]{1,0:T(8,128)S(1)}, f32[640,512]{1,0:T(8,128)S(1)}, u32[]{:S(2)}, u32[]{:S(2)}) collective-permute-start(f32[640,512]{1,0:T(8,128)S(1)} %get-tuple-element.70), channel_id=1, source_target_pairs={{0,16},{16,32},{32,48},{48,64},{64,80},{80,96},{96,112},{112,128},... | collective-permute-start | bytes 3932168 | tf_op jit(solution)/shard_map/ppermute | solution.py:34
  44.8 2.1 %collective-permute-start.18 = (f32[256,256]{1,0:T(8,128)S(1)}, f32[256,256]{1,0:T(8,128)S(1)}, u32[]{:S(2)}, u32[]{:S(2)}) collective-permute-start(f32[256,256]{1,0:T(8,128)S(1)} %get-tuple-element.61), channel_id=1, source_target_pairs={{0,7},{1,0},{2,1},{3,2},{4,3},{5,4},{6,5},{7,6},{8,15},{9,8},{10,9... | collective-permute-start | bytes 786440 | tf_op jit(solution)/shard_map/ppermute | solution.py:82
  49.5 2.1 %collective-permute-start.7 = (bf16[256,512]{1,0:T(8,128)(2,1)S(1)}, bf16[256,512]{1,0:T(8,128)(2,1)S(1)}, u32[]{:S(2)}, u32[]{:S(2)}) collective-permute-start(bf16[256,512]{1,0:T(8,128)(2,1)S(1)} %get-tuple-element.49), channel_id=1, source_target_pairs={{0,8},{1,9},{2,10},{3,11},{4,12},{5,13},{6,14},{7,15},{8,0},{9,1},... | collective-permute-start | bytes 786440 | tf_op jit(solution)/shard_map/ppermute | solution.py:82
  52.0 3.0 %collective-permute-start.19 = (f32[256,256]{1,0:T(8,128)S(1)}, f32[256,256]{1,0:T(8,128)S(1)}, u32[]{:S(2)}, u32[]{:S(2)}) collective-permute-start(f32[256,256]{1,0:T(8,128)S(1)} %shard_map.81), channel_id=1, source_target_pairs={{0,7},{1,0},{2,1},{3,2},{4,3},{5,4},{6,5},{7,6},{8,15},{9,8},{10,9... | collective-permute-start | bytes 786440 | tf_op jit(solution)/shard_map/ppermute | solution.py:82
  55.0 1.3 %collective-permute-done.14.refs_0_ = f32[256,256]{1,0:T(8,128)S(1)} collective-permute-done((f32[256,256]{1,0:T(8,128)S(1)}, f32[256,256]{1,0:T(8,128)S(1)}, u32[]{:S(2)}, u32[]{:S(2)}) %collective-permute-start.14) | collective-permute-done | bytes 262176 | tf_op jit(solution)/shard_map/ppermute | solution.py:82
  56.4 3.8 %collective-permute-start.16 = (f32[256,256]{1,0:T(8,128)S(1)}, f32[256,256]{1,0:T(8,128)S(1)}, u32[]{:S(2)}, u32[]{:S(2)}) collective-permute-start(f32[256,256]{1,0:T(8,128)S(1)} %shard_map.79), channel_id=1, source_target_pairs={{0,7},{1,0},{2,1},{3,2},{4,3},{5,4},{6,5},{7,6},{8,15},{9,8},{10,9... | collective-permute-start | bytes 786440 | tf_op jit(solution)/shard_map/ppermute | solution.py:82
  60.8 3.3 %collective-permute-start.20 = (f32[256,256]{1,0:T(8,128)S(1)}, f32[256,256]{1,0:T(8,128)S(1)}, u32[]{:S(2)}, u32[]{:S(2)}) collective-permute-start(f32[256,256]{1,0:T(8,128)S(1)} %shard_map.82), channel_id=1, source_target_pairs={{0,7},{1,0},{2,1},{3,2},{4,3},{5,4},{6,5},{7,6},{8,15},{9,8},{10,9... | collective-permute-start | bytes 786440 | tf_op jit(solution)/shard_map/ppermute | solution.py:82
  64.1 2.1 %collective-permute-done.16.refs_0_ = f32[256,256]{1,0:T(8,128)S(1)} collective-permute-done((f32[256,256]{1,0:T(8,128)S(1)}, f32[256,256]{1,0:T(8,128)S(1)}, u32[]{:S(2)}, u32[]{:S(2)}) %collective-permute-start.16) | collective-permute-done | bytes 262176 | tf_op jit(solution)/shard_map/ppermute | solution.py:82
  66.3 3.8 %collective-permute-start.17 = (f32[256,256]{1,0:T(8,128)S(1)}, f32[256,256]{1,0:T(8,128)S(1)}, u32[]{:S(2)}, u32[]{:S(2)}) collective-permute-start(f32[256,256]{1,0:T(8,128)S(1)} %shard_map.80), channel_id=1, source_target_pairs={{0,7},{1,0},{2,1},{3,2},{4,3},{5,4},{6,5},{7,6},{8,15},{9,8},{10,9... | collective-permute-start | bytes 786440 | tf_op jit(solution)/shard_map/ppermute | solution.py:82
  70.5 5.5 %collective-permute-done.6.refs_0_ = f32[256,256]{1,0:T(8,128)S(1)} collective-permute-done((f32[256,256]{1,0:T(8,128)S(1)}, f32[256,256]{1,0:T(8,128)S(1)}, u32[]{:S(2)}, u32[]{:S(2)}) %collective-permute-start.6) | collective-permute-done | bytes 262176 | tf_op jit(solution)/shard_map/ppermute | solution.py:82
  76.2 1.3 %collective-permute-done.17.refs_2_ = f32[256,256]{1,0:T(8,128)S(1)} collective-permute-done((f32[256,256]{1,0:T(8,128)S(1)}, f32[256,256]{1,0:T(8,128)S(1)}, u32[]{:S(2)}, u32[]{:S(2)}) %collective-permute-start.17) | collective-permute-done | bytes 262176 | tf_op jit(solution)/shard_map/ppermute | solution.py:82
  77.5 1.9 %collective-permute-done.13.refs_1_ = f32[256,256]{1,0:T(8,128)S(1)} collective-permute-done((f32[256,256]{1,0:T(8,128)S(1)}, f32[256,256]{1,0:T(8,128)S(1)}, u32[]{:S(2)}, u32[]{:S(2)}) %collective-permute-start.13) | collective-permute-done | bytes 262176 | tf_op jit(solution)/shard_map/ppermute | solution.py:82
  79.4 4.3 %collective-permute-done.8.refs_0_ = f32[256,256]{1,0:T(8,128)S(1)} collective-permute-done((f32[256,256]{1,0:T(8,128)S(1)}, f32[256,256]{1,0:T(8,128)S(1)}, u32[]{:S(2)}, u32[]{:S(2)}) %collective-permute-start.8) | collective-permute-done | bytes 262176 | tf_op jit(solution)/shard_map/ppermute | solution.py:82
  83.8 7.3 %collective-permute-start.22 = (f32[256,512]{1,0:T(8,128)S(1)}, f32[256,512]{1,0:T(8,128)S(1)}, u32[]{:S(2)}, u32[]{:S(2)}) collective-permute-start(f32[256,512]{1,0:T(8,128)S(1)} %shard_map.83.refs_0_.refs_1_), channel_id=1, source_target_pairs={{16,0},{32,16},{48,32},{64,48},{80,64},{96,80},{112,96},{128,112},... | collective-permute-start | bytes 1572872 | tf_op jit(solution)/shard_map/ppermute | solution.py:34
  93.0 1.9 %collective-permute-start.23 = (f32[256,512]{1,0:T(8,128)S(1)}, f32[256,512]{1,0:T(8,128)S(1)}, u32[]{:S(2)}, u32[]{:S(2)}) collective-permute-start(f32[256,512]{1,0:T(8,128)S(1)} %shard_map.90), channel_id=1, source_target_pairs={{0,16},{16,32},{32,48},{48,64},{64,80},{80,96},{96,112},{112,128},... | collective-permute-start | bytes 1572872 | tf_op jit(solution)/shard_map/ppermute | solution.py:34
  94.9 1.5 %shard_map.87.refs_0_ = f32[256,512]{1,0:T(8,128)S(1)} custom-call(f32[256,512]{1,0:T(8,128)S(1)} %shard_map.83.refs_0_.refs_1_, f32[256,256]{1,0:T(8,128)S(1)} %get-tuple-element.66.refs_1_, f32[512,512]{1,0:T(8,128)S(1)} %shard_map.85.refs_1_.refs_2_.refs_0_, f32[640,512]{1,0:T(8,128)S(1)} %collective-permute-done.21.refs_3_), custom_call_target="tpu_custom_call" | custom-call | flops 2000000000 | bytes 1048576 | tf_op jit(solution)/shard_map/pallas_call | solution.py:65
  98.7 6.9 %collective-permute-done.23 = f32[256,512]{1,0:T(8,128)S(1)} collective-permute-done((f32[256,512]{1,0:T(8,128)S(1)}, f32[256,512]{1,0:T(8,128)S(1)}, u32[]{:S(2)}, u32[]{:S(2)}) %collective-permute-start.23) | collective-permute-done | bytes 524320 | tf_op jit(solution)/shard_map/ppermute | solution.py:34
  (54 shorter events, 14.3 us)
Async XLA Ops:
  1.0 15.3 %copy-start = (bf16[1,256,512]{2,1,0:T(8,128)(2,1)S(1)}, bf16[1,256,512]{2,1,0:T(8,128)(2,1)}, u32[]{:S(2)}) copy-start(bf16[1,256,512]{2,1,0:T(8,128)(2,1)} %param.7) | copy-start | bytes 786436
  1.0 15.3 %collective-permute-start = (bf16[256,512]{1,0:T(8,128)(2,1)S(1)}, bf16[256,512]{1,0:T(8,128)(2,1)S(1)}, u32[]{:S(2)}, u32[]{:S(2)}) collective-permute-start(bf16[256,512]{1,0:T(8,128)(2,1)S(1)} %shard_map.65), channel_id=1, source_target_pairs={{0,8},{1,9},{2,10},{3,11},{4,12},{5,13},{6,14},{7,15},{8,0},{9,1},... | collective-permute-start | bytes 786440 | tf_op jit(solution)/shard_map/ppermute | solution.py:82
  5.0 9.6 %collective-permute-start.2 = (bf16[256,256]{1,0:T(8,128)(2,1)S(1)}, bf16[256,256]{1,0:T(8,128)(2,1)S(1)}, u32[]{:S(2)}, u32[]{:S(2)}) collective-permute-start(bf16[256,256]{1,0:T(8,128)(2,1)S(1)} %get-tuple-element.42), channel_id=1, source_target_pairs={{0,8},{1,9},{2,10},{3,11},{4,12},{5,13},{6,14},{7,15},{8,0},{9,1},... | collective-permute-start | bytes 393224 | tf_op jit(solution)/shard_map/ppermute | solution.py:82
  6.5 9.8 %collective-permute-start.9 = (bf16[256,256]{1,0:T(8,128)(2,1)S(1)}, bf16[256,256]{1,0:T(8,128)(2,1)S(1)}, u32[]{:S(2)}, u32[]{:S(2)}) collective-permute-start(bf16[256,256]{1,0:T(8,128)(2,1)S(1)} %get-tuple-element.52), channel_id=1, source_target_pairs={{0,8},{1,9},{2,10},{3,11},{4,12},{5,13},{6,14},{7,15},{8,0},{9,1},... | collective-permute-start | bytes 393224 | tf_op jit(solution)/shard_map/ppermute | solution.py:82
  16.3 15.8 %copy-start.3 = (f32[1,256,256]{2,1,0:T(8,128)S(1)}, f32[1,256,256]{2,1,0:T(8,128)}, u32[]{:S(2)}) copy-start(f32[1,256,256]{2,1,0:T(8,128)} %param.8) | copy-start | bytes 786436
  16.3 15.8 %copy-start.4 = (f32[1,256,256]{2,1,0:T(8,128)S(1)}, f32[1,256,256]{2,1,0:T(8,128)}, u32[]{:S(2)}) copy-start(f32[1,256,256]{2,1,0:T(8,128)} %param.10) | copy-start | bytes 786436
  16.6 14.1 %collective-permute-start.10 = (f32[256,256]{1,0:T(8,128)S(1)}, f32[256,256]{1,0:T(8,128)S(1)}, u32[]{:S(2)}, u32[]{:S(2)}) collective-permute-start(f32[256,256]{1,0:T(8,128)S(1)} %get-tuple-element.53), channel_id=1, source_target_pairs={{0,1},{1,2},{2,3},{3,4},{4,5},{5,6},{6,7},{7,0},{8,9},{9,10},{10,1... | collective-permute-start | bytes 786440 | tf_op jit(solution)/shard_map/ppermute | solution.py:82
  18.6 17.1 %collective-permute-start.5 = (bf16[256,512]{1,0:T(8,128)(2,1)S(1)}, bf16[256,512]{1,0:T(8,128)(2,1)S(1)}, u32[]{:S(2)}, u32[]{:S(2)}) collective-permute-start(bf16[256,512]{1,0:T(8,128)(2,1)S(1)} %get-tuple-element.46), channel_id=1, source_target_pairs={{0,8},{1,9},{2,10},{3,11},{4,12},{5,13},{6,14},{7,15},{8,0},{9,1},... | collective-permute-start | bytes 786440 | tf_op jit(solution)/shard_map/ppermute | solution.py:82
  20.8 9.7 %collective-permute-start.3 = (bf16[256,256]{1,0:T(8,128)(2,1)S(1)}, bf16[256,256]{1,0:T(8,128)(2,1)S(1)}, u32[]{:S(2)}, u32[]{:S(2)}) collective-permute-start(bf16[256,256]{1,0:T(8,128)(2,1)S(1)} %get-tuple-element.43), channel_id=1, source_target_pairs={{0,8},{1,9},{2,10},{3,11},{4,12},{5,13},{6,14},{7,15},{8,0},{9,1},... | collective-permute-start | bytes 393224 | tf_op jit(solution)/shard_map/ppermute | solution.py:82
  22.2 27.4 %collective-permute-start.15 = (bf16[256,256]{1,0:T(8,128)(2,1)S(1)}, bf16[256,256]{1,0:T(8,128)(2,1)S(1)}, u32[]{:S(2)}, u32[]{:S(2)}) collective-permute-start(bf16[256,256]{1,0:T(8,128)(2,1)S(1)} %get-tuple-element.58), channel_id=1, source_target_pairs={{0,8},{1,9},{2,10},{3,11},{4,12},{5,13},{6,14},{7,15},{8,0},{9,1},... | collective-permute-start | bytes 393224 | tf_op jit(solution)/shard_map/ppermute | solution.py:82
  30.8 10.1 %collective-permute-start.11 = (f32[256,256]{1,0:T(8,128)S(1)}, f32[256,256]{1,0:T(8,128)S(1)}, u32[]{:S(2)}, u32[]{:S(2)}) collective-permute-start(f32[256,256]{1,0:T(8,128)S(1)} %shard_map.74), channel_id=1, source_target_pairs={{0,1},{1,2},{2,3},{3,4},{4,5},{5,6},{6,7},{7,0},{8,9},{9,10},{10,1... | collective-permute-start | bytes 786440 | tf_op jit(solution)/shard_map/ppermute | solution.py:82
  33.4 2.8 %copy-start.1 = (f32[1,512,512]{2,1,0:T(8,128)S(1)}, f32[1,512,512]{2,1,0:T(8,128)}, u32[]{:S(2)}) copy-start(f32[1,512,512]{2,1,0:T(8,128)} %param.9) | copy-start | bytes 3145732
  33.7 14.7 %collective-permute-start.1 = (f32[256,256]{1,0:T(8,128)S(1)}, f32[256,256]{1,0:T(8,128)S(1)}, u32[]{:S(2)}, u32[]{:S(2)}) collective-permute-start(f32[256,256]{1,0:T(8,128)S(1)} %shard_map.66), channel_id=1, source_target_pairs={{0,1},{1,2},{2,3},{3,4},{4,5},{5,6},{6,7},{7,0},{8,9},{9,10},{10,1... | collective-permute-start | bytes 786440 | tf_op jit(solution)/shard_map/ppermute | solution.py:82
  36.2 4.8 %copy-start.2 = (f32[1,512,512]{2,1,0:T(8,128)S(1)}, f32[1,512,512]{2,1,0:T(8,128)}, u32[]{:S(2)}) copy-start(f32[1,512,512]{2,1,0:T(8,128)} %param.11) | copy-start | bytes 3145732
  42.8 52.1 %collective-permute-start.21 = (f32[640,512]{1,0:T(8,128)S(1)}, f32[640,512]{1,0:T(8,128)S(1)}, u32[]{:S(2)}, u32[]{:S(2)}) collective-permute-start(f32[640,512]{1,0:T(8,128)S(1)} %get-tuple-element.70), channel_id=1, source_target_pairs={{0,16},{16,32},{32,48},{48,64},{64,80},{80,96},{96,112},{112,128},... | collective-permute-start | bytes 3932168 | tf_op jit(solution)/shard_map/ppermute | solution.py:34
  44.8 7.2 %collective-permute-start.18 = (f32[256,256]{1,0:T(8,128)S(1)}, f32[256,256]{1,0:T(8,128)S(1)}, u32[]{:S(2)}, u32[]{:S(2)}) collective-permute-start(f32[256,256]{1,0:T(8,128)S(1)} %get-tuple-element.61), channel_id=1, source_target_pairs={{0,7},{1,0},{2,1},{3,2},{4,3},{5,4},{6,5},{7,6},{8,15},{9,8},{10,9... | collective-permute-start | bytes 786440 | tf_op jit(solution)/shard_map/ppermute | solution.py:82
  47.1 9.2 %collective-permute-start.14 = (f32[256,256]{1,0:T(8,128)S(1)}, f32[256,256]{1,0:T(8,128)S(1)}, u32[]{:S(2)}, u32[]{:S(2)}) collective-permute-start(f32[256,256]{1,0:T(8,128)S(1)} %shard_map.77), channel_id=1, source_target_pairs={{0,7},{1,0},{2,1},{3,2},{4,3},{5,4},{6,5},{7,6},{8,15},{9,8},{10,9... | collective-permute-start | bytes 786440 | tf_op jit(solution)/shard_map/ppermute | solution.py:82
  48.5 11.7 %collective-permute-start.4 = (f32[256,256]{1,0:T(8,128)S(1)}, f32[256,256]{1,0:T(8,128)S(1)}, u32[]{:S(2)}, u32[]{:S(2)}) collective-permute-start(f32[256,256]{1,0:T(8,128)S(1)} %shard_map.68), channel_id=1, source_target_pairs={{0,1},{1,2},{2,3},{3,4},{4,5},{5,6},{6,7},{7,0},{8,9},{9,10},{10,1... | collective-permute-start | bytes 786440 | tf_op jit(solution)/shard_map/ppermute | solution.py:82
  49.5 10.7 %collective-permute-start.7 = (bf16[256,512]{1,0:T(8,128)(2,1)S(1)}, bf16[256,512]{1,0:T(8,128)(2,1)S(1)}, u32[]{:S(2)}, u32[]{:S(2)}) collective-permute-start(bf16[256,512]{1,0:T(8,128)(2,1)S(1)} %get-tuple-element.49), channel_id=1, source_target_pairs={{0,8},{1,9},{2,10},{3,11},{4,12},{5,13},{6,14},{7,15},{8,0},{9,1},... | collective-permute-start | bytes 786440 | tf_op jit(solution)/shard_map/ppermute | solution.py:82
  52.0 8.7 %collective-permute-start.19 = (f32[256,256]{1,0:T(8,128)S(1)}, f32[256,256]{1,0:T(8,128)S(1)}, u32[]{:S(2)}, u32[]{:S(2)}) collective-permute-start(f32[256,256]{1,0:T(8,128)S(1)} %shard_map.81), channel_id=1, source_target_pairs={{0,7},{1,0},{2,1},{3,2},{4,3},{5,4},{6,5},{7,6},{8,15},{9,8},{10,9... | collective-permute-start | bytes 786440 | tf_op jit(solution)/shard_map/ppermute | solution.py:82
  56.4 9.9 %collective-permute-start.16 = (f32[256,256]{1,0:T(8,128)S(1)}, f32[256,256]{1,0:T(8,128)S(1)}, u32[]{:S(2)}, u32[]{:S(2)}) collective-permute-start(f32[256,256]{1,0:T(8,128)S(1)} %shard_map.79), channel_id=1, source_target_pairs={{0,7},{1,0},{2,1},{3,2},{4,3},{5,4},{6,5},{7,6},{8,15},{9,8},{10,9... | collective-permute-start | bytes 786440 | tf_op jit(solution)/shard_map/ppermute | solution.py:82
  60.2 10.2 %collective-permute-start.12 = (f32[256,256]{1,0:T(8,128)S(1)}, f32[256,256]{1,0:T(8,128)S(1)}, u32[]{:S(2)}, u32[]{:S(2)}) collective-permute-start(f32[256,256]{1,0:T(8,128)S(1)} %shard_map.75), channel_id=1, source_target_pairs={{0,1},{1,2},{2,3},{3,4},{4,5},{5,6},{6,7},{7,0},{8,9},{9,10},{10,1... | collective-permute-start | bytes 786440 | tf_op jit(solution)/shard_map/ppermute | solution.py:82
  60.2 15.8 %collective-permute-start.6 = (f32[256,256]{1,0:T(8,128)S(1)}, f32[256,256]{1,0:T(8,128)S(1)}, u32[]{:S(2)}, u32[]{:S(2)}) collective-permute-start(f32[256,256]{1,0:T(8,128)S(1)} %shard_map.70), channel_id=1, source_target_pairs={{0,1},{1,2},{2,3},{3,4},{4,5},{5,6},{6,7},{7,0},{8,9},{9,10},{10,1... | collective-permute-start | bytes 786440 | tf_op jit(solution)/shard_map/ppermute | solution.py:82
  60.8 15.3 %collective-permute-start.20 = (f32[256,256]{1,0:T(8,128)S(1)}, f32[256,256]{1,0:T(8,128)S(1)}, u32[]{:S(2)}, u32[]{:S(2)}) collective-permute-start(f32[256,256]{1,0:T(8,128)S(1)} %shard_map.82), channel_id=1, source_target_pairs={{0,7},{1,0},{2,1},{3,2},{4,3},{5,4},{6,5},{7,6},{8,15},{9,8},{10,9... | collective-permute-start | bytes 786440 | tf_op jit(solution)/shard_map/ppermute | solution.py:82
  66.3 11.2 %collective-permute-start.17 = (f32[256,256]{1,0:T(8,128)S(1)}, f32[256,256]{1,0:T(8,128)S(1)}, u32[]{:S(2)}, u32[]{:S(2)}) collective-permute-start(f32[256,256]{1,0:T(8,128)S(1)} %shard_map.80), channel_id=1, source_target_pairs={{0,7},{1,0},{2,1},{3,2},{4,3},{5,4},{6,5},{7,6},{8,15},{9,8},{10,9... | collective-permute-start | bytes 786440 | tf_op jit(solution)/shard_map/ppermute | solution.py:82
  70.4 9.0 %collective-permute-start.13 = (f32[256,256]{1,0:T(8,128)S(1)}, f32[256,256]{1,0:T(8,128)S(1)}, u32[]{:S(2)}, u32[]{:S(2)}) collective-permute-start(f32[256,256]{1,0:T(8,128)S(1)} %shard_map.76), channel_id=1, source_target_pairs={{0,1},{1,2},{2,3},{3,4},{4,5},{5,6},{6,7},{7,0},{8,9},{9,10},{10,1... | collective-permute-start | bytes 786440 | tf_op jit(solution)/shard_map/ppermute | solution.py:82
  76.1 7.7 %collective-permute-start.8 = (f32[256,256]{1,0:T(8,128)S(1)}, f32[256,256]{1,0:T(8,128)S(1)}, u32[]{:S(2)}, u32[]{:S(2)}) collective-permute-start(f32[256,256]{1,0:T(8,128)S(1)} %shard_map.72), channel_id=1, source_target_pairs={{0,1},{1,2},{2,3},{3,4},{4,5},{5,6},{6,7},{7,0},{8,9},{9,10},{10,1... | collective-permute-start | bytes 786440 | tf_op jit(solution)/shard_map/ppermute | solution.py:82
  83.8 14.0 %collective-permute-start.22 = (f32[256,512]{1,0:T(8,128)S(1)}, f32[256,512]{1,0:T(8,128)S(1)}, u32[]{:S(2)}, u32[]{:S(2)}) collective-permute-start(f32[256,512]{1,0:T(8,128)S(1)} %shard_map.83.refs_0_.refs_1_), channel_id=1, source_target_pairs={{16,0},{32,16},{48,32},{64,48},{80,64},{96,80},{112,96},{128,112},... | collective-permute-start | bytes 1572872 | tf_op jit(solution)/shard_map/ppermute | solution.py:34
  93.0 12.6 %collective-permute-start.23 = (f32[256,512]{1,0:T(8,128)S(1)}, f32[256,512]{1,0:T(8,128)S(1)}, u32[]{:S(2)}, u32[]{:S(2)}) collective-permute-start(f32[256,512]{1,0:T(8,128)S(1)} %shard_map.90), channel_id=1, source_target_pairs={{0,16},{16,32},{32,48},{48,64},{64,80},{80,96},{96,112},{112,128},... | collective-permute-start | bytes 1572872 | tf_op jit(solution)/shard_map/ppermute | solution.py:34

commit v5 on v4

--- a/solution.py
+++ b/solution.py
@@ -184,8 +184,8 @@
                 short_way[part] = sent(short_way[part], SHORT)
             else:
                 short_way[part] = hop(short_way[part], SHORT, short_next, part)
-        marks.append(long_way[1])
-    long_1, long_2, long_3 = marks
+        marks.append(long_way[0])
+    long_1, _, long_3 = marks
     long_way = [sent(long_way[part], LONG) for part in range(2)]
 
     def whole_gradient(*values):
@@ -215,11 +215,11 @@
 
     left, left_next, left_back, packed = local(left_side, 10**9, [square, square, square, (BLOCK // 2, OUT)], factor_in, coupling)
     (right,) = local(lambda factor: (invert(factor),), 2 * 10**9, [full], after(factor_out, long_1))
-    right_next, weights = local(right_side, 2 * 10**9, [full, (OUT + BLOCK // 2, OUT)], coupling_out, after(right, long_2), packed)
+    right_next, weights = local(right_side, 2 * 10**9, [full, (OUT + BLOCK // 2, OUT)], coupling_out, right, packed)
     (right_back,) = local(lambda right, out: (mm(right, out),), 10**9, [full], after(right, long_3), coupling_out)
     weights = passed_along(weights, 1)
-    following = passed_along(gradient, -1)
     (passed,) = local(product, 10**9, [wide], left_back, gradient, right_back)
+    following = passed_along(after(gradient, passed), -1)
     back = passed_along(passed, 1)
     (mine,) = local(own_terms, 2 * 10**9, [wide], gradient, left, right, weights)
     (mine,) = local(

time: 107 us -> 97.2 us (0.908)
  waiting for transfers between devices: 41.5 us -> 32.3 us
    ppermute x21, waiting for transfers between devices: 33.3 us -> 24 us  [sent(): return lax.ppermute(value, AXES, pairs)]
    ppermute x21, starting transfers between devices: 37.4 us -> 35.6 us  [sent(): return lax.ppermute(value, AXES, pairs)]
    ppermute x3, starting transfers between devices: 11.1 us -> 12.7 us  [passed_along(): lax.ppermute(value, 'pipe', [(source, source + steps) for source in range...]
  transfers between devices with their start and end apart: 24 -> 24, of which waited for: 13 -> 11; matrix products, arithmetic and copies ran while one was open for 0% -> 0% of each run, Pallas kernels for 13% -> 14%
where the time goes in v5:
time: 97.2 us; the launch traced here: 97 us
  starting transfers between devices  48.3 us (50%)
  waiting for transfers between devices  32.3 us (33%)
  Pallas kernels  15.1 us (16%)
    ppermute x21, starting transfers between devices, sent(): return lax.ppermute(value, AXES, pairs)  35.6 us
    ppermute x21, waiting for transfers between devices, sent(): return lax.ppermute(value, AXES, pairs)  24 us
    ppermute x3, starting transfers between devices, passed_along(): lax.ppermute(value, 'pipe', [(source, source + steps) for source in range...  12.7 us
    pallas_call x25, Pallas kernels, local(): pl.pallas_call(kernel, out_shape=[jax.ShapeDtypeStruct(shape, jnp.float32...  12.4 us
    ppermute x3, waiting for transfers between devices, passed_along(): lax.ppermute(value, 'pipe', [(source, source + steps) for source in range...  8.24 us
    pallas_call x2, Pallas kernels, gather(): pl.pallas_call(kernel, out_shape=[jax.ShapeDtypeStruct((TOKENS, width), j...  2.75 us
  transfers between devices with their start and end apart: 24, of which 11 were waited for; matrix products, arithmetic and copies ran while one was open for 0% of the time, Pallas kernels for 14%

profile of v5, /device:TPU:2, one launch (start us, length us, event | category | flops | bytes accessed | tf_op | source)
XLA Modules:
  0.0 97.0 jit_solution(14410745225464261379)
XLA Ops:
  1.0 2.2 %collective-permute-start = (bf16[256,512]{1,0:T(8,128)(2,1)S(1)}, bf16[256,512]{1,0:T(8,128)(2,1)S(1)}, u32[]{:S(2)}, u32[]{:S(2)}) collective-permute-start(bf16[256,512]{1,0:T(8,128)(2,1)S(1)} %shard_map.65), channel_id=1, source_target_pairs={{0,8},{1,9},{2,10},{3,11},{4,12},{5,13},{6,14},{7,15},{8,0},{9,1},... | collective-permute-start | bytes 786440 | tf_op jit(solution)/shard_map/ppermute | solution.py:82
  3.2 1.8 %shard_map.64 = (bf16[256,256]{1,0:T(8,128)(2,1)S(1)}, bf16[256,256]{1,0:T(8,128)(2,1)S(1)}, bf16[256,256]{1,0:T(8,128)(2,1)S(1)}, bf16[256,256]{1,0:T(8,128)(2,...) custom-call(bf16[256,4096]{1,0:T(8,128)(2,1)} %bitcast.23, ...), custom_call_target="tpu_custom_call" | custom-call | flops 100000000 | bytes 4194304 | tf_op jit(solution)/shard_map/pallas_call | solution.py:116
  5.0 5.7 %collective-permute-done.refs_2_.refs_3_ = bf16[256,512]{1,0:T(8,128)(2,1)S(1)} collective-permute-done((bf16[256,512]{1,0:T(8,128)(2,1)S(1)}, bf16[256,512]{1,0:T(8,128)(2,1)S(1)}, u32[]{:S(2)}, u32[]{:S(2)}) %collective-permute-start) | collective-permute-done | bytes 262176 | tf_op jit(solution)/shard_map/ppermute | solution.py:82
  10.9 2.0 %collective-permute-start.1 = (f32[256,256]{1,0:T(8,128)S(1)}, f32[256,256]{1,0:T(8,128)S(1)}, u32[]{:S(2)}, u32[]{:S(2)}) collective-permute-start(f32[256,256]{1,0:T(8,128)S(1)} %shard_map.66), channel_id=1, source_target_pairs={{0,1},{1,2},{2,3},{3,4},{4,5},{5,6},{6,7},{7,0},{8,9},{9,10},{10,1... | collective-permute-start | bytes 786440 | tf_op jit(solution)/shard_map/ppermute | solution.py:82
  12.9 2.1 %collective-permute-start.2 = (bf16[256,256]{1,0:T(8,128)(2,1)S(1)}, bf16[256,256]{1,0:T(8,128)(2,1)S(1)}, u32[]{:S(2)}, u32[]{:S(2)}) collective-permute-start(bf16[256,256]{1,0:T(8,128)(2,1)S(1)} %get-tuple-element.42), channel_id=1, source_target_pairs={{0,8},{1,9},{2,10},{3,11},{4,12},{5,13},{6,14},{7,15},{8,0},{9,1},... | collective-permute-start | bytes 393224 | tf_op jit(solution)/shard_map/ppermute | solution.py:82
  15.1 1.4 %collective-permute-start.9 = (bf16[256,256]{1,0:T(8,128)(2,1)S(1)}, bf16[256,256]{1,0:T(8,128)(2,1)S(1)}, u32[]{:S(2)}, u32[]{:S(2)}) collective-permute-start(bf16[256,256]{1,0:T(8,128)(2,1)S(1)} %get-tuple-element.52), channel_id=1, source_target_pairs={{0,8},{1,9},{2,10},{3,11},{4,12},{5,13},{6,14},{7,15},{8,0},{9,1},... | collective-permute-start | bytes 393224 | tf_op jit(solution)/shard_map/ppermute | solution.py:82
  16.5 2.1 %collective-permute-start.3 = (bf16[256,256]{1,0:T(8,128)(2,1)S(1)}, bf16[256,256]{1,0:T(8,128)(2,1)S(1)}, u32[]{:S(2)}, u32[]{:S(2)}) collective-permute-start(bf16[256,256]{1,0:T(8,128)(2,1)S(1)} %get-tuple-element.43), channel_id=1, source_target_pairs={{0,8},{1,9},{2,10},{3,11},{4,12},{5,13},{6,14},{7,15},{8,0},{9,1},... | collective-permute-start | bytes 393224 | tf_op jit(solution)/shard_map/ppermute | solution.py:82
  18.6 1.4 %collective-permute-start.5 = (bf16[256,512]{1,0:T(8,128)(2,1)S(1)}, bf16[256,512]{1,0:T(8,128)(2,1)S(1)}, u32[]{:S(2)}, u32[]{:S(2)}) collective-permute-start(bf16[256,512]{1,0:T(8,128)(2,1)S(1)} %get-tuple-element.46), channel_id=1, source_target_pairs={{0,8},{1,9},{2,10},{3,11},{4,12},{5,13},{6,14},{7,15},{8,0},{9,1},... | collective-permute-start | bytes 786440 | tf_op jit(solution)/shard_map/ppermute | solution.py:82
  20.0 1.3 %shard_map.84 = (f32[256,256]{1,0:T(8,128)S(1)}, f32[256,256]{1,0:T(8,128)S(1)}, f32[256,256]{1,0:T(8,128)S(1)}, f32[128,512]{1,0:T(8,128)S(1)}) custom-call(f32[256,256]{1,0:T(8,128)S(1)} %bitcast.20, f32[256,256]{1,0:T(8,128)S(1)} %bitcast.21), custom_call_target="tpu_custom_call" | custom-call | flops 1000000000 | bytes 1048576 | tf_op jit(solution)/shard_map/pallas_call | solution.py:65
  21.3 2.2 %collective-permute-start.15 = (bf16[256,256]{1,0:T(8,128)(2,1)S(1)}, bf16[256,256]{1,0:T(8,128)(2,1)S(1)}, u32[]{:S(2)}, u32[]{:S(2)}) collective-permute-start(bf16[256,256]{1,0:T(8,128)(2,1)S(1)} %get-tuple-element.58), channel_id=1, source_target_pairs={{0,8},{1,9},{2,10},{3,11},{4,12},{5,13},{6,14},{7,15},{8,0},{9,1},... | collective-permute-start | bytes 393224 | tf_op jit(solution)/shard_map/ppermute | solution.py:82
  23.9 2.1 %collective-permute-start.10 = (f32[256,256]{1,0:T(8,128)S(1)}, f32[256,256]{1,0:T(8,128)S(1)}, u32[]{:S(2)}, u32[]{:S(2)}) collective-permute-start(f32[256,256]{1,0:T(8,128)S(1)} %get-tuple-element.53), channel_id=1, source_target_pairs={{0,1},{1,2},{2,3},{3,4},{4,5},{5,6},{6,7},{7,0},{8,9},{9,10},{10,1... | collective-permute-start | bytes 786440 | tf_op jit(solution)/shard_map/ppermute | solution.py:82
  26.3 3.8 %collective-permute-start.14 = (f32[256,256]{1,0:T(8,128)S(1)}, f32[256,256]{1,0:T(8,128)S(1)}, u32[]{:S(2)}, u32[]{:S(2)}) collective-permute-start(f32[256,256]{1,0:T(8,128)S(1)} %shard_map.77), channel_id=1, source_target_pairs={{0,7},{1,0},{2,1},{3,2},{4,3},{5,4},{6,5},{7,6},{8,15},{9,8},{10,9... | collective-permute-start | bytes 786440 | tf_op jit(solution)/shard_map/ppermute | solution.py:82
  30.5 2.2 %shard_map.85.refs_1_.refs_2_.refs_0_ = f32[512,512]{1,0:T(8,128)S(1)} custom-call(f32[512,512]{1,0:T(8,128)S(1)} %bitcast.17), custom_call_target="tpu_custom_call" | custom-call | flops 2000000000 | bytes 1048576 | tf_op jit(solution)/shard_map/pallas_call | solution.py:65
  32.6 1.8 %shard_map.86 = (f32[512,512]{1,0:T(8,128)S(1)}, f32[640,512]{1,0:T(8,128)S(1)}) custom-call(f32[512,512]{1,0:T(8,128)S(1)} %bitcast.18, f32[512,512]{1,0:T(8,128)S(1)} %shard_map.85.refs_1_.refs_2_.refs_0_, f32[128,512]{1,0:T(8,128)S(1)} %get-tuple-element.68.refs_2_), custom_call_target="tpu_custom_call" | custom-call | flops 2000000000 | bytes 1048576 | tf_op jit(solution)/shard_map/pallas_call | solution.py:65
  34.5 1.9 %collective-permute-start.21 = (f32[640,512]{1,0:T(8,128)S(1)}, f32[640,512]{1,0:T(8,128)S(1)}, u32[]{:S(2)}, u32[]{:S(2)}) collective-permute-start(f32[640,512]{1,0:T(8,128)S(1)} %get-tuple-element.69), channel_id=1, source_target_pairs={{0,16},{16,32},{32,48},{48,64},{64,80},{80,96},{96,112},{112,128},... | collective-permute-start | bytes 3932168 | tf_op jit(solution)/shard_map/ppermute | solution.py:34
  36.4 2.4 %collective-permute-start.18 = (f32[256,256]{1,0:T(8,128)S(1)}, f32[256,256]{1,0:T(8,128)S(1)}, u32[]{:S(2)}, u32[]{:S(2)}) collective-permute-start(f32[256,256]{1,0:T(8,128)S(1)} %get-tuple-element.61), channel_id=1, source_target_pairs={{0,7},{1,0},{2,1},{3,2},{4,3},{5,4},{6,5},{7,6},{8,15},{9,8},{10,9... | collective-permute-start | bytes 786440 | tf_op jit(solution)/shard_map/ppermute | solution.py:82
  39.0 2.3 %collective-permute-start.7 = (bf16[256,512]{1,0:T(8,128)(2,1)S(1)}, bf16[256,512]{1,0:T(8,128)(2,1)S(1)}, u32[]{:S(2)}, u32[]{:S(2)}) collective-permute-start(bf16[256,512]{1,0:T(8,128)(2,1)S(1)} %get-tuple-element.49), channel_id=1, source_target_pairs={{0,8},{1,9},{2,10},{3,11},{4,12},{5,13},{6,14},{7,15},{8,0},{9,1},... | collective-permute-start | bytes 786440 | tf_op jit(solution)/shard_map/ppermute | solution.py:82
  42.1 2.6 %collective-permute-done.18.refs_0_ = f32[256,256]{1,0:T(8,128)S(1)} collective-permute-done((f32[256,256]{1,0:T(8,128)S(1)}, f32[256,256]{1,0:T(8,128)S(1)}, u32[]{:S(2)}, u32[]{:S(2)}) %collective-permute-start.18) | collective-permute-done | bytes 262176 | tf_op jit(solution)/shard_map/ppermute | solution.py:82
  44.7 3.2 %collective-permute-start.16 = (f32[256,256]{1,0:T(8,128)S(1)}, f32[256,256]{1,0:T(8,128)S(1)}, u32[]{:S(2)}, u32[]{:S(2)}) collective-permute-start(f32[256,256]{1,0:T(8,128)S(1)} %shard_map.79), channel_id=1, source_target_pairs={{0,7},{1,0},{2,1},{3,2},{4,3},{5,4},{6,5},{7,6},{8,15},{9,8},{10,9... | collective-permute-start | bytes 786440 | tf_op jit(solution)/shard_map/ppermute | solution.py:82
  48.8 2.2 %collective-permute-done.11.refs_0_ = f32[256,256]{1,0:T(8,128)S(1)} collective-permute-done((f32[256,256]{1,0:T(8,128)S(1)}, f32[256,256]{1,0:T(8,128)S(1)}, u32[]{:S(2)}, u32[]{:S(2)}) %collective-permute-start.11) | collective-permute-done | bytes 262176 | tf_op jit(solution)/shard_map/ppermute | solution.py:82
  51.8 3.8 %collective-permute-start.17 = (f32[256,256]{1,0:T(8,128)S(1)}, f32[256,256]{1,0:T(8,128)S(1)}, u32[]{:S(2)}, u32[]{:S(2)}) collective-permute-start(f32[256,256]{1,0:T(8,128)S(1)} %shard_map.80), channel_id=1, source_target_pairs={{0,7},{1,0},{2,1},{3,2},{4,3},{5,4},{6,5},{7,6},{8,15},{9,8},{10,9... | collective-permute-start | bytes 786440 | tf_op jit(solution)/shard_map/ppermute | solution.py:82
  55.6 1.6 %collective-permute-done.19.refs_0_ = f32[256,256]{1,0:T(8,128)S(1)} collective-permute-done((f32[256,256]{1,0:T(8,128)S(1)}, f32[256,256]{1,0:T(8,128)S(1)}, u32[]{:S(2)}, u32[]{:S(2)}) %collective-permute-start.19) | collective-permute-done | bytes 262176 | tf_op jit(solution)/shard_map/ppermute | solution.py:82
  57.2 3.5 %collective-permute-start.20 = (f32[256,256]{1,0:T(8,128)S(1)}, f32[256,256]{1,0:T(8,128)S(1)}, u32[]{:S(2)}, u32[]{:S(2)}) collective-permute-start(f32[256,256]{1,0:T(8,128)S(1)} %shard_map.82), channel_id=1, source_target_pairs={{0,7},{1,0},{2,1},{3,2},{4,3},{5,4},{6,5},{7,6},{8,15},{9,8},{10,9... | collective-permute-start | bytes 786440 | tf_op jit(solution)/shard_map/ppermute | solution.py:82
  60.9 5.2 %collective-permute-done.12.refs_0_ = f32[256,256]{1,0:T(8,128)S(1)} collective-permute-done((f32[256,256]{1,0:T(8,128)S(1)}, f32[256,256]{1,0:T(8,128)S(1)}, u32[]{:S(2)}, u32[]{:S(2)}) %collective-permute-start.12) | collective-permute-done | bytes 262176 | tf_op jit(solution)/shard_map/ppermute | solution.py:82
  67.2 1.3 %collective-permute-done.20.refs_3_ = f32[256,256]{1,0:T(8,128)S(1)} collective-permute-done((f32[256,256]{1,0:T(8,128)S(1)}, f32[256,256]{1,0:T(8,128)S(1)}, u32[]{:S(2)}, u32[]{:S(2)}) %collective-permute-start.20) | collective-permute-done | bytes 262176 | tf_op jit(solution)/shard_map/ppermute | solution.py:82
  68.4 1.6 %collective-permute-done.8.refs_0_ = f32[256,256]{1,0:T(8,128)S(1)} collective-permute-done((f32[256,256]{1,0:T(8,128)S(1)}, f32[256,256]{1,0:T(8,128)S(1)}, u32[]{:S(2)}, u32[]{:S(2)}) %collective-permute-start.8) | collective-permute-done | bytes 262176 | tf_op jit(solution)/shard_map/ppermute | solution.py:82
  70.1 3.7 %collective-permute-done.13.refs_1_ = f32[256,256]{1,0:T(8,128)S(1)} collective-permute-done((f32[256,256]{1,0:T(8,128)S(1)}, f32[256,256]{1,0:T(8,128)S(1)}, u32[]{:S(2)}, u32[]{:S(2)}) %collective-permute-start.13) | collective-permute-done | bytes 262176 | tf_op jit(solution)/shard_map/ppermute | solution.py:82
  74.7 8.8 %collective-permute-start.22 = (f32[256,512]{1,0:T(8,128)S(1)}, f32[256,512]{1,0:T(8,128)S(1)}, u32[]{:S(2)}, u32[]{:S(2)}) collective-permute-start(f32[256,512]{1,0:T(8,128)S(1)} %shard_map.83.refs_0_.refs_1_), channel_id=1, source_target_pairs={{16,0},{32,16},{48,32},{64,48},{80,64},{96,80},{112,96},{128,112},... | collective-permute-start | bytes 1572872 | tf_op jit(solution)/shard_map/ppermute | solution.py:34
  83.5 1.9 %collective-permute-start.23 = (f32[256,512]{1,0:T(8,128)S(1)}, f32[256,512]{1,0:T(8,128)S(1)}, u32[]{:S(2)}, u32[]{:S(2)}) collective-permute-start(f32[256,512]{1,0:T(8,128)S(1)} %shard_map.89), channel_id=1, source_target_pairs={{0,16},{16,32},{32,48},{48,64},{64,80},{80,96},{96,112},{112,128},... | collective-permute-start | bytes 1572872 | tf_op jit(solution)/shard_map/ppermute | solution.py:34
  85.5 1.5 %shard_map.87.refs_0_ = f32[256,512]{1,0:T(8,128)S(1)} custom-call(f32[256,512]{1,0:T(8,128)S(1)} %shard_map.83.refs_0_.refs_1_, f32[256,256]{1,0:T(8,128)S(1)} %get-tuple-element.66.refs_1_, f32[512,512]{1,0:T(8,128)S(1)} %shard_map.85.refs_1_.refs_2_.refs_0_, f32[640,512]{1,0:T(8,128)S(1)} %collective-permute-done.21.refs_3_), custom_call_target="tpu_custom_call" | custom-call | flops 2000000000 | bytes 1048576 | tf_op jit(solution)/shard_map/pallas_call | solution.py:65
  87.0 3.2 %collective-permute-done.22.refs_2_ = f32[256,512]{1,0:T(8,128)S(1)} collective-permute-done((f32[256,512]{1,0:T(8,128)S(1)}, f32[256,512]{1,0:T(8,128)S(1)}, u32[]{:S(2)}, u32[]{:S(2)}) %collective-permute-start.22) | collective-permute-done | bytes 524320 | tf_op jit(solution)/shard_map/ppermute | solution.py:34
  91.1 5.1 %collective-permute-done.23 = f32[256,512]{1,0:T(8,128)S(1)} collective-permute-done((f32[256,512]{1,0:T(8,128)S(1)}, f32[256,512]{1,0:T(8,128)S(1)}, u32[]{:S(2)}, u32[]{:S(2)}) %collective-permute-start.23) | collective-permute-done | bytes 524320 | tf_op jit(solution)/shard_map/ppermute | solution.py:34
  (54 shorter events, 8.8 us)
Async XLA Ops:
  1.0 9.7 %copy-start = (bf16[1,256,512]{2,1,0:T(8,128)(2,1)S(1)}, bf16[1,256,512]{2,1,0:T(8,128)(2,1)}, u32[]{:S(2)}) copy-start(bf16[1,256,512]{2,1,0:T(8,128)(2,1)} %param.7) | copy-start | bytes 786436
  1.0 19.0 %copy-start.3 = (f32[1,256,256]{2,1,0:T(8,128)S(1)}, f32[1,256,256]{2,1,0:T(8,128)}, u32[]{:S(2)}) copy-start(f32[1,256,256]{2,1,0:T(8,128)} %param.8) | copy-start | bytes 786436
  1.0 19.0 %copy-start.4 = (f32[1,256,256]{2,1,0:T(8,128)S(1)}, f32[1,256,256]{2,1,0:T(8,128)}, u32[]{:S(2)}) copy-start(f32[1,256,256]{2,1,0:T(8,128)} %param.10) | copy-start | bytes 786436
  1.0 9.6 %collective-permute-start = (bf16[256,512]{1,0:T(8,128)(2,1)S(1)}, bf16[256,512]{1,0:T(8,128)(2,1)S(1)}, u32[]{:S(2)}, u32[]{:S(2)}) collective-permute-start(bf16[256,512]{1,0:T(8,128)(2,1)S(1)} %shard_map.65), channel_id=1, source_target_pairs={{0,8},{1,9},{2,10},{3,11},{4,12},{5,13},{6,14},{7,15},{8,0},{9,1},... | collective-permute-start | bytes 786440 | tf_op jit(solution)/shard_map/ppermute | solution.py:82
  10.9 19.4 %collective-permute-start.1 = (f32[256,256]{1,0:T(8,128)S(1)}, f32[256,256]{1,0:T(8,128)S(1)}, u32[]{:S(2)}, u32[]{:S(2)}) collective-permute-start(f32[256,256]{1,0:T(8,128)S(1)} %shard_map.66), channel_id=1, source_target_pairs={{0,1},{1,2},{2,3},{3,4},{4,5},{5,6},{6,7},{7,0},{8,9},{9,10},{10,1... | collective-permute-start | bytes 786440 | tf_op jit(solution)/shard_map/ppermute | solution.py:82
  12.9 8.4 %collective-permute-start.2 = (bf16[256,256]{1,0:T(8,128)(2,1)S(1)}, bf16[256,256]{1,0:T(8,128)(2,1)S(1)}, u32[]{:S(2)}, u32[]{:S(2)}) collective-permute-start(bf16[256,256]{1,0:T(8,128)(2,1)S(1)} %get-tuple-element.42), channel_id=1, source_target_pairs={{0,8},{1,9},{2,10},{3,11},{4,12},{5,13},{6,14},{7,15},{8,0},{9,1},... | collective-permute-start | bytes 393224 | tf_op jit(solution)/shard_map/ppermute | solution.py:82
  15.1 8.5 %collective-permute-start.9 = (bf16[256,256]{1,0:T(8,128)(2,1)S(1)}, bf16[256,256]{1,0:T(8,128)(2,1)S(1)}, u32[]{:S(2)}, u32[]{:S(2)}) collective-permute-start(bf16[256,256]{1,0:T(8,128)(2,1)S(1)} %get-tuple-element.52), channel_id=1, source_target_pairs={{0,8},{1,9},{2,10},{3,11},{4,12},{5,13},{6,14},{7,15},{8,0},{9,1},... | collective-permute-start | bytes 393224 | tf_op jit(solution)/shard_map/ppermute | solution.py:82
  16.5 9.8 %collective-permute-start.3 = (bf16[256,256]{1,0:T(8,128)(2,1)S(1)}, bf16[256,256]{1,0:T(8,128)(2,1)S(1)}, u32[]{:S(2)}, u32[]{:S(2)}) collective-permute-start(bf16[256,256]{1,0:T(8,128)(2,1)S(1)} %get-tuple-element.43), channel_id=1, source_target_pairs={{0,8},{1,9},{2,10},{3,11},{4,12},{5,13},{6,14},{7,15},{8,0},{9,1},... | collective-permute-start | bytes 393224 | tf_op jit(solution)/shard_map/ppermute | solution.py:82
  18.6 20.3 %collective-permute-start.5 = (bf16[256,512]{1,0:T(8,128)(2,1)S(1)}, bf16[256,512]{1,0:T(8,128)(2,1)S(1)}, u32[]{:S(2)}, u32[]{:S(2)}) collective-permute-start(bf16[256,512]{1,0:T(8,128)(2,1)S(1)} %get-tuple-element.46), channel_id=1, source_target_pairs={{0,8},{1,9},{2,10},{3,11},{4,12},{5,13},{6,14},{7,15},{8,0},{9,1},... | collective-permute-start | bytes 786440 | tf_op jit(solution)/shard_map/ppermute | solution.py:82
  21.3 15.1 %collective-permute-start.15 = (bf16[256,256]{1,0:T(8,128)(2,1)S(1)}, bf16[256,256]{1,0:T(8,128)(2,1)S(1)}, u32[]{:S(2)}, u32[]{:S(2)}) collective-permute-start(bf16[256,256]{1,0:T(8,128)(2,1)S(1)} %get-tuple-element.58), channel_id=1, source_target_pairs={{0,8},{1,9},{2,10},{3,11},{4,12},{5,13},{6,14},{7,15},{8,0},{9,1},... | collective-permute-start | bytes 393224 | tf_op jit(solution)/shard_map/ppermute | solution.py:82
  23.9 6.5 %copy-start.1 = (f32[1,512,512]{2,1,0:T(8,128)S(1)}, f32[1,512,512]{2,1,0:T(8,128)}, u32[]{:S(2)}) copy-start(f32[1,512,512]{2,1,0:T(8,128)} %param.9) | copy-start | bytes 3145732
  23.9 14.9 %collective-permute-start.10 = (f32[256,256]{1,0:T(8,128)S(1)}, f32[256,256]{1,0:T(8,128)S(1)}, u32[]{:S(2)}, u32[]{:S(2)}) collective-permute-start(f32[256,256]{1,0:T(8,128)S(1)} %get-tuple-element.53), channel_id=1, source_target_pairs={{0,1},{1,2},{2,3},{3,4},{4,5},{5,6},{6,7},{7,0},{8,9},{9,10},{10,1... | collective-permute-start | bytes 786440 | tf_op jit(solution)/shard_map/ppermute | solution.py:82
  26.3 12.7 %collective-permute-start.14 = (f32[256,256]{1,0:T(8,128)S(1)}, f32[256,256]{1,0:T(8,128)S(1)}, u32[]{:S(2)}, u32[]{:S(2)}) collective-permute-start(f32[256,256]{1,0:T(8,128)S(1)} %shard_map.77), channel_id=1, source_target_pairs={{0,7},{1,0},{2,1},{3,2},{4,3},{5,4},{6,5},{7,6},{8,15},{9,8},{10,9... | collective-permute-start | bytes 786440 | tf_op jit(solution)/shard_map/ppermute | solution.py:82
  30.4 2.2 %copy-start.2 = (f32[1,512,512]{2,1,0:T(8,128)S(1)}, f32[1,512,512]{2,1,0:T(8,128)}, u32[]{:S(2)}) copy-start(f32[1,512,512]{2,1,0:T(8,128)} %param.11) | copy-start | bytes 3145732
  34.5 51.0 %collective-permute-start.21 = (f32[640,512]{1,0:T(8,128)S(1)}, f32[640,512]{1,0:T(8,128)S(1)}, u32[]{:S(2)}, u32[]{:S(2)}) collective-permute-start(f32[640,512]{1,0:T(8,128)S(1)} %get-tuple-element.69), channel_id=1, source_target_pairs={{0,16},{16,32},{32,48},{48,64},{64,80},{80,96},{96,112},{112,128},... | collective-permute-start | bytes 3932168 | tf_op jit(solution)/shard_map/ppermute | solution.py:34
  36.4 8.3 %collective-permute-start.18 = (f32[256,256]{1,0:T(8,128)S(1)}, f32[256,256]{1,0:T(8,128)S(1)}, u32[]{:S(2)}, u32[]{:S(2)}) collective-permute-start(f32[256,256]{1,0:T(8,128)S(1)} %get-tuple-element.61), channel_id=1, source_target_pairs={{0,7},{1,0},{2,1},{3,2},{4,3},{5,4},{6,5},{7,6},{8,15},{9,8},{10,9... | collective-permute-start | bytes 786440 | tf_op jit(solution)/shard_map/ppermute | solution.py:82
  38.8 9.1 %collective-permute-start.4 = (f32[256,256]{1,0:T(8,128)S(1)}, f32[256,256]{1,0:T(8,128)S(1)}, u32[]{:S(2)}, u32[]{:S(2)}) collective-permute-start(f32[256,256]{1,0:T(8,128)S(1)} %shard_map.68), channel_id=1, source_target_pairs={{0,1},{1,2},{2,3},{3,4},{4,5},{5,6},{6,7},{7,0},{8,9},{9,10},{10,1... | collective-permute-start | bytes 786440 | tf_op jit(solution)/shard_map/ppermute | solution.py:82
  38.9 12.0 %collective-permute-start.11 = (f32[256,256]{1,0:T(8,128)S(1)}, f32[256,256]{1,0:T(8,128)S(1)}, u32[]{:S(2)}, u32[]{:S(2)}) collective-permute-start(f32[256,256]{1,0:T(8,128)S(1)} %shard_map.74), channel_id=1, source_target_pairs={{0,1},{1,2},{2,3},{3,4},{4,5},{5,6},{6,7},{7,0},{8,9},{9,10},{10,1... | collective-permute-start | bytes 786440 | tf_op jit(solution)/shard_map/ppermute | solution.py:82
  39.0 12.0 %collective-permute-start.7 = (bf16[256,512]{1,0:T(8,128)(2,1)S(1)}, bf16[256,512]{1,0:T(8,128)(2,1)S(1)}, u32[]{:S(2)}, u32[]{:S(2)}) collective-permute-start(bf16[256,512]{1,0:T(8,128)(2,1)S(1)} %get-tuple-element.49), channel_id=1, source_target_pairs={{0,8},{1,9},{2,10},{3,11},{4,12},{5,13},{6,14},{7,15},{8,0},{9,1},... | collective-permute-start | bytes 786440 | tf_op jit(solution)/shard_map/ppermute | solution.py:82
  44.7 7.1 %collective-permute-start.16 = (f32[256,256]{1,0:T(8,128)S(1)}, f32[256,256]{1,0:T(8,128)S(1)}, u32[]{:S(2)}, u32[]{:S(2)}) collective-permute-start(f32[256,256]{1,0:T(8,128)S(1)} %shard_map.79), channel_id=1, source_target_pairs={{0,7},{1,0},{2,1},{3,2},{4,3},{5,4},{6,5},{7,6},{8,15},{9,8},{10,9... | collective-permute-start | bytes 786440 | tf_op jit(solution)/shard_map/ppermute | solution.py:82
  47.9 9.3 %collective-permute-start.19 = (f32[256,256]{1,0:T(8,128)S(1)}, f32[256,256]{1,0:T(8,128)S(1)}, u32[]{:S(2)}, u32[]{:S(2)}) collective-permute-start(f32[256,256]{1,0:T(8,128)S(1)} %shard_map.81), channel_id=1, source_target_pairs={{0,7},{1,0},{2,1},{3,2},{4,3},{5,4},{6,5},{7,6},{8,15},{9,8},{10,9... | collective-permute-start | bytes 786440 | tf_op jit(solution)/shard_map/ppermute | solution.py:82
  50.9 9.8 %collective-permute-start.6 = (f32[256,256]{1,0:T(8,128)S(1)}, f32[256,256]{1,0:T(8,128)S(1)}, u32[]{:S(2)}, u32[]{:S(2)}) collective-permute-start(f32[256,256]{1,0:T(8,128)S(1)} %shard_map.70), channel_id=1, source_target_pairs={{0,1},{1,2},{2,3},{3,4},{4,5},{5,6},{6,7},{7,0},{8,9},{9,10},{10,1... | collective-permute-start | bytes 786440 | tf_op jit(solution)/shard_map/ppermute | solution.py:82
  51.0 15.1 %collective-permute-start.12 = (f32[256,256]{1,0:T(8,128)S(1)}, f32[256,256]{1,0:T(8,128)S(1)}, u32[]{:S(2)}, u32[]{:S(2)}) collective-permute-start(f32[256,256]{1,0:T(8,128)S(1)} %shard_map.75), channel_id=1, source_target_pairs={{0,1},{1,2},{2,3},{3,4},{4,5},{5,6},{6,7},{7,0},{8,9},{9,10},{10,1... | collective-permute-start | bytes 786440 | tf_op jit(solution)/shard_map/ppermute | solution.py:82
  51.8 15.3 %collective-permute-start.17 = (f32[256,256]{1,0:T(8,128)S(1)}, f32[256,256]{1,0:T(8,128)S(1)}, u32[]{:S(2)}, u32[]{:S(2)}) collective-permute-start(f32[256,256]{1,0:T(8,128)S(1)} %shard_map.80), channel_id=1, source_target_pairs={{0,7},{1,0},{2,1},{3,2},{4,3},{5,4},{6,5},{7,6},{8,15},{9,8},{10,9... | collective-permute-start | bytes 786440 | tf_op jit(solution)/shard_map/ppermute | solution.py:82
  57.2 11.2 %collective-permute-start.20 = (f32[256,256]{1,0:T(8,128)S(1)}, f32[256,256]{1,0:T(8,128)S(1)}, u32[]{:S(2)}, u32[]{:S(2)}) collective-permute-start(f32[256,256]{1,0:T(8,128)S(1)} %shard_map.82), channel_id=1, source_target_pairs={{0,7},{1,0},{2,1},{3,2},{4,3},{5,4},{6,5},{7,6},{8,15},{9,8},{10,9... | collective-permute-start | bytes 786440 | tf_op jit(solution)/shard_map/ppermute | solution.py:82
  60.8 9.3 %collective-permute-start.8 = (f32[256,256]{1,0:T(8,128)S(1)}, f32[256,256]{1,0:T(8,128)S(1)}, u32[]{:S(2)}, u32[]{:S(2)}) collective-permute-start(f32[256,256]{1,0:T(8,128)S(1)} %shard_map.72), channel_id=1, source_target_pairs={{0,1},{1,2},{2,3},{3,4},{4,5},{5,6},{6,7},{7,0},{8,9},{9,10},{10,1... | collective-permute-start | bytes 786440 | tf_op jit(solution)/shard_map/ppermute | solution.py:82
  66.1 7.7 %collective-permute-start.13 = (f32[256,256]{1,0:T(8,128)S(1)}, f32[256,256]{1,0:T(8,128)S(1)}, u32[]{:S(2)}, u32[]{:S(2)}) collective-permute-start(f32[256,256]{1,0:T(8,128)S(1)} %shard_map.76), channel_id=1, source_target_pairs={{0,1},{1,2},{2,3},{3,4},{4,5},{5,6},{6,7},{7,0},{8,9},{9,10},{10,1... | collective-permute-start | bytes 786440 | tf_op jit(solution)/shard_map/ppermute | solution.py:82
  74.7 15.5 %collective-permute-start.22 = (f32[256,512]{1,0:T(8,128)S(1)}, f32[256,512]{1,0:T(8,128)S(1)}, u32[]{:S(2)}, u32[]{:S(2)}) collective-permute-start(f32[256,512]{1,0:T(8,128)S(1)} %shard_map.83.refs_0_.refs_1_), channel_id=1, source_target_pairs={{16,0},{32,16},{48,32},{64,48},{80,64},{96,80},{112,96},{128,112},... | collective-permute-start | bytes 1572872 | tf_op jit(solution)/shard_map/ppermute | solution.py:34
  83.5 12.6 %collective-permute-start.23 = (f32[256,512]{1,0:T(8,128)S(1)}, f32[256,512]{1,0:T(8,128)S(1)}, u32[]{:S(2)}, u32[]{:S(2)}) collective-permute-start(f32[256,512]{1,0:T(8,128)S(1)} %shard_map.89), channel_id=1, source_target_pairs={{0,16},{16,32},{32,48},{48,64},{64,80},{80,96},{96,112},{112,128},... | collective-permute-start | bytes 1572872 | tf_op jit(solution)/shard_map/ppermute | solution.py:34
